TPU v7x, 512 devices: a whole 4x8x8 slice. The times are simulated.
512 devices in a mesh: row: 32 (over y, z_lo, core), col: 16 (over z_hi, x).
Axes of the slice: x: 4, y: 8, z: 8 (z_hi: 4, z_lo: 2; z = z_hi * 2 + z_lo), core: 2. Of those that a mesh axis runs over, the one named last changes fastest.
Arguments:
- residual: float32 [8192, 8192], P('row', 'col'), may hold values from -0.15625 to 0.15625
- direction: float32 [8192, 8192], P('row', 'col'), may hold values from -6 to 6
- ground_shift: float32 [1], replicated, may hold values from 1.6937256e-06 to 6.7749024e-06
- previous: float32 [1], replicated, may hold values from 3072 to 12288
Outputs:
- next_direction: float32 [8192, 8192], P('row', 'col')
- step_ratio: float32 [1], replicated
All inputs are finite; a program needn't handle non-finite values.
Results may differ from a plain program's by a relative error of at most 0.00015.
Values sent between devices are 32-bit elements; how exact they have to be, the bound alone decides.
No kernel may reach another device: no remote copies, remote signals or barrier semaphores. Data moves between devices by JAX's collectives and lax.ppermute only.
A program may use at most 64 MiB of HBM per device.

v0:
```python
import jax
import jax.numpy as jnp
from jax import lax
from jax.sharding import Mesh
from jax.sharding import PartitionSpec as P

COL = ("col_0", "col_1")
ROW = ("row_0", "row_1", "row_2")
ROW_COL = ("row_0", "row_1", "row_2", "col_0", "col_1")


PRECISE = lax.Precision.HIGHEST


def over_axes(array, axes):
    for axis in axes:
        array = lax.psum(array, axis)
    return array


def mixing_tables(devices):
    target = jnp.arange(devices, dtype=jnp.int32)[:, None]
    source = jnp.arange(devices, dtype=jnp.int32)[None, :]
    angles = jnp.pi * (target * source % (2 * devices)).astype(jnp.float32) / devices
    parity = jnp.where(source % 2 == 0, 1.0, -1.0).astype(jnp.float32)
    return (jnp.cos(angles), jnp.where(target > 0, jnp.sin(angles), parity))


def local_tables(extent, devices, device_index):
    length = extent * devices
    halfway = extent // 2
    position = jnp.arange(extent, dtype=jnp.int32)[:, None]
    steps_m = jnp.arange(halfway, dtype=jnp.int32)
    second_wave = jnp.where(device_index == 0, devices, 2 * devices - device_index)
    first_waves = 2 * devices * steps_m + device_index
    second_waves = 2 * devices * steps_m + second_wave

    def table_pair(wavenums):
        phases = wavenums[None, :] * (2 * position + 1) % (4 * length)
        angles = jnp.pi * phases.astype(jnp.float32) / (2 * length)
        scaling = jnp.where(wavenums == 0, jnp.sqrt(1.0 / length), jnp.sqrt(2.0 / length)).astype(
            jnp.float32
        )
        return (scaling[None, :] * jnp.cos(angles), scaling[None, :] * jnp.sin(angles))

    cos_one, sin_one = table_pair(first_waves)
    cos_two, sin_two = table_pair(second_waves)
    nonzero = (device_index > 0).astype(jnp.float32)
    tables = (
        cos_one,
        -nonzero * sin_one,
        nonzero * cos_two,
        jnp.where(device_index > 0, sin_two, cos_two),
    )
    return (tables, jnp.concatenate([first_waves, second_waves]))


def spread_forward(mix_cos, mix_sin):

    def combine(pieces):
        source = pieces[0]
        real_part = jnp.einsum("td,dab->tab", mix_cos, source, precision=PRECISE)
        imag_part = jnp.einsum("td,dab->tab", mix_sin, source, precision=PRECISE)
        return (real_part, imag_part)

    return combine


def spread_inverse(mix_cos, mix_sin):

    def combine(pieces):
        real_part = jnp.einsum("td,tab->dab", mix_cos, pieces[0], precision=PRECISE)
        imag_part = jnp.einsum("td,tab->dab", mix_sin, pieces[1], precision=PRECISE)
        return (real_part + imag_part,)

    return combine


def across_columns(arrays, combine):
    devices = lax.axis_size(COL)

    def handle(pieces):
        mixed = combine(pieces)
        return lax.all_to_all(mixed, COL, split_axis=0, concat_axis=0, tiled=True)

    shaped = tuple(
        (
            member.reshape((devices, member.shape[0] // devices) + member.shape[1:])
            for member in arrays
        )
    )
    result = handle(lax.all_to_all(shaped, COL, split_axis=0, concat_axis=0, tiled=True))
    return tuple((member.reshape((-1,) + member.shape[2:]) for member in result))


def across_rows(arrays, combine):
    devices = lax.axis_size(ROW)

    def handle(pieces):
        mixed = combine(pieces)
        return lax.all_to_all(mixed, ROW, split_axis=0, concat_axis=0, tiled=True)

    shaped = tuple(
        (
            member.reshape((devices, member.shape[0] // devices) + member.shape[1:])
            for member in arrays
        )
    )
    result = handle(lax.all_to_all(shaped, ROW, split_axis=0, concat_axis=0, tiled=True))
    return tuple((member.reshape((-1,) + member.shape[2:]) for member in result))


def body(residual, direction, ground_shift, previous):
    row_count = lax.axis_size(ROW)
    col_count = lax.axis_size(COL)
    row_index = lax.axis_index(ROW)
    col_index = lax.axis_index(COL)
    rows_here = residual.shape[0]
    cols_here = residual.shape[1]
    halfway_rows = rows_here // 2
    halfway_cols = cols_here // 2
    col_tables, col_waves = local_tables(cols_here, col_count, col_index)
    row_tables, row_waves = local_tables(rows_here, row_count, row_index)
    col_cos, col_sin = mixing_tables(col_count)
    row_cos, row_sin = mixing_tables(row_count)
    real_part, imag_part = across_columns((residual,), spread_forward(col_cos, col_sin))
    left_half = jnp.dot(real_part, col_tables[0], precision=PRECISE) + jnp.dot(
        imag_part, col_tables[1], precision=PRECISE
    )
    right_half = jnp.dot(real_part, col_tables[2], precision=PRECISE) + jnp.dot(
        imag_part, col_tables[3], precision=PRECISE
    )
    partial_spectrum = jnp.concatenate([left_half, right_half], axis=1)
    real_part, imag_part = across_rows((partial_spectrum,), spread_forward(row_cos, row_sin))
    upper_half = jnp.dot(row_tables[0].T, real_part, precision=PRECISE) + jnp.dot(
        row_tables[1].T, imag_part, precision=PRECISE
    )
    lower_half = jnp.dot(row_tables[2].T, real_part, precision=PRECISE) + jnp.dot(
        row_tables[3].T, imag_part, precision=PRECISE
    )
    spectrum = jnp.concatenate([upper_half, lower_half], axis=0)
    row_total = rows_here * row_count
    col_total = cols_here * col_count
    row_sine = jnp.sin(jnp.pi * row_waves.astype(jnp.float32) / (2 * row_total))
    col_sine = jnp.sin(jnp.pi * col_waves.astype(jnp.float32) / (2 * col_total))
    eigenvalue = 4.0 * (row_sine * row_sine)[:, None] + 4.0 * (col_sine * col_sine)[None, :]
    weight = 1.0 / (eigenvalue + ground_shift[0])
    scaled = weight * spectrum
    upper_half = scaled[:halfway_rows]
    lower_half = scaled[halfway_rows:]
    back_real = jnp.dot(row_tables[0], upper_half, precision=PRECISE) + jnp.dot(
        row_tables[2], lower_half, precision=PRECISE
    )
    back_imag = jnp.dot(row_tables[1], upper_half, precision=PRECISE) + jnp.dot(
        row_tables[3], lower_half, precision=PRECISE
    )
    partial_field = across_rows((back_real, back_imag), spread_inverse(row_cos, row_sin))[0]
    left_half = partial_field[:, :halfway_cols]
    right_half = partial_field[:, halfway_cols:]
    back_real = jnp.dot(left_half, col_tables[0].T, precision=PRECISE) + jnp.dot(
        right_half, col_tables[2].T, precision=PRECISE
    )
    back_imag = jnp.dot(left_half, col_tables[1].T, precision=PRECISE) + jnp.dot(
        right_half, col_tables[3].T, precision=PRECISE
    )
    precond = across_columns((back_real, back_imag), spread_inverse(col_cos, col_sin))[0]
    local_inner = jnp.sum(spectrum * scaled)
    inner_total = over_axes(local_inner, ROW_COL)
    step_ratio = inner_total / previous[0]
    return (precond + step_ratio * direction, jnp.reshape(step_ratio, (1,)))


def solution(mesh):
    finer = Mesh(mesh.devices.reshape(8, 2, 2, 4, 4), ("row_0", "row_1", "row_2", "col_0", "col_1"))
    return jax.shard_map(
        body,
        mesh=finer,
        in_specs=(P(ROW, COL), P(ROW, COL), P(), P()),
        out_specs=(P(ROW, COL), P()),
        check_vma=False,
    )
```

profile of v0, /device:TPU:1, one launch (start us, length us, event | category | flops | bytes accessed | tf_op | source)
XLA Modules:
  0.0 330.9 jit_solution(59591209044560012)
XLA Ops:
  0.6 26.4 %all_to_all.60 = f32[16,16,512]{2,1,0:T(8,128)S(1)} all-to-all(f32[16,16,512]{2,1,0:T(8,128)} %bitcast.57), channel_id=1, replica_groups=mesh['row_0'=8,'row_1'=2,'row_2'=2,'col_0'=4,'col_1'=4] {'col_0','col_1'}, dimensions={0} | all-to-all | bytes 1048576 | tf_op jit(solution)/shard_map/all_to_all | solution.py:92
  27.0 0.9 fusion.27
  27.9 1.1 copy.34
  29.0 7.5 %all-to-all-start.1 = ((f32[16,16,512]{2,1,0:T(8,128)}), f32[16,16,512]{2,1,0:T(8,128)S(1)}, u32[]{:S(2)}, u32[]{:S(2)}) async-start(f32[16,16,512]{2,1,0:T(8,128)} %copy.34), calls=%async_computation.1 | async-start | bytes 1048576 | tf_op jit(solution)/shard_map/all_to_all | solution.py:84
  36.6 0.9 fusion.25
  37.5 1.1 copy.37
  38.6 9.9 %all-to-all-done.1 = f32[16,16,512]{2,1,0:T(8,128)S(1)} async-done(((f32[16,16,512]{2,1,0:T(8,128)}), f32[16,16,512]{2,1,0:T(8,128)S(1)}, u32[]{:S(2)}, u32[]{:S(2)}) %all-to-all-start.1) | async-done | bytes 524320 | tf_op jit(solution)/shard_map/all_to_all | solution.py:84
  48.5 6.8 %all-to-all-start.2 = ((f32[16,16,512]{2,1,0:T(8,128)}), f32[16,16,512]{2,1,0:T(8,128)S(1)}, u32[]{:S(2)}, u32[]{:S(2)}) async-start(f32[16,16,512]{2,1,0:T(8,128)} %copy.37), calls=%async_computation.2 | async-start | bytes 1048576 | tf_op jit(solution)/shard_map/all_to_all | solution.py:84
  55.3 3.0 fusion.33
  58.3 2.9 fusion.30
  61.3 4.8 %all-to-all-done.2 = f32[16,16,512]{2,1,0:T(8,128)S(1)} async-done(((f32[16,16,512]{2,1,0:T(8,128)}), f32[16,16,512]{2,1,0:T(8,128)S(1)}, u32[]{:S(2)}, u32[]{:S(2)}) %all-to-all-start.2) | async-done | bytes 524320 | tf_op jit(solution)/shard_map/all_to_all | solution.py:84
  66.1 3.1 convolution_add_fusion.8
  69.2 3.2 convolution_add_fusion.9
  72.5 0.2 copy.38
  72.7 34.1 %all_to_all.61 = f32[32,8,512]{2,1,0:T(8,128)S(1)} all-to-all(f32[32,8,512]{2,1,0:T(8,128)S(1)} %bitcast.56), channel_id=1, replica_groups=mesh['row_0'=8,'row_1'=2,'row_2'=2,'col_0'=4,'col_1'=4] {'row_0','row_1'..., dimensions={0} | all-to-all | bytes 1048576 | tf_op jit(solution)/shard_map/all_to_all | solution.py:109
  106.7 0.9 fusion.23
  107.7 1.1 copy.41
  108.8 4.9 %all-to-all-start.4 = ((f32[32,8,512]{2,1,0:T(8,128)}), f32[32,8,512]{2,1,0:T(8,128)S(1)}, u32[]{:S(2)}, u32[]{:S(2)}) async-start(f32[32,8,512]{2,1,0:T(8,128)} %copy.41), calls=%async_computation.4 | async-start | bytes 1048576 | tf_op jit(solution)/shard_map/all_to_all | solution.py:101
  114.4 0.9 fusion.21
  115.3 1.1 copy.44
  116.4 14.3 %all-to-all-done.4 = f32[32,8,512]{2,1,0:T(8,128)S(1)} async-done(((f32[32,8,512]{2,1,0:T(8,128)}), f32[32,8,512]{2,1,0:T(8,128)S(1)}, u32[]{:S(2)}, u32[]{:S(2)}) %all-to-all-start.4) | async-done | bytes 524320 | tf_op jit(solution)/shard_map/all_to_all | solution.py:101
  130.7 4.9 %all-to-all-start.5 = ((f32[32,8,512]{2,1,0:T(8,128)}), f32[32,8,512]{2,1,0:T(8,128)S(1)}, u32[]{:S(2)}, u32[]{:S(2)}) async-start(f32[32,8,512]{2,1,0:T(8,128)} %copy.44), calls=%async_computation.5 | async-start | bytes 1048576 | tf_op jit(solution)/shard_map/all_to_all | solution.py:101
  135.6 0.1 fusion.143
  135.7 1.0 fusion.10
  136.7 1.0 fusion.12
  137.7 14.9 %all-to-all-done.5 = f32[32,8,512]{2,1,0:T(8,128)S(1)} async-done(((f32[32,8,512]{2,1,0:T(8,128)}), f32[32,8,512]{2,1,0:T(8,128)S(1)}, u32[]{:S(2)}, u32[]{:S(2)}) %all-to-all-start.5) | async-done | bytes 524320 | tf_op jit(solution)/shard_map/all_to_all | solution.py:101
  152.6 1.0 convolution_add_fusion.6
  153.6 1.0 convolution_add_fusion.7
  154.6 0.9 multiply_reduce_fusion
  155.5 1.1 fusion.65
  156.7 1.9 fusion.1
  158.6 5.2 %all-to-all-start.6 = ((f32[32,8,512]{2,1,0:T(8,128)}), f32[32,8,512]{2,1,0:T(8,128)S(1)}, u32[]{:S(2)}, u32[]{:S(2)}) async-start(f32[32,8,512]{2,1,0:T(8,128)} %fusion.1), calls=%async_computation.6 | async-start | bytes 1048576 | tf_op jit(solution)/shard_map/all_to_all | solution.py:109
  163.8 1.1 fusion.63
  164.9 2.0 fusion
  166.9 13.8 %all-to-all-done.6 = f32[32,8,512]{2,1,0:T(8,128)S(1)} async-done(((f32[32,8,512]{2,1,0:T(8,128)}), f32[32,8,512]{2,1,0:T(8,128)S(1)}, u32[]{:S(2)}, u32[]{:S(2)}) %all-to-all-start.6) | async-done | bytes 524320 | tf_op jit(solution)/shard_map/all_to_all | solution.py:109
  180.7 4.9 %all-to-all-start.7 = ((f32[32,8,512]{2,1,0:T(8,128)}), f32[32,8,512]{2,1,0:T(8,128)S(1)}, u32[]{:S(2)}, u32[]{:S(2)}) async-start(f32[32,8,512]{2,1,0:T(8,128)} %fusion), calls=%async_computation.7 | async-start | bytes 1048576 | tf_op jit(solution)/shard_map/all_to_all | solution.py:109
  185.5 0.9 fusion.18
  186.4 16.1 %all-to-all-done.7 = f32[32,8,512]{2,1,0:T(8,128)S(1)} async-done(((f32[32,8,512]{2,1,0:T(8,128)}), f32[32,8,512]{2,1,0:T(8,128)S(1)}, u32[]{:S(2)}, u32[]{:S(2)}) %all-to-all-start.7) | async-done | bytes 524320 | tf_op jit(solution)/shard_map/all_to_all | solution.py:109
  202.5 0.9 convolution_add_fusion.1
  203.5 0.3 copy.47
  203.8 20.6 %all_to_all.62 = f32[32,8,512]{2,1,0:T(8,128)S(1)} all-to-all(f32[32,8,512]{2,1,0:T(8,128)S(1)} %copy.47), channel_id=1, replica_groups=mesh['row_0'=8,'row_1'=2,'row_2'=2,'col_0'=4,'col_1'=4] {'row_0','row_1'..., dimensions={0} | all-to-all | bytes 1048576 | tf_op jit(solution)/shard_map/all_to_all | solution.py:101
  224.4 2.6 fusion.29
  227.0 3.6 %convolution_add_fusion.5 = f32[256,512]{1,0:T(8,128)} fusion(f32[256,512]{1,0:T(8,128)S(1)} %fusion.29, f32[256]{0:T(256)S(1)} %compare_select_fusion.2, f32[]{:T(128)S(6)} %convert_element_type.56, s32[256]{0:T(256)S(1)} %get-tuple-element.4, s32[512]{0:T(512)S(1)} %multiply_add_fusion, f32[256,512]{1,0:T(8,128)S(1)} %bitcast.63), kind=kOutput, calls=%fused_computation.7 | convolution fusion | flops 404881408 | bytes 1314820 | tf_op jit(solution)/shard_map/dot_general | solution.py:160
  230.6 5.6 %all-to-all-start.9 = ((f32[16,16,512]{2,1,0:T(8,128)}), f32[16,16,512]{2,1,0:T(8,128)S(1)}, u32[]{:S(2)}, u32[]{:S(2)}) async-start(f32[16,16,512]{2,1,0:T(8,128)} %bitcast.17), calls=%async_computation.9 | async-start | bytes 1048576 | tf_op jit(solution)/shard_map/all_to_all | solution.py:92
  236.2 2.6 fusion.31
  238.8 3.8 %convolution_add_fusion.4 = f32[256,512]{1,0:T(8,128)} fusion(f32[256,512]{1,0:T(8,128)S(1)} %fusion.31, f32[256]{0:T(256)S(1)} %compare_select_fusion.2, s32[256]{0:T(256)S(1)} %get-tuple-element.4, s32[512]{0:T(512)S(1)} %multiply_add_fusion, pred[]{:T(512)S(6)} %gt.32, f32[256,512]{1,0:T(8,128)S(1)} %bitcast.65), kind=kOutput, calls=%fused_computation.6 | convolution fusion | flops 405012480 | bytes 1314817 | tf_op jit(solution)/shard_map/dot_general | solution.py:163
  242.6 5.8 %all-to-all-done.9 = f32[16,16,512]{2,1,0:T(8,128)S(1)} async-done(((f32[16,16,512]{2,1,0:T(8,128)}), f32[16,16,512]{2,1,0:T(8,128)S(1)}, u32[]{:S(2)}, u32[]{:S(2)}) %all-to-all-start.9) | async-done | bytes 524320 | tf_op jit(solution)/shard_map/all_to_all | solution.py:92
  248.4 5.9 %all-to-all-start.10 = ((f32[16,16,512]{2,1,0:T(8,128)}), f32[16,16,512]{2,1,0:T(8,128)S(1)}, u32[]{:S(2)}, u32[]{:S(2)}) async-start(f32[16,16,512]{2,1,0:T(8,128)} %bitcast.19), calls=%async_computation.10 | async-start | bytes 1048576 | tf_op jit(solution)/shard_map/all_to_all | solution.py:92
  254.3 0.8 fusion.15
  255.2 10.6 %all-to-all-done.10 = f32[16,16,512]{2,1,0:T(8,128)S(1)} async-done(((f32[16,16,512]{2,1,0:T(8,128)}), f32[16,16,512]{2,1,0:T(8,128)S(1)}, u32[]{:S(2)}, u32[]{:S(2)}) %all-to-all-start.10) | async-done | bytes 524320 | tf_op jit(solution)/shard_map/all_to_all | solution.py:92
  265.8 0.9 convolution_add_fusion
  266.7 1.1 copy.50
  267.8 0.0 copy-start
  267.8 4.5 %all-to-all-start.11 = ((f32[16,16,512]{2,1,0:T(8,128)}), f32[16,16,512]{2,1,0:T(8,128)S(1)}, u32[]{:S(2)}, u32[]{:S(2)}) async-start(f32[16,16,512]{2,1,0:T(8,128)} %copy.50), calls=%async_computation.11 | async-start | bytes 1048576 | tf_op jit(solution)/shard_map/all_to_all | solution.py:84
  272.3 19.0 %psum.35 = f32[]{:T(128)} all-reduce(f32[]{:T(128)} %get-tuple-element.2), channel_id=1, replica_groups=mesh['row_0'=8,'row_1'=2,'row_2'=2,'col_0'=4,'col_1'=4] {'row_0'}, use_global_device_ids=true, to_apply=%region_1.2 | all-reduce | flops 1 | bytes 8 | tf_op jit(solution)/shard_map/psum | solution.py:17
  291.3 7.3 %psum.36 = f32[]{:T(128)} all-reduce(f32[]{:T(128)} %psum.35), channel_id=1, replica_groups=mesh['row_0'=8,'row_1'=2,'row_2'=2,'col_0'=4,'col_1'=4] {'row_1'}, use_global_device_ids=true, to_apply=%region_2.3 | all-reduce | flops 1 | bytes 8 | tf_op jit(solution)/shard_map/psum | solution.py:17
  298.7 8.2 %psum.37 = f32[]{:T(128)} all-reduce(f32[]{:T(128)} %psum.36), channel_id=1, replica_groups=mesh['row_0'=8,'row_1'=2,'row_2'=2,'col_0'=4,'col_1'=4] {'row_2'}, use_global_device_ids=true, to_apply=%region_3.4 | all-reduce | flops 1 | bytes 8 | tf_op jit(solution)/shard_map/psum | solution.py:17
  306.9 11.3 %psum.38 = f32[]{:T(128)} all-reduce(f32[]{:T(128)} %psum.37), channel_id=1, replica_groups=mesh['row_0'=8,'row_1'=2,'row_2'=2,'col_0'=4,'col_1'=4] {'col_0'}, use_global_device_ids=true, to_apply=%region_4.5 | all-reduce | flops 1 | bytes 8 | tf_op jit(solution)/shard_map/psum | solution.py:17
  318.8 9.1 %psum.39 = f32[]{:T(128)} all-reduce(f32[]{:T(128)} %psum.38), channel_id=1, replica_groups=mesh['row_0'=8,'row_1'=2,'row_2'=2,'col_0'=4,'col_1'=4] {'col_1'}, use_global_device_ids=true, to_apply=%region_5.6 | all-reduce | flops 1 | bytes 8 | tf_op jit(solution)/shard_map/psum | solution.py:17
  328.6 0.0 all-to-all-done.11
  328.6 0.0 copy-done
  328.6 0.9 bitcast_add_fusion
  (14 shorter events, 0.1 us)
Async XLA Ops:
  29.0 19.5 %all-to-all-start.1 = ((f32[16,16,512]{2,1,0:T(8,128)}), f32[16,16,512]{2,1,0:T(8,128)S(1)}, u32[]{:S(2)}, u32[]{:S(2)}) async-start(f32[16,16,512]{2,1,0:T(8,128)} %copy.34), calls=%async_computation.1 | async-start | bytes 1048576 | tf_op jit(solution)/shard_map/all_to_all | solution.py:84
  48.5 17.6 %all-to-all-start.2 = ((f32[16,16,512]{2,1,0:T(8,128)}), f32[16,16,512]{2,1,0:T(8,128)S(1)}, u32[]{:S(2)}, u32[]{:S(2)}) async-start(f32[16,16,512]{2,1,0:T(8,128)} %copy.37), calls=%async_computation.2 | async-start | bytes 1048576 | tf_op jit(solution)/shard_map/all_to_all | solution.py:84
  108.8 21.9 %all-to-all-start.4 = ((f32[32,8,512]{2,1,0:T(8,128)}), f32[32,8,512]{2,1,0:T(8,128)S(1)}, u32[]{:S(2)}, u32[]{:S(2)}) async-start(f32[32,8,512]{2,1,0:T(8,128)} %copy.41), calls=%async_computation.4 | async-start | bytes 1048576 | tf_op jit(solution)/shard_map/all_to_all | solution.py:101
  130.7 21.9 %all-to-all-start.5 = ((f32[32,8,512]{2,1,0:T(8,128)}), f32[32,8,512]{2,1,0:T(8,128)S(1)}, u32[]{:S(2)}, u32[]{:S(2)}) async-start(f32[32,8,512]{2,1,0:T(8,128)} %copy.44), calls=%async_computation.5 | async-start | bytes 1048576 | tf_op jit(solution)/shard_map/all_to_all | solution.py:101
  158.6 22.1 %all-to-all-start.6 = ((f32[32,8,512]{2,1,0:T(8,128)}), f32[32,8,512]{2,1,0:T(8,128)S(1)}, u32[]{:S(2)}, u32[]{:S(2)}) async-start(f32[32,8,512]{2,1,0:T(8,128)} %fusion.1), calls=%async_computation.6 | async-start | bytes 1048576 | tf_op jit(solution)/shard_map/all_to_all | solution.py:109
  180.7 21.9 %all-to-all-start.7 = ((f32[32,8,512]{2,1,0:T(8,128)}), f32[32,8,512]{2,1,0:T(8,128)S(1)}, u32[]{:S(2)}, u32[]{:S(2)}) async-start(f32[32,8,512]{2,1,0:T(8,128)} %fusion), calls=%async_computation.7 | async-start | bytes 1048576 | tf_op jit(solution)/shard_map/all_to_all | solution.py:109
  230.6 17.8 %all-to-all-start.9 = ((f32[16,16,512]{2,1,0:T(8,128)}), f32[16,16,512]{2,1,0:T(8,128)S(1)}, u32[]{:S(2)}, u32[]{:S(2)}) async-start(f32[16,16,512]{2,1,0:T(8,128)} %bitcast.17), calls=%async_computation.9 | async-start | bytes 1048576 | tf_op jit(solution)/shard_map/all_to_all | solution.py:92
  248.4 17.4 %all-to-all-start.10 = ((f32[16,16,512]{2,1,0:T(8,128)}), f32[16,16,512]{2,1,0:T(8,128)S(1)}, u32[]{:S(2)}, u32[]{:S(2)}) async-start(f32[16,16,512]{2,1,0:T(8,128)} %bitcast.19), calls=%async_computation.10 | async-start | bytes 1048576 | tf_op jit(solution)/shard_map/all_to_all | solution.py:92
  267.8 60.8 %copy-start = (f32[256,512]{1,0:T(8,128)S(1)}, f32[256,512]{1,0:T(8,128)}, u32[]{:S(2)}) copy-start(f32[256,512]{1,0:T(8,128)} %param.5) | copy-start | bytes 1572868
  267.8 60.8 %all-to-all-start.11 = ((f32[16,16,512]{2,1,0:T(8,128)}), f32[16,16,512]{2,1,0:T(8,128)S(1)}, u32[]{:S(2)}, u32[]{:S(2)}) async-start(f32[16,16,512]{2,1,0:T(8,128)} %copy.50), calls=%async_computation.11 | async-start | bytes 1048576 | tf_op jit(solution)/shard_map/all_to_all | solution.py:84
where the time goes:
time: 337 us; the launch traced here: 331 us
  blocking collectives  136 us (40%)
  waiting for transfers between devices  90.2 us (27%)
  starting transfers between devices  50.1 us (15%)
  matrix products  42.1 us (12%)
  local copies, waits for them, and re-layouts  6.02 us (2%)
  between operations  4.38 us (1%)
    psum x5, blocking collectives, over_axes(): array = lax.psum(array, axis)  54.9 us
    all_to_all x1, blocking collectives, across_rows(): lax.all_to_all(shaped, ROW, split_axis=0, concat_axis=0, tiled=True)  34.1 us
    all_to_all x2, waiting for transfers between devices, across_rows(): lax.all_to_all(shaped, ROW, split_axis=0, concat_axis=0, tiled=True)  29.9 us
    all_to_all x2, waiting for transfers between devices, handle(): return lax.all_to_all(mixed, ROW, split_axis=0, concat_axis=0, tiled=True)  29.1 us
    all_to_all x1, blocking collectives, across_columns(): lax.all_to_all(shaped, COL, split_axis=0, concat_axis=0, tiled=True)  26.4 us
    all_to_all x1, blocking collectives, handle(): return lax.all_to_all(mixed, ROW, split_axis=0, concat_axis=0, tiled=True)  20.6 us
    all_to_all x3, starting transfers between devices, handle(): return lax.all_to_all(mixed, COL, split_axis=0, concat_axis=0, tiled=True)  18.8 us
    all_to_all x2, waiting for transfers between devices, across_columns(): lax.all_to_all(shaped, COL, split_axis=0, concat_axis=0, tiled=True)  16.4 us
  transfers between devices with their start and end apart: 9, of which 8 were waited for; matrix products, arithmetic and copies ran while one was open for 7% of the time, Pallas kernels for 0%

commit v1 on v0

v1 whole, which is shorter than its diff:
```python
import numpy as np
import jax
import jax.numpy as jnp
from jax import lax
from jax.sharding import PartitionSpec as P

ROW = "row"
COL = "col"
LANES = 128

HI = lax.Precision.HIGHEST


def mm(a, b, dims):
    return lax.dot_general(a, b, (dims, ((), ())), precision=HI)


def cosines(length):
    wave = np.arange(length)[:, None]
    place = np.arange(length)[None, :]
    angle = np.pi * (wave * (2 * place + 1) % (4 * length)) / (2 * length)
    scale = np.where(wave == 0, np.sqrt(1.0 / length), np.sqrt(2.0 / length))
    return scale * np.cos(angle)


def stiffness(waves, length):
    return 4.0 * np.sin(np.pi * waves / (2 * length)) ** 2


def sines(blocks):
    index = np.arange(blocks + 1)
    table = np.sqrt(2.0 / blocks) * np.sin(np.pi * (index[:, None] * index[None, :] % (2 * blocks)) / blocks)
    table[blocks] = 0.0
    return table[:, :blocks]


def block_constants(extent, blocks):
    table = cosines(extent)
    edge = table[:, 0]
    sign = np.where(np.arange(extent) % 2 == 0, 1.0, -1.0)
    dst = sines(blocks)
    theta = np.cos(np.pi * np.arange(blocks) / blocks)
    return dict(
        table=table,
        lam=stiffness(np.arange(extent), extent),
        edges=np.stack([edge, edge * sign]),
        squares=np.stack([edge**2 * (1 + sign), edge**2 * (1 - sign)]),
        dst=dst[:blocks],
        after=dst[1:],
        gaps=np.stack([1 - theta, 1 + theta], axis=1),
    )


def wave_constants(extent, blocks):
    length = extent * blocks
    half = extent // 2
    kind = np.arange(blocks)
    block = np.arange(blocks)
    angle = np.pi * (kind[:, None] * block[None, :] % (2 * blocks)) / blocks
    parity = np.where(block % 2 == 0, 1.0, -1.0)
    mix = np.stack([np.cos(angle), np.where(kind[:, None] > 0, np.sin(angle), parity[None, :])], axis=1)
    first = kind
    second = np.where(kind == 0, blocks, 2 * blocks - kind)
    place = 2 * np.arange(extent) + 1
    phase_one = np.pi * (first[:, None] * place[None, :] % (4 * length)) / (2 * length)
    phase_two = np.pi * (second[:, None] * place[None, :] % (4 * length)) / (2 * length)
    inner = (kind > 0)[:, None] * 1.0
    twiddle = np.stack(
        [
            np.cos(phase_one),
            -inner * np.sin(phase_one),
            -np.sin(phase_one),
            -inner * np.cos(phase_one),
            inner * np.cos(phase_two),
            np.where(kind[:, None] > 0, np.sin(phase_two), np.cos(phase_two)),
            -inner * np.sin(phase_two),
            np.where(kind[:, None] > 0, np.cos(phase_two), -np.sin(phase_two)),
        ],
        axis=1,
    )
    twiddle[0, 2] = 0.0
    steps = np.arange(half)
    fine = np.pi * (steps[None, :] * place[:, None] % (2 * extent)) / extent
    waves = np.stack([first, second], axis=1)[:, :, None] + 2 * blocks * steps[None, None, :]
    energy = np.where(waves == 0, 1.0 / length, 2.0 / length)
    return dict(
        mix=mix,
        twiddle=twiddle,
        fine=np.concatenate([np.cos(fine), np.sin(fine)], axis=0),
        lam=stiffness(waves, length),
        energy=energy,
    )


def f32(table):
    return jnp.asarray(np.asarray(table, np.float32))


def pick(table, index):
    return lax.dynamic_index_in_dim(f32(table), index, 0, keepdims=False)


def gather(payload, axis):
    return lax.all_gather(payload, axis)


def pack(pieces):
    flat = [piece.reshape(-1) for piece in pieces]
    size = sum(piece.shape[0] for piece in flat)
    return jnp.concatenate(flat).reshape(size // LANES, LANES)


def spread(value):
    return jnp.full((LANES,), value)


def body(row_of, col_of, waves_of, field, direction, ground, previous):
    rows, cols = field.shape
    row_count = row_of["dst"].shape[0]
    col_count = col_of["dst"].shape[0]
    half = rows // 2
    me_row = lax.axis_index(ROW)
    me_col = lax.axis_index(COL)
    g = ground[0]

    row_table, col_table = f32(row_of["table"]), f32(col_of["table"])
    top, bottom = f32(row_of["edges"][0])[:, None], f32(row_of["edges"][1])[:, None]
    left, right = f32(col_of["edges"][0])[None, :], f32(col_of["edges"][1])[None, :]

    weight = 1.0 / (f32(row_of["lam"])[:, None] + f32(col_of["lam"])[None, :] + g)
    block = mm(row_table, mm(field, col_table, ((1,), (1,))), ((1,), (0,)))
    solved = weight * block

    sums = mm(f32(row_of["squares"]), weight, ((1,), (0,)))
    gaps = f32(row_of["gaps"])
    row_inverse = 1.0 / (1.0 + gaps[:, :1] * sums[:1] + gaps[:, 1:] * sums[1:])
    lam_here = pick(waves_of["lam"], me_row).reshape(1, rows)
    long_weight = 1.0 / (f32(col_of["lam"])[:, None] + lam_here + g)
    sums = mm(f32(col_of["squares"]), long_weight, ((1,), (0,)))
    gaps = f32(col_of["gaps"])
    col_inverse = pick(waves_of["energy"], me_row).reshape(1, rows) / (
        1.0 + gaps[:, :1] * sums[:1] + gaps[:, 1:] * sums[1:]
    )

    row_edges = mm(f32(row_of["edges"]), solved, ((1,), (0,)))
    col_edges = mm(f32(col_of["edges"]), solved, ((1,), (1,)))
    energy = jnp.sum(solved * block)
    seen = gather(pack([row_edges, col_edges, spread(energy)]), ROW).reshape(row_count, -1)
    tops, bottoms = seen[:, :cols], seen[:, cols : 2 * cols]
    lefts, rights = seen[:, 2 * cols : 2 * cols + rows], seen[:, 2 * cols + rows : 2 * cols + 2 * rows]
    energy = jnp.sum(seen[:, 2 * cols + 2 * rows])

    dst, after = row_of["dst"], row_of["after"]
    jumps = mm(f32(np.concatenate([after.T, -dst.T], axis=1)), jnp.concatenate([bottoms, tops], axis=0), ((1,), (0,)))
    bends = row_inverse * jumps
    energy = energy - jnp.sum(bends * jumps)

    sides = mm(
        jnp.concatenate([bends * left, bends * right], axis=0), weight, ((1,), (1,))
    )
    mix = waves_of["mix"]
    mix_here = pick(np.concatenate([mix, mix @ dst, mix @ after], axis=2), me_row)
    mixed = []
    for which, side in ((0, lefts), (1, rights)):
        part = sides[which * row_count : (which + 1) * row_count]
        mixed.append(
            mm(mix_here[:, :row_count], side, ((1,), (0,)))
            + mm(mix_here[:, row_count : 2 * row_count], part, ((1,), (0,))) * top.T
            - mm(mix_here[:, 2 * row_count :], part, ((1,), (0,))) * bottom.T
        )
    in_place = mm(jnp.concatenate(mixed, axis=0), row_table, ((1,), (0,))).reshape(2, 2, rows)
    real, imag = in_place[:, 0], in_place[:, 1]
    tw = pick(waves_of["twiddle"], me_row)
    fine = f32(waves_of["fine"])
    first = jnp.concatenate([real * tw[0] + imag * tw[1], real * tw[2] + imag * tw[3]], axis=1)
    second = jnp.concatenate([real * tw[4] + imag * tw[5], real * tw[6] + imag * tw[7]], axis=1)
    waves = mm(jnp.concatenate([first, second], axis=0), fine, ((1,), (0,)))
    waves = jnp.concatenate([waves[:2], waves[2:]], axis=1)

    seen = gather(pack([waves, spread(energy)]), COL).reshape(col_count, -1)
    energy = jnp.sum(seen[:, 2 * rows])
    dst_c, after_c = col_of["dst"], col_of["after"]
    leaps = mm(
        f32(np.concatenate([after_c.T, -dst_c.T], axis=1)),
        jnp.concatenate([seen[:, rows : 2 * rows], seen[:, :rows]], axis=0),
        ((1,), (0,)),
    )
    folds = col_inverse * leaps
    fold_energy = jnp.sum(folds * leaps)
    mine = mm(pick(np.stack([dst_c, after_c], axis=1), me_col), folds, ((1,), (0,)))
    back = mm(jnp.concatenate([mine[:, :half], mine[:, half:]], axis=0), fine, ((1,), (1,)))
    c_one, s_one, c_two, s_two = back[:2, :rows], back[:2, rows:], back[2:, :rows], back[2:, rows:]
    real = c_one * tw[0] + s_one * tw[2] + c_two * tw[4] + s_two * tw[6]
    imag = c_one * tw[1] + s_one * tw[3] + c_two * tw[5] + s_two * tw[7]
    hats = mm(jnp.concatenate([real, imag], axis=0), row_table, ((1,), (1,)))

    seen = gather(pack([hats, spread(fold_energy)]), ROW).reshape(row_count, -1)
    energy = energy - jnp.sum(seen[:, 4 * rows])
    parts = seen[:, : 4 * rows].reshape(row_count, 2, 2, rows)
    unmix = np.concatenate([mix[:, 0].T, mix[:, 1].T], axis=1)
    spectra = jnp.concatenate([parts[:, 0], parts[:, 1]], axis=0).reshape(2 * row_count, 2 * rows)
    here = mm(pick(unmix, me_row)[None], spectra, ((1,), (0,)))
    side_left, side_right = here[:, :rows].T, here[:, rows:].T
    pulls = mm(f32(np.concatenate([after.T @ unmix, dst.T @ unmix], axis=0)), spectra, ((1,), (0,)))
    pulls_left = pulls[:row_count, :rows] * bottom.T - pulls[row_count:, :rows] * top.T
    pulls_right = pulls[:row_count, rows:] * bottom.T - pulls[row_count:, rows:] * top.T
    pulled = mm(jnp.concatenate([pulls_left, pulls_right], axis=0), weight, ((1,), (0,)))
    jumps = jumps + left * pulled[:row_count] - right * pulled[row_count:]
    ends = mm(pick(np.stack([dst, after], axis=1), me_row), row_inverse * jumps, ((1,), (0,)))
    spectrum = weight * (
        block + top * ends[:1] - bottom * ends[1:] + side_left * left - side_right * right
    )
    precond = mm(row_table, mm(spectrum, col_table, ((1,), (0,))), ((0,), (0,)))
    ratio = energy / previous[0]
    return precond + ratio * direction, jnp.reshape(ratio, (1,))


def build(row_count, col_count, rows, cols):
    row_of = block_constants(rows, row_count)
    col_of = block_constants(cols, col_count)
    waves_of = wave_constants(rows, row_count)

    def run(field, direction, ground, previous):
        return body(row_of, col_of, waves_of, field, direction, ground, previous)

    return run


def solution(mesh):
    row_count, col_count = mesh.shape[ROW], mesh.shape[COL]

    def step(residual, direction, ground_shift, previous):
        rows, cols = residual.shape[0] // row_count, residual.shape[1] // col_count
        return jax.shard_map(
            build(row_count, col_count, rows, cols),
            mesh=mesh,
            in_specs=(P(ROW, COL), P(ROW, COL), P(), P()),
            out_specs=(P(ROW, COL), P()),
            check_vma=False,
        )(residual, direction, ground_shift, previous)

    return step
```

time: 337 us -> 154 us (0.46); the launches traced: 331 us -> 153 us
  waiting for transfers between devices: 90.2 us -> 0 us
  starting transfers between devices: 50.1 us -> 0 us
  matrix products: 42.1 us -> 16.7 us
  blocking collectives: 136 us -> 117 us
  local copies, waits for them, and re-layouts: 6.02 us -> 11.1 us
    all_gather x0 -> x3, blocking collectives: none -> 117 us  [gather(): return lax.all_gather(payload, axis)]
    all_to_all x9 -> x0, waiting for transfers between devices: 90.2 us -> none  [the longest x2 29.9 us: across_rows(): lax.all_to_all(shaped, ROW, split_axis=0, concat_axis=0, tiled=True)]
    all_to_all x3 -> x0, blocking collectives: 81.1 us -> none  [the longest x1 34.1 us: across_rows(): lax.all_to_all(shaped, ROW, split_axis=0, concat_axis=0, tiled=True)]
    psum x5 -> x0, blocking collectives: 54.9 us -> none  [over_axes(): array = lax.psum(array, axis)]
    all_to_all x9 -> x0, starting transfers between devices: 50.1 us -> none  [the longest x3 18.8 us: handle(): return lax.all_to_all(mixed, COL, split_axis=0, concat_axis=0, tiled=True)]
    dot_general x24 -> x29, matrix products: 42.1 us -> 16.7 us  [mm(): return lax.dot_general(a, b, (dims, ((), ())), precision=HI)]
    unnamed x2 -> x59, local copies, waits for them, and re-layouts: 0.01 us -> 7.05 us
    dot_general x4 -> x0, local copies, waits for them, and re-layouts: 4.41 us -> none  [the longest x2 2.21 us: combine(): imag_part = jnp.einsum('td,dab->tab', mix_sin, source, precision=PRECISE)]
  transfers between devices with their start and end apart: 9 -> 0, of which waited for: 8 -> 0; matrix products, arithmetic and copies ran while one was open for 7% -> 0% of each run, Pallas kernels for 0% -> 0%
where the time goes in v1:
time: 154 us; the launch traced here: 153 us
  blocking collectives  117 us (76%)
  matrix products  16.7 us (11%)
  local copies, waits for them, and re-layouts  11.1 us (7%)
  between operations  6.07 us (4%)
  other arithmetic  2 us (1%)
    all_gather x3, blocking collectives, gather(): return lax.all_gather(payload, axis)  117 us
    dot_general x29, matrix products, mm(): return lax.dot_general(a, b, (dims, ((), ())), precision=HI)  16.7 us
    unnamed x59, local copies, waits for them, and re-layouts  7.05 us

profile of v1, /device:TPU:1, one launch (start us, length us, event | category | flops | bytes accessed | tf_op | source)
XLA Modules:
  0.0 153.2 jit_solution(14081233854780895186)
XLA Ops:
  0.6 0.0 copy-start
  1.3 0.3 copy-done
  1.7 2.3 %fusion.122 = f32[512,256]{1,0:T(8,128)S(1)} fusion(f32[512,512]{1,0:T(8,128)} %constant.96.clone, f32[256,512]{1,0:T(8,128)S(1)} %copy-done), kind=kOutput, calls=%fused_computation.179 | convolution fusion | flops 805306368 | bytes 2097152 | tf_op jit(solution)/shard_map/dot_general | solution.py:15
  4.0 1.3 multiply_reduce_fusion
  5.3 0.7 copy-done.19
  6.0 0.5 convolution_bitcast_fusion
  6.5 0.7 copy-done.14
  7.2 0.6 convolution_bitcast_fusion.2
  7.8 0.7 broadcast_in_dim.2
  8.5 37.8 %all_gather.9 = f32[32,13,128]{2,1,0:T(8,128)S(1)} all-gather(f32[1,13,128]{2,1,0:T(8,128)S(1)} %maximum_bitcast_fusion), channel_id=1, replica_groups=mesh['row'=32,'col'=16] {'row'}, dimensions={0}, use_global_device_ids=true | all-gather | bytes 219648 | tf_op jit(solution)/shard_map/all_gather | solution.py:104
  46.3 0.1 copy.70
  46.4 0.6 copy-done.7
  47.0 0.2 fusion.48
  47.2 0.5 copy-done.18
  47.7 0.5 fusion.31
  48.2 0.0 copy-start.21
  48.2 0.0 copy-start.22
  48.2 0.2 copy-done.11
  48.4 0.5 copy-done.16
  48.9 0.8 multiply_reduce_fusion.1
  49.7 0.7 fusion.29
  50.4 0.0 copy-start.8
  50.4 0.7 fusion.89
  51.1 0.2 convolution_multiply_fusion.3
  51.3 0.5 copy-done.9
  51.8 0.2 convolution_multiply_fusion.2
  52.0 0.1 fusion.3
  52.1 0.0 copy-start.3
  52.1 0.2 convolution_multiply_fusion.1
  52.3 0.2 convolution_multiply_fusion
  52.5 0.1 fusion.4
  52.7 0.2 fusion.81
  52.9 1.0 constant_dynamic-slice_fusion.6
  54.0 0.2 fusion.79
  54.2 0.7 slice_reduce_fusion.1
  56.2 41.3 %all_gather.10 = f32[16,5,128]{2,1,0:T(8,128)S(1)} all-gather(f32[1,5,128]{2,1,0:T(8,128)S(1)} %pad_bitcast_fusion.1), channel_id=1, replica_groups=mesh['row'=32,'col'=16] {'col'}, dimensions={0}, use_global_device_ids=true | all-gather | bytes 43520 | tf_op jit(solution)/shard_map/all_gather | solution.py:104
  97.5 0.7 copy-done.10
  98.2 0.1 fusion.70
  98.3 0.0 copy-start.13
  98.3 0.7 fusion.87
  99.0 0.4 fusion.15
  99.4 0.1 fusion.120
  99.5 0.0 copy-start.23
  99.5 0.0 copy-start.24
  99.5 0.7 copy-done.12
  100.2 0.7 multiply_reduce_fusion.2
  100.9 0.9 fusion.72
  101.8 0.3 fusion.82
  102.1 0.3 convolution_bitcast_fusion.1
  102.4 0.7 pad_bitcast_fusion
  103.1 38.3 %all_gather.11 = f32[32,9,128]{2,1,0:T(8,128)S(1)} all-gather(f32[1,9,128]{2,1,0:T(8,128)S(1)} %pad_bitcast_fusion), channel_id=1, replica_groups=mesh['row'=32,'col'=16] {'row'}, dimensions={0}, use_global_device_ids=true | all-gather | bytes 152064 | tf_op jit(solution)/shard_map/all_gather | solution.py:104
  141.5 0.1 copy.71
  141.5 0.7 slice_reduce_fusion
  142.2 0.6 slice_reduce_fusion.2
  144.8 0.1 reshape.84
  144.9 0.7 copy-done.5
  145.7 0.3 fusion.123
  146.0 0.7 copy-done.6
  146.7 0.3 fusion
  147.0 0.5 fusion.28
  147.5 0.9 fusion.43
  148.5 0.9 fusion.37
  149.4 1.3 fusion.5
  150.7 1.4 convolution_add_fusion
  (52 shorter events, 0.3 us)
Async XLA Ops:
  0.6 1.1 copy-start
  1.7 2.3 %copy-start.1 = (f32[256,256]{1,0:T(8,128)S(1)}, f32[256,256]{1,0:T(8,128)}, u32[]{:S(2)}) copy-start(f32[256,256]{1,0:T(8,128)} %constant.95.clone) | copy-start | bytes 786436
  1.7 2.3 %copy-start.15 = (f32[512]{0:T(512)S(1)}, f32[512]{0:T(512)}, u32[]{:S(2)}) copy-start(f32[512]{0:T(512)} %constant.102.clone) | copy-start | bytes 6148
  1.7 2.3 %copy-start.20 = (f32[256]{0:T(256)S(1)}, f32[256]{0:T(256)}, u32[]{:S(2)}) copy-start(f32[256]{0:T(256)} %constant.101.clone) | copy-start | bytes 3076
  5.3 0.7 copy-start.19
  6.5 0.7 copy-start.14
  46.3 0.7 copy-start.7
  47.0 0.7 copy-start.18
  47.7 0.7 copy-start.11
  47.7 0.7 copy-start.17
  48.2 0.7 copy-start.16
  48.2 0.7 copy-start.21
  48.2 0.7 copy-start.22
  50.4 0.7 copy-start.8
  51.1 0.7 copy-start.9
  52.1 1.9 %copy-start.3 = (f32[512,128]{1,0:T(8,128)S(1)}, f32[512,128]{1,0:T(8,128)}, u32[]{:S(2)}) copy-start(f32[512,128]{1,0:T(8,128)} %constant.114.clone) | copy-start | bytes 786436
  97.5 0.7 copy-start.10
  98.3 0.7 copy-start.13
  99.4 0.7 copy-start.12
  99.5 0.7 copy-start.23
  99.5 0.7 copy-start.24
  144.9 0.8 copy-start.5
  145.9 0.8 copy-start.6
  147.0 2.4 %copy-start.2 = (f32[512,512]{1,0:T(8,128)S(1)}, f32[512,512]{1,0:T(8,128)}, u32[]{:S(2)}) copy-start(f32[512,512]{1,0:T(8,128)} %constant.96.clone) | copy-start | bytes 3145732
  149.3 1.3 copy-start.4

commit v2 on v1

--- a/solution.py
+++ b/solution.py
@@ -101,13 +101,16 @@
 
 
 def gather(payload, axis):
-    return lax.all_gather(payload, axis)
+    copies = jnp.broadcast_to(payload[None], (lax.axis_size(axis),) + payload.shape)
+    return lax.all_to_all(copies, axis, 0, 0, tiled=True)
 
 
 def pack(pieces):
     flat = [piece.reshape(-1) for piece in pieces]
     size = sum(piece.shape[0] for piece in flat)
-    return jnp.concatenate(flat).reshape(size // LANES, LANES)
+    full = -(-size // (8 * LANES)) * 8 * LANES
+    flat.append(jnp.zeros((full - size,), jnp.float32))
+    return jnp.concatenate(flat).reshape(full // LANES, LANES)
 
 
 def spread(value):

time: 154 us -> 92.2 us (0.60)
  blocking collectives: 117 us -> 0 us
  starting transfers between devices: 0 us -> 28.4 us
  waiting for transfers between devices: 0 us -> 26 us
    all_gather x3 -> x0, blocking collectives: 117 us -> none  [gather(): return lax.all_gather(payload, axis)]
    all_to_all x0 -> x3, starting transfers between devices: none -> 28.4 us  [gather(): return lax.all_to_all(copies, axis, 0, 0, tiled=True)]
    all_to_all x0 -> x3, waiting for transfers between devices: none -> 26 us  [gather(): return lax.all_to_all(copies, axis, 0, 0, tiled=True)]
    broadcast_in_dim x0 -> x4, local copies, waits for them, and re-layouts: none -> 2.08 us  [the longest x3 2.08 us: gather(): jnp.broadcast_to(payload[None], (lax.axis_size(axis),) + payload.shape)]
  transfers between devices with their start and end apart: 0 -> 3, of which waited for: 0 -> 3; matrix products, arithmetic and copies ran while one was open for 0% -> 4% of each run, Pallas kernels for 0% -> 0%
where the time goes in v2:
time: 92.2 us; the launch traced here: 91.1 us
  starting transfers between devices  28.4 us (31%)
  waiting for transfers between devices  26 us (28%)
  matrix products  16.7 us (18%)
  local copies, waits for them, and re-layouts  12 us (13%)
  between operations  6.21 us (7%)
  other arithmetic  1.89 us (2%)
    all_to_all x3, starting transfers between devices, gather(): return lax.all_to_all(copies, axis, 0, 0, tiled=True)  28.4 us
    all_to_all x3, waiting for transfers between devices, gather(): return lax.all_to_all(copies, axis, 0, 0, tiled=True)  26 us
    dot_general x29, matrix products, mm(): return lax.dot_general(a, b, (dims, ((), ())), precision=HI)  16.7 us
    unnamed x59, local copies, waits for them, and re-layouts  5.96 us
    broadcast_in_dim x3, local copies, waits for them, and re-layouts, gather(): jnp.broadcast_to(payload[None], (lax.axis_size(axis),) + payload.shape)  2.08 us
  transfers between devices with their start and end apart: 3, of which 3 were waited for; matrix products, arithmetic and copies ran while one was open for 4% of the time, Pallas kernels for 0%

profile of v2, /device:TPU:1, one launch (start us, length us, event | category | flops | bytes accessed | tf_op | source)
XLA Modules:
  0.0 91.1 jit_solution(8704936120840662122)
XLA Ops:
  0.6 0.0 copy-start
  1.3 0.3 copy-done
  1.7 2.3 %fusion.122 = f32[512,256]{1,0:T(8,128)S(1)} fusion(f32[512,512]{1,0:T(8,128)} %constant.98.clone, f32[256,512]{1,0:T(8,128)S(1)} %copy-done), kind=kOutput, calls=%fused_computation.179 | convolution fusion | flops 805306368 | bytes 2097152 | tf_op jit(solution)/shard_map/dot_general | solution.py:15
  4.0 0.0 copy-start.20
  4.0 0.7 copy-done.20
  4.7 1.3 %multiply_reduce_fusion = (f32[]{:T(128)}, f32[256,512]{1,0:T(8,128)S(1)}) fusion(f32[]{:T(128)} %bitcast.127, f32[512]{0:T(512)S(1)} %copy-done.15, f32[256]{0:T(256)S(1)} %copy-done.20, f32[256,256]{1,0:T(8,128)S(1)} %copy-done.1, f32[512,256]{1,0:T(8,128)S(1)} %fusion.122), kind=kOutput, calls=%fused_computation.29 | convolution fusion | flops 403439616 | bytes 1313800 | tf_op jit(solution)/shard_map/dot_general | solution.py:15
  6.0 0.6 convolution_bitcast_fusion.2
  6.6 0.7 copy-done.19
  7.3 0.5 convolution_bitcast_fusion
  7.8 0.7 broadcast_in_dim.20
  8.5 0.7 broadcast_in_dim.43
  9.2 10.6 %all-to-all-start = ((f32[32,16,128]{2,1,0:T(8,128)}), f32[32,16,128]{2,1,0:T(8,128)S(1)}, u32[]{:S(2)}, u32[]{:S(2)}) async-start(f32[32,16,128]{2,1,0:T(8,128)} %broadcast_in_dim.43), calls=%async_computation | async-start | bytes 524288 | tf_op jit(solution)/shard_map/all_to_all | solution.py:105
  19.8 0.7 copy-done.18
  20.5 0.5 fusion.31
  20.9 0.7 fusion.87
  21.7 1.0 %constant_dynamic-slice_fusion.6 = (f32[1,1,256]{2,1,0:T(1,128)S(1)}, f32[1,1,256]{2,1,0:T(1,128)S(1)}, f32[1,1,256]{2,1,0:T(1,128)S(1)}, f32[1,1,256]{2,1,0:T(1...) fusion(f32[32,8,256]{2,1,0:T(8,128)} %constant.115.clone, ...), kind=kLoop, calls=%fused_computation.124 | loop fusion | bytes 16416 | tf_op jit(solution)/shard_map/slice | solution.py:178
  22.6 0.7 fusion.89
  23.3 0.7 copy-done.13
  24.0 0.4 fusion.15
  24.4 6.8 %all-to-all-done = f32[32,16,128]{2,1,0:T(8,128)S(1)} async-done(((f32[32,16,128]{2,1,0:T(8,128)}), f32[32,16,128]{2,1,0:T(8,128)S(1)}, u32[]{:S(2)}, u32[]{:S(2)}) %all-to-all-start) | async-done | bytes 262176 | tf_op jit(solution)/shard_map/all_to_all | solution.py:105
  31.2 0.1 copy.80
  31.3 0.6 slice_reduce_fusion.1
  31.9 0.1 copy-done.7
  32.0 0.2 fusion.48
  32.3 0.5 copy-done.11
  32.7 0.2 copy-done.16
  32.9 0.8 broadcast_multiply_fusion.1
  33.7 0.7 fusion.29
  34.4 0.2 convolution_multiply_fusion.2
  34.6 0.2 convolution_multiply_fusion
  34.8 0.0 copy-done.9
  34.8 0.2 convolution_multiply_fusion.1
  35.0 0.2 convolution_multiply_fusion.3
  35.2 0.1 fusion.3
  35.4 0.1 fusion.4
  35.5 0.2 fusion.81
  35.8 0.2 fusion.79
  37.4 0.6 broadcast_in_dim.46
  38.1 11.7 %all-to-all-start.1 = ((f32[16,8,128]{2,1,0:T(8,128)}), f32[16,8,128]{2,1,0:T(8,128)S(1)}, u32[]{:S(2)}, u32[]{:S(2)}) async-start(f32[16,8,128]{2,1,0:T(8,128)} %broadcast_in_dim.46), calls=%async_computation.1 | async-start | bytes 131072 | tf_op jit(solution)/shard_map/all_to_all | solution.py:105
  49.8 8.9 %all-to-all-done.1 = f32[16,8,128]{2,1,0:T(8,128)S(1)} async-done(((f32[16,8,128]{2,1,0:T(8,128)}), f32[16,8,128]{2,1,0:T(8,128)S(1)}, u32[]{:S(2)}, u32[]{:S(2)}) %all-to-all-start.1) | async-done | bytes 65568 | tf_op jit(solution)/shard_map/all_to_all | solution.py:105
  58.7 0.7 copy-done.10
  59.4 0.1 fusion.70
  59.5 0.0 copy-start.12
  59.6 0.7 copy-done.12
  60.3 0.7 multiply_reduce_fusion.2
  61.0 0.9 fusion.72
  61.9 0.3 fusion.82
  62.2 0.3 convolution_bitcast_fusion.1
  62.5 0.7 broadcast_in_dim.47
  63.3 0.7 broadcast_in_dim.50
  64.0 6.2 %all-to-all-start.2 = ((f32[32,16,128]{2,1,0:T(8,128)}), f32[32,16,128]{2,1,0:T(8,128)S(1)}, u32[]{:S(2)}, u32[]{:S(2)}) async-start(f32[32,16,128]{2,1,0:T(8,128)} %broadcast_in_dim.50), calls=%async_computation.2 | async-start | bytes 524288 | tf_op jit(solution)/shard_map/all_to_all | solution.py:105
  70.8 0.6 slice_reduce_fusion.2
  71.4 10.2 %all-to-all-done.2 = f32[32,16,128]{2,1,0:T(8,128)S(1)} async-done(((f32[32,16,128]{2,1,0:T(8,128)}), f32[32,16,128]{2,1,0:T(8,128)S(1)}, u32[]{:S(2)}, u32[]{:S(2)}) %all-to-all-start.2) | async-done | bytes 262176 | tf_op jit(solution)/shard_map/all_to_all | solution.py:105
  81.6 0.1 copy.79
  81.7 0.6 slice_reduce_fusion
  82.3 0.1 reshape.87
  82.5 0.9 fusion.37
  83.4 0.3 fusion.123
  83.7 0.5 copy-done.6
  84.1 0.3 fusion
  84.4 0.5 fusion.28
  85.0 0.9 %fusion.43 = f32[2,512]{1,0:T(2,128)S(1)} fusion(f32[64,512]{1,0:T(8,128)S(1)} %fusion.28, f32[32,512]{1,0:T(8,128)S(1)} %get-tuple-element.39, f32[512]{0:T(512)S(1)} %copy-done.16, f32[512]{0:T(512)S(1)} %copy-done.17, f32[512]{0:T(512)S(1)} %bitcast.172, f32[32]{0:T(128)S(1)} %copy-done.21, f32[512]{0:T(512)S(1)} %bitcast.170, f32[32]{0:T(128)S(1)} %copy-done.22, ...), kind=kOutput, calls=%fused_computation.61 | convolution fusion | flops 557056 | bytes 210180 | tf_op jit(solution)/shard_map/dot_general | solution.py:15
  87.3 1.3 %fusion.5 = f32[256,512]{1,0:T(8,128)S(1)} fusion(f32[512,512]{1,0:T(8,128)S(1)} %copy-done.2, f32[256,512]{1,0:T(8,128)S(1)} %get-tuple-element.38, f32[512]{0:T(512)S(1)} %copy-done.16, f32[256]{0:T(256)S(1)} %bitcast.176, f32[512]{0:T(512)S(1)} %copy-done.17, f32[256]{0:T(256)S(1)} %bitcast.175, f32[512]{0:T(512)S(1)} %bitcast.174, ...), kind=kOutput, calls=%fused_computation.18 | convolution fusion | flops 806879232 | bytes 2112516 | tf_op jit(solution)/shard_map/dot_general | solution.py:15
  88.6 1.4 %convolution_add_fusion = f32[256,512]{1,0:T(8,128)} fusion(f32[256,256]{1,0:T(8,128)S(1)} %copy-done.1, f32[256,512]{1,0:T(8,128)S(1)} %fusion.5, f32[256,512]{1,0:T(8,128)S(1)} %copy-done.4, f32[]{:T(128)} %div.36), kind=kOutput, calls=%fused_computation | convolution fusion | flops 402915328 | bytes 1835012 | tf_op jit(solution)/shard_map/dot_general | solution.py:15
  (62 shorter events, 0.4 us)
Async XLA Ops:
  0.6 1.1 %copy-start = (f32[256,512]{1,0:T(8,128)S(1)}, f32[256,512]{1,0:T(8,128)}, u32[]{:S(2)}) copy-start(f32[256,512]{1,0:T(8,128)} %param.30) | copy-start | bytes 1572868
  1.7 2.3 %copy-start.1 = (f32[256,256]{1,0:T(8,128)S(1)}, f32[256,256]{1,0:T(8,128)}, u32[]{:S(2)}) copy-start(f32[256,256]{1,0:T(8,128)} %constant.97.clone) | copy-start | bytes 786436
  1.7 2.3 %copy-start.15 = (f32[512]{0:T(512)S(1)}, f32[512]{0:T(512)}, u32[]{:S(2)}) copy-start(f32[512]{0:T(512)} %constant.104.clone) | copy-start | bytes 6148
  4.0 0.7 copy-start.20
  4.7 1.3 %copy-start.14 = (f32[2,512]{1,0:T(2,128)S(1)}, f32[2,512]{1,0:T(2,128)}, u32[]{:S(2)}) copy-start(f32[2,512]{1,0:T(2,128)} %constant.112.clone) | copy-start | bytes 12292
  6.6 0.7 copy-start.19
  9.2 22.0 %all-to-all-start = ((f32[32,16,128]{2,1,0:T(8,128)}), f32[32,16,128]{2,1,0:T(8,128)S(1)}, u32[]{:S(2)}, u32[]{:S(2)}) async-start(f32[32,16,128]{2,1,0:T(8,128)} %broadcast_in_dim.43), calls=%async_computation | async-start | bytes 524288 | tf_op jit(solution)/shard_map/all_to_all | solution.py:105
  19.8 0.7 copy-start.18
  23.3 0.7 copy-start.13
  31.3 0.7 copy-start.7
  32.0 0.7 copy-start.11
  32.0 0.7 copy-start.17
  32.2 0.7 copy-start.16
  32.2 0.7 copy-start.21
  32.2 0.7 copy-start.22
  33.7 0.7 copy-start.8
  33.7 1.1 %copy-start.9 = (f32[256]{0:T(256)S(1)}, f32[256]{0:T(256)}, u32[]{:S(2)}) copy-start(f32[256]{0:T(256)} %constant.99.clone) | copy-start | bytes 3076
  34.6 1.2 %copy-start.3 = (f32[512,128]{1,0:T(8,128)S(1)}, f32[512,128]{1,0:T(8,128)}, u32[]{:S(2)}) copy-start(f32[512,128]{1,0:T(8,128)} %constant.116.clone) | copy-start | bytes 786436
  38.1 20.7 %all-to-all-start.1 = ((f32[16,8,128]{2,1,0:T(8,128)}), f32[16,8,128]{2,1,0:T(8,128)S(1)}, u32[]{:S(2)}, u32[]{:S(2)}) async-start(f32[16,8,128]{2,1,0:T(8,128)} %broadcast_in_dim.46), calls=%async_computation.1 | async-start | bytes 131072 | tf_op jit(solution)/shard_map/all_to_all | solution.py:105
  58.7 0.7 copy-start.10
  59.5 0.7 copy-start.12
  59.6 0.7 copy-start.23
  59.6 0.7 copy-start.24
  64.0 17.6 %all-to-all-start.2 = ((f32[32,16,128]{2,1,0:T(8,128)}), f32[32,16,128]{2,1,0:T(8,128)S(1)}, u32[]{:S(2)}, u32[]{:S(2)}) async-start(f32[32,16,128]{2,1,0:T(8,128)} %broadcast_in_dim.50), calls=%async_computation.2 | async-start | bytes 524288 | tf_op jit(solution)/shard_map/all_to_all | solution.py:105
  82.5 0.9 copy-start.5
  83.4 0.8 copy-start.6
  84.4 2.8 %copy-start.2 = (f32[512,512]{1,0:T(8,128)S(1)}, f32[512,512]{1,0:T(8,128)}, u32[]{:S(2)}) copy-start(f32[512,512]{1,0:T(8,128)} %constant.98.clone) | copy-start | bytes 3145732
  87.3 1.3 %copy-start.4 = (f32[256,512]{1,0:T(8,128)S(1)}, f32[256,512]{1,0:T(8,128)}, u32[]{:S(2)}) copy-start(f32[256,512]{1,0:T(8,128)} %param.31) | copy-start | bytes 1572868

commit v3 on v1

v3 whole, which is shorter than its diff:
```python
import numpy as np
import jax
import jax.numpy as jnp
from jax import lax
from jax.experimental import pallas as pl
from jax.experimental.pallas import tpu as pltpu
from jax.sharding import PartitionSpec as P

ROW = "row"
COL = "col"
TILE = 8

HI = lax.Precision.HIGHEST


def cosines(length):
    wave = np.arange(length)[:, None]
    place = np.arange(length)[None, :]
    angle = np.pi * (wave * (2 * place + 1) % (4 * length)) / (2 * length)
    scale = np.where(wave == 0, np.sqrt(1.0 / length), np.sqrt(2.0 / length))
    return scale * np.cos(angle)


def stiffness(waves, length):
    return 4.0 * np.sin(np.pi * waves / (2 * length)) ** 2


def sines(blocks):
    index = np.arange(blocks + 1)
    table = np.sqrt(2.0 / blocks) * np.sin(np.pi * (index[:, None] * index[None, :] % (2 * blocks)) / blocks)
    table[blocks] = 0.0
    return table[:, :blocks]


def block_constants(extent, blocks):
    table = cosines(extent)
    edge = table[:, 0]
    sign = np.where(np.arange(extent) % 2 == 0, 1.0, -1.0)
    dst = sines(blocks)
    theta = np.cos(np.pi * np.arange(blocks) / blocks)
    return dict(
        table=table,
        lam=stiffness(np.arange(extent), extent),
        edges=np.stack([edge, edge * sign]),
        columns=np.stack([edge, edge * sign], axis=1),
        squares=np.stack([edge**2 * (1 + sign), edge**2 * (1 - sign)]),
        dst=dst[:blocks],
        after=dst[1:],
        gaps=np.stack([1 - theta, 1 + theta], axis=1),
    )


def wave_constants(extent, blocks):
    length = extent * blocks
    half = extent // 2
    kind = np.arange(blocks)
    block = np.arange(blocks)
    angle = np.pi * (kind[:, None] * block[None, :] % (2 * blocks)) / blocks
    parity = np.where(block % 2 == 0, 1.0, -1.0)
    mix = np.stack([np.cos(angle), np.where(kind[:, None] > 0, np.sin(angle), parity[None, :])], axis=1)
    first = kind
    second = np.where(kind == 0, blocks, 2 * blocks - kind)
    place = 2 * np.arange(extent) + 1
    phase_one = np.pi * (first[:, None] * place[None, :] % (4 * length)) / (2 * length)
    phase_two = np.pi * (second[:, None] * place[None, :] % (4 * length)) / (2 * length)
    inner = (kind > 0)[:, None] * 1.0
    twiddle = np.stack(
        [
            np.cos(phase_one),
            -inner * np.sin(phase_one),
            -np.sin(phase_one),
            -inner * np.cos(phase_one),
            inner * np.cos(phase_two),
            np.where(kind[:, None] > 0, np.sin(phase_two), np.cos(phase_two)),
            -inner * np.sin(phase_two),
            np.where(kind[:, None] > 0, np.cos(phase_two), -np.sin(phase_two)),
        ],
        axis=1,
    )
    twiddle[0, 2] = 0.0
    steps = np.arange(half)
    fine = np.pi * (steps[None, :] * place[:, None] % (2 * extent)) / extent
    waves = np.stack([first, second], axis=1)[:, :, None] + 2 * blocks * steps[None, None, :]
    energy = np.where(waves == 0, 1.0 / length, 2.0 / length)
    return dict(
        mix=mix,
        twiddle=twiddle,
        fine=np.concatenate([np.cos(fine), np.sin(fine)], axis=0),
        lam=stiffness(waves, length),
        energy=energy,
    )


def rows_of(height, width, placed):
    table = np.zeros((height, width))
    for at, row in placed.items():
        table[at] = row
    return table


def kernel_constants(rows, cols, row_count, col_count):
    row = block_constants(rows, row_count)
    col = block_constants(cols, col_count)
    wave = wave_constants(rows, row_count)
    half = rows // 2
    top, bottom = row["edges"]
    left, right = col["edges"]
    mix, dst, after = wave["mix"], row["dst"], row["after"]
    blank = np.zeros((row_count, row_count))

    send_low = rows_of(TILE, rows, {0: top, 2: bottom})
    send_high = rows_of(TILE, rows, {1: top, 3: bottom})
    send_side = rows_of(TILE, cols, {4: left, 5: right})

    def doubled(per_class):
        none = np.zeros_like(per_class)
        pair = [np.concatenate([per_class, none], 1), np.concatenate([none, per_class], 1)]
        zero = np.zeros((row_count, 2 * row_count))
        return np.stack(pair + pair + [zero] * 4, axis=1)

    classes = np.concatenate(
        [doubled(m) for m in (mix[:, 0], mix[:, 1], mix[:, 0] @ dst, mix[:, 1] @ dst, mix[:, 0] @ after, mix[:, 1] @ after)],
        axis=1,
    )
    dst_c, after_c = col["dst"], col["after"]
    gap = np.zeros((col_count, TILE * col_count))
    leaps_first, leaps_second, sum_energy = gap.copy(), gap.copy(), np.zeros((TILE, TILE * col_count))
    leaps_first[:, 1::TILE], leaps_first[:, 0::TILE] = after_c.T, -dst_c.T
    leaps_second[:, 3::TILE], leaps_second[:, 2::TILE] = after_c.T, -dst_c.T
    sum_energy[:, 4::TILE] = 1.0
    own_c = np.zeros((col_count, 2 * TILE, col_count))
    own_c[:, 0], own_c[:, 1] = dst_c, after_c
    own_c[:, TILE + 2], own_c[:, TILE + 3] = dst_c, after_c

    unmix = np.concatenate([mix[:, 0].T, mix[:, 1].T], axis=1)
    own_r = np.zeros((row_count, 3 * TILE, 2 * row_count))
    own_r[:, 2] = unmix
    own_r[:, TILE + 3] = -unmix
    own_r[:, 2 * TILE, :row_count], own_r[:, 2 * TILE + 1, :row_count] = dst, after
    return dict(
        row_table=row["table"],
        col_table=col["table"],
        row_lam=row["lam"][:, None],
        col_lam=col["lam"][None, :],
        col_lam_down=col["lam"][:, None],
        row_edges=rows_of(TILE, rows, {0: top, 1: bottom}),
        col_edges=rows_of(TILE, cols, {0: left, 1: right}),
        row_squares=rows_of(TILE, rows, {0: row["squares"][0], 1: row["squares"][1]}),
        col_squares=rows_of(TILE, cols, {0: col["squares"][0], 1: col["squares"][1]}),
        row_gaps=row["gaps"],
        col_gaps=col["gaps"],
        send_low=send_low,
        send_high=send_high,
        send_side=send_side,
        jumps=np.concatenate([after.T, -dst.T], axis=1),
        classes=classes,
        twiddle=wave["twiddle"],
        twiddle_all=np.transpose(wave["twiddle"], (1, 0, 2)).reshape(TILE * row_count, rows),
        fine_cos=wave["fine"][:rows],
        fine_sin=wave["fine"][rows:],
        wave_lam=wave["lam"].reshape(row_count, 1, rows),
        wave_energy=wave["energy"].reshape(row_count, 1, rows),
        leaps=np.concatenate([leaps_first, leaps_second, sum_energy], axis=0),
        own_c=own_c,
        pulls=np.concatenate([after.T @ unmix, dst.T @ unmix], axis=0),
        own_r=own_r,
        pair_rows=rows_of(TILE, rows, {0: top, 1: -bottom}),
        pair_cols=rows_of(TILE, cols, {2: left, 3: right}),
    )


def nn(a, b):
    return lax.dot_general(a, b, (((1,), (0,)), ((), ())), precision=HI, preferred_element_type=jnp.float32)


def nt(a, b):
    return lax.dot_general(a, b, (((1,), (1,)), ((), ())), precision=HI, preferred_element_type=jnp.float32)


def tn(a, b):
    return lax.dot_general(a, b, (((0,), (0,)), ((), ())), precision=HI, preferred_element_type=jnp.float32)


def row_number(shape):
    return lax.broadcasted_iota(jnp.int32, shape, 0)


def send_all(out_ref, tile):
    for peer in range(out_ref.shape[0]):
        out_ref[peer] = tile


def edges_kernel(g, field, col_table, row_table, row_lam, col_lam, low, high, side, block_out, weight_out, send_out):
    rows = field.shape[0]
    block = nn(row_table[...], nt(field[...], col_table[...]))
    weight = 1.0 / (row_lam[...] + col_lam[...] + g[0])
    solved = weight * block
    block_out[...] = block
    weight_out[...] = weight
    energy = jnp.sum(solved * block)
    tile = nn(low[...], solved[:, :rows]) + nn(high[...], solved[:, rows:]) + nt(side[...], solved)
    tile = jnp.where(row_number(tile.shape) == 6, energy, tile)
    send_all(send_out, jnp.concatenate([tile[:, : rows // 2], tile[:, rows // 2 :]], axis=0))


def systems_kernel(g, me, weight, row_squares, row_gaps, col_lam, col_squares, col_gaps, wave_lam, wave_energy, row_out, col_out):
    sums = nn(row_squares[...], weight[...])
    row_out[...] = 1.0 / (1.0 + row_gaps[:, 0:1] * sums[0:1] + row_gaps[:, 1:2] * sums[1:2])
    long_weight = 1.0 / (col_lam[...] + wave_lam[me[0]] + g[0])
    sums = nn(col_squares[...], long_weight)
    col_out[...] = wave_energy[me[0]] / (1.0 + col_gaps[:, 0:1] * sums[0:1] + col_gaps[:, 1:2] * sums[1:2])


def classes_kernel(me, seen, weight, row_inverse, jump_table, classes, row_edges, col_edges, row_table, twiddle, fine_cos, fine_sin, jumps_out, send_out):
    count, rows = jump_table.shape[0], weight.shape[0]

    def strided(at):
        parts = [seen[pl.ds(at + side, count, stride=2 * TILE), :] for side in (0, TILE)]
        return jnp.concatenate(parts, axis=1)

    ends_low = jnp.concatenate([strided(2), strided(0)], axis=0)
    ends_high = jnp.concatenate([strided(3), strided(1)], axis=0)
    sides = jnp.concatenate([strided(4), strided(5)], axis=0)
    energy = jnp.sum(strided(6)[:, 0:1])
    jumps = [nn(jump_table[...], ends_low), nn(jump_table[...], ends_high)]
    total = jnp.zeros((), jnp.float32)
    moved = jnp.zeros((2 * count, rows), jnp.float32)
    for half in range(2):
        span = slice(half * rows, (half + 1) * rows)
        jumps_out[:, span] = jumps[half]
        bends = row_inverse[:, span] * jumps[half]
        total = total + jnp.sum(bends * jumps[half])
        both = jnp.concatenate([bends * col_edges[0:1, span], bends * col_edges[1:2, span]], axis=0)
        moved = moved + nt(both, weight[:, span])
    table = classes[me[0]]
    mixed = nn(table[: 2 * TILE], sides)
    bent = nn(table[2 * TILE :], moved)
    mixed = mixed + bent[: 2 * TILE] * row_edges[0:1] - bent[2 * TILE :] * row_edges[1:2]
    placed = nn(mixed, row_table[...])
    real, imag = placed[:TILE], placed[TILE:]
    tw = twiddle[me[0]]
    opening = row_number((TILE, rows)) < 2
    even = real * jnp.where(opening, tw[0:1], tw[4:5]) + imag * jnp.where(opening, tw[1:2], tw[5:6])
    odd = real * jnp.where(opening, tw[2:3], tw[6:7]) + imag * jnp.where(opening, tw[3:4], tw[7:8])
    tile = nn(even, fine_cos[...]) + nn(odd, fine_sin[...])
    send_all(send_out, jnp.where(row_number(tile.shape) == 4, energy - total, tile))


def folds_kernel(me, seen, col_inverse, leaps, own, send_out):
    count, half = col_inverse.shape[0], seen.shape[1]
    out = nn(leaps[...], seen[...])
    first, second = out[:count], out[count : 2 * count]
    fold_first = col_inverse[:, :half] * first
    fold_second = col_inverse[:, half:] * second
    energy = out[2 * count : 2 * count + 1, 0:1] / send_out.shape[0]
    energy = energy - jnp.sum(fold_first * first + fold_second * second)
    table = own[me[0]]
    tile = nn(table[:TILE], fold_first) + nn(table[TILE:], fold_second)
    send_all(send_out, jnp.where(row_number(tile.shape) == 4, energy, tile))


def finish_kernel(previous, me, seen, block, weight, direction, jumps, row_inverse, twiddle, fine_cos, fine_sin, pulls, own, row_edges, col_edges, pair_rows, pair_cols, row_table, col_table, out, ratio_out):
    count = jumps.shape[0]

    def strided(at):
        return seen[pl.ds(at, count, stride=TILE), :]

    waves = jnp.concatenate([strided(0), strided(1), strided(2), strided(3)], axis=0)
    ratio = jnp.sum(strided(4)[:, 0:1]) / previous[0]
    ratio_out[0] = ratio
    even = nt(waves, fine_cos[...])
    odd = nt(waves, fine_sin[...])

    def tw(at):
        return twiddle[at * count : (at + 1) * count]

    spectra = []
    for at in range(2):
        one, two = slice(at * count, (at + 1) * count), slice((at + 2) * count, (at + 3) * count)
        real = even[one] * tw(0) + odd[one] * tw(2) + even[two] * tw(4) + odd[two] * tw(6)
        imag = even[one] * tw(1) + odd[one] * tw(3) + even[two] * tw(5) + odd[two] * tw(7)
        spectra.append(jnp.concatenate([real, imag], axis=0))
    table = own[me[0]]
    mine = nn(table[:TILE], spectra[0]) + nn(table[TILE : 2 * TILE], spectra[1])
    pulled = jnp.concatenate([nn(pulls[...], spectra[0]), nn(pulls[...], spectra[1]), mine], axis=0)
    hats = nt(pulled, row_table[...])
    edge_top, edge_bottom = row_edges[0:1], row_edges[1:2]
    both = jnp.concatenate(
        [
            hats[:count] * edge_bottom - hats[count : 2 * count] * edge_top,
            hats[2 * count : 3 * count] * edge_bottom - hats[3 * count : 4 * count] * edge_top,
        ],
        axis=0,
    )
    mine = hats[4 * count :]
    shifts = nn(both, weight[...])
    jump = jumps[...] + col_edges[0:1] * shifts[:count] - col_edges[1:2] * shifts[count:]
    ends = nn(table[2 * TILE :, :count], row_inverse[...] * jump)
    spectrum = weight[...] * (block[...] + tn(pair_rows[...] + mine, pair_cols[...] + ends))
    out[...] = tn(row_table[...], nn(spectrum, col_table[...])) + ratio * direction[...]


def f32(table):
    return jnp.asarray(np.asarray(table, np.float32))


def call(kernel, name, outs, scalars, arrays, flops, room=16 * 2**20):
    vmem = pl.BlockSpec(memory_space=pltpu.VMEM)
    smem = pl.BlockSpec(memory_space=pltpu.SMEM)
    spaces = [pltpu.SMEM if shape == (1,) else pltpu.VMEM for shape in outs]
    shapes = [space(shape, jnp.float32) for space, shape in zip(spaces, outs)]
    specs = [smem if shape == (1,) else vmem for shape in outs]
    moved = sum(4 * int(np.prod(shape)) for shape in outs) + sum(4 * a.size for a in arrays)
    return pl.pallas_call(
        kernel,
        out_shape=shapes,
        in_specs=[smem] * len(scalars) + [vmem] * len(arrays),
        out_specs=specs,
        name=name,
        compiler_params=pltpu.CompilerParams(vmem_limit_bytes=room),
        cost_estimate=pl.CostEstimate(flops=flops, bytes_accessed=moved, transcendentals=0),
    )(*scalars, *[pltpu.with_memory_space_constraint(a, pltpu.VMEM) for a in arrays])


def exchange(copies, axis):
    seen = lax.all_to_all(copies, axis, 0, 0, tiled=True)
    return seen.reshape(seen.shape[0] * seen.shape[1], seen.shape[2])


def body(of, row_count, col_count, field, direction, ground, previous):
    rows, cols = field.shape
    half = rows // 2
    me_row = lax.axis_index(ROW).reshape(1)
    me_col = lax.axis_index(COL).reshape(1)
    k = {name: f32(table) for name, table in of.items()}

    block, weight, send = call(
        edges_kernel,
        "edges",
        [(rows, cols), (rows, cols), (row_count, 2 * TILE, half)],
        [ground],
        [field, k["col_table"], k["row_table"], k["row_lam"], k["col_lam"], k["send_low"], k["send_high"], k["send_side"]],
        2 * rows * cols * (rows + cols),
    )
    seen = exchange(send, ROW)
    row_inverse, col_inverse = call(
        systems_kernel,
        "systems",
        [(row_count, cols), (col_count, rows)],
        [ground, me_row],
        [weight, k["row_squares"], k["row_gaps"], k["col_lam_down"], k["col_squares"], k["col_gaps"], k["wave_lam"], k["wave_energy"]],
        2 * rows * cols * 32,
    )
    jumps, send = call(
        classes_kernel,
        "classes",
        [(row_count, cols), (col_count, TILE, half)],
        [me_row],
        [seen, weight, row_inverse, k["jumps"], k["classes"], k["row_edges"], k["col_edges"], k["row_table"], k["twiddle"], k["fine_cos"], k["fine_sin"]],
        2 * rows * cols * 128,
    )
    seen = exchange(send, COL)
    (send,) = call(
        folds_kernel,
        "folds",
        [(row_count, TILE, half)],
        [me_col],
        [seen, col_inverse, k["leaps"], k["own_c"]],
        2 * rows * cols * 16,
    )
    seen = exchange(send, ROW)
    out, ratio = call(
        finish_kernel,
        "finish",
        [(rows, cols), (1,)],
        [previous, me_row],
        [seen, block, weight, direction, jumps, row_inverse, k["twiddle_all"], k["fine_cos"], k["fine_sin"], k["pulls"], k["own_r"], k["row_edges"], k["col_edges"], k["pair_rows"], k["pair_cols"], k["row_table"], k["col_table"]],
        2 * rows * cols * (rows + cols + 128),
    )
    return out, ratio


def solution(mesh):
    row_count, col_count = mesh.shape[ROW], mesh.shape[COL]

    def step(residual, direction, ground_shift, previous):
        rows, cols = residual.shape[0] // row_count, residual.shape[1] // col_count
        of = kernel_constants(rows, cols, row_count, col_count)

        def local(field, heading, ground, last):
            return body(of, row_count, col_count, field, heading, ground, last)

        return jax.shard_map(
            local,
            mesh=mesh,
            in_specs=(P(ROW, COL), P(ROW, COL), P(), P()),
            out_specs=(P(ROW, COL), P()),
            check_vma=False,
        )(residual, direction, ground_shift, previous)

    return step
```

time: 154 us -> 88.5 us (0.57)
  blocking collectives: 117 us -> 0 us
  starting transfers between devices: 0 us -> 28.8 us
  waiting for transfers between devices: 0 us -> 27.2 us
  matrix products: 16.7 us -> 0 us
  Pallas kernels: 0 us -> 11.3 us
  local copies, waits for them, and re-layouts: 11.1 us -> 17.4 us
  between operations: 6.07 us -> 2.8 us
  other arithmetic: 2 us -> 0 us
    all_gather x3 -> x0, blocking collectives: 117 us -> none  [gather(): return lax.all_gather(payload, axis)]
    all_to_all x0 -> x3, starting transfers between devices: none -> 28.8 us  [exchange(): seen = lax.all_to_all(copies, axis, 0, 0, tiled=True)]
    all_to_all x0 -> x3, waiting for transfers between devices: none -> 27.2 us  [exchange(): seen = lax.all_to_all(copies, axis, 0, 0, tiled=True)]
    dot_general x29 -> x0, matrix products: 16.7 us -> none  [mm(): return lax.dot_general(a, b, (dims, ((), ())), precision=HI)]
    pallas_call x0 -> x5, Pallas kernels: none -> 11.3 us  [call(): pl.pallas_call(kernel, out_shape=shapes, in_specs=[smem] * len(scalars) +...]
    unnamed x59 -> x85, local copies, waits for them, and re-layouts: 7.05 us -> 17.4 us
    reduce_sum x3 -> x0, other arithmetic: 1.94 us -> none  [the longest x1 0.67 us: body(): energy = jnp.sum(seen[:, 2 * cols + 2 * rows])]
  transfers between devices with their start and end apart: 0 -> 3, of which waited for: 0 -> 3; matrix products, arithmetic and copies ran while one was open for 0% -> 0% of each run, Pallas kernels for 0% -> 1%
where the time goes in v3:
time: 88.5 us; the launch traced here: 87.5 us
  starting transfers between devices  28.8 us (33%)
  waiting for transfers between devices  27.2 us (31%)
  local copies, waits for them, and re-layouts  17.4 us (20%)
  Pallas kernels  11.3 us (13%)
  between operations  2.8 us (3%)
    all_to_all x3, starting transfers between devices, exchange(): seen = lax.all_to_all(copies, axis, 0, 0, tiled=True)  28.8 us
    all_to_all x3, waiting for transfers between devices, exchange(): seen = lax.all_to_all(copies, axis, 0, 0, tiled=True)  27.2 us
    unnamed x85, local copies, waits for them, and re-layouts  17.4 us
    pallas_call x5, Pallas kernels, call(): pl.pallas_call(kernel, out_shape=shapes, in_specs=[smem] * len(scalars) +...  11.3 us
  transfers between devices with their start and end apart: 3, of which 3 were waited for; matrix products, arithmetic and copies ran while one was open for 0% of the time, Pallas kernels for 1%

profile of v3, /device:TPU:1, one launch (start us, length us, event | category | flops | bytes accessed | tf_op | source)
XLA Modules:
  0.0 87.5 jit_solution(10346474465572243617)
XLA Ops:
  0.6 0.0 copy-start.41
  0.6 0.0 copy-start.35
  0.7 0.0 copy-start.40
  0.7 0.0 copy-start.39
  1.3 0.0 copy-done.41
  1.4 0.0 copy-done.35
  1.4 0.0 copy-done.40
  1.4 0.0 copy-done.39
  1.4 0.0 copy-start
  1.4 1.2 %copy-done = f32[512,512]{1,0:T(8,128)S(1)} copy-done((f32[512,512]{1,0:T(8,128)S(1)}, f32[512,512]{1,0:T(8,128)}, u32[]{:S(2)}) %copy-start) | copy-done | bytes 1048600
  2.6 0.9 %copy-done.2 = f32[256,256]{1,0:T(8,128)S(1)} copy-done((f32[256,256]{1,0:T(8,128)S(1)}, f32[256,256]{1,0:T(8,128)}, u32[]{:S(2)}) %copy-start.2) | copy-done | bytes 262168
  3.6 1.0 %copy-done.6 = f32[256,512]{1,0:T(8,128)S(1)} copy-done((f32[256,512]{1,0:T(8,128)S(1)}, f32[256,512]{1,0:T(8,128)}, u32[]{:S(2)}) %copy-start.6) | copy-done | bytes 524312
  4.6 0.9 %copy-done.18 = f32[256,1]{1,0:T(8,128)S(1)} copy-done((f32[256,1]{1,0:T(8,128)S(1)}, f32[256,1]{1,0:T(8,128)}, u32[]{:S(2)}) %copy-start.18) | copy-done | bytes 1048
  5.5 0.0 copy-start.32
  5.5 0.0 copy-start.37
  5.6 0.0 copy-start.38
  5.6 4.1 %edges.1 = (f32[256,512]{1,0:T(8,128)S(1)}, f32[256,512]{1,0:T(8,128)S(1)}, f32[32,16,128]{2,1,0:T(8,128)}) custom-call(f32[1]{0:T(128)S(6)} %copy.36.g, f32[256,512]{1,0:T(8,128)S(1)} %copy-done.6, f32[512,512]{1,0:T(8,128)S(1)} %copy-done, f32[256,256]{1,0:T(8,128)S(1)} %copy-done.2, f32[256,1]{1,0:T(8,128)S(1)} %copy-done.18, f32[1,512]{1,0:T(1,128)S(1)} %copy-done.41, ...), custom_call_target="tpu_custom_call" | custom-call | flops 201326592 | bytes 3181568 | tf_op jit(solution)/shard_map/edges/pallas_call | solution.py:314
  9.6 10.7 %all-to-all-start = ((f32[32,16,128]{2,1,0:T(8,128)}), f32[32,16,128]{2,1,0:T(8,128)S(1)}, u32[]{:S(2)}, u32[]{:S(2)}) async-start(f32[32,16,128]{2,1,0:T(8,128)} %get-tuple-element.9), calls=%async_computation | async-start | bytes 524288 | tf_op jit(solution)/shard_map/all_to_all | solution.py:326
  20.3 0.0 copy-done.15
  20.3 0.0 copy-done.26
  20.3 0.0 copy-done.27
  20.4 0.0 copy-done.31
  20.4 0.0 copy-done.32
  20.4 0.0 copy-done.37
  20.4 0.0 copy-done.38
  20.4 0.0 copy-start.3
  20.4 0.0 copy-start.7
  20.4 0.0 copy-start.21
  20.4 0.7 systems.1
  21.1 0.0 copy-start.11
  21.1 0.6 copy-done.11
  21.7 0.6 copy-done.33
  22.3 9.4 %all-to-all-done = f32[32,16,128]{2,1,0:T(8,128)S(1)} async-done(((f32[32,16,128]{2,1,0:T(8,128)}), f32[32,16,128]{2,1,0:T(8,128)S(1)}, u32[]{:S(2)}, u32[]{:S(2)}) %all-to-all-start) | async-done | bytes 262176 | tf_op jit(solution)/shard_map/all_to_all | solution.py:326
  31.7 0.0 copy-done.4
  31.7 0.0 copy-done.3
  31.8 0.0 copy-done.7
  31.8 0.0 copy-done.21
  31.8 0.0 copy-start.8
  31.8 0.9 %copy-done.8 = f32[256,128]{1,0:T(8,128)S(1)} copy-done((f32[256,128]{1,0:T(8,128)S(1)}, f32[256,128]{1,0:T(8,128)}, u32[]{:S(2)}) %copy-start.8) | copy-done | bytes 131096
  32.7 0.8 copy-done.12
  33.5 0.9 %copy-done.16 = f32[32,8,256]{2,1,0:T(8,128)S(1)} copy-done((f32[32,8,256]{2,1,0:T(8,128)S(1)}, f32[32,8,256]{2,1,0:T(8,128)}, u32[]{:S(2)}) %copy-start.16) | copy-done | bytes 262168
  34.5 0.7 copy-done.24
  35.2 0.7 copy-done.30
  35.9 1.8 %classes.2 = (f32[32,512]{1,0:T(8,128)S(1)}, f32[16,8,128]{2,1,0:T(8,128)S(1)}) custom-call(s32[1]{0:T(128)} %bitcast.me, f32[512,128]{1,0:T(8,128)S(1)} %bitcast.5, f32[256,512]{1,0:T(8,128)S(1)} %get-tuple-element.10.weight, f32[32,512]{1,0:T(8,128)S(1)} %copy-done.12, f32[32,64]{1,0:T(8,128)S(1)} %copy-done.30, f32[32,48,64]{2,1,0:T(8,128)S(1)} %copy-done.4, ...), custom_call_target="tpu_custom_call" | custom-call | flops 33554432 | bytes 2195456 | tf_op jit(solution)/shard_map/classes/pallas_call | solution.py:314
  37.7 0.6 copy-done.19
  38.3 0.6 copy-done.22
  38.9 11.8 %all-to-all-start.1 = ((f32[16,8,128]{2,1,0:T(8,128)}), f32[16,8,128]{2,1,0:T(8,128)S(1)}, u32[]{:S(2)}, u32[]{:S(2)}) async-start(f32[16,8,128]{2,1,0:T(8,128)} %copy-done.22), calls=%async_computation.1 | async-start | bytes 131072 | tf_op jit(solution)/shard_map/all_to_all | solution.py:326
  50.8 9.0 %all-to-all-done.1 = f32[16,8,128]{2,1,0:T(8,128)S(1)} async-done(((f32[16,8,128]{2,1,0:T(8,128)}), f32[16,8,128]{2,1,0:T(8,128)S(1)}, u32[]{:S(2)}, u32[]{:S(2)}) %all-to-all-start.1) | async-done | bytes 65568 | tf_op jit(solution)/shard_map/all_to_all | solution.py:326
  59.7 0.9 %copy-done.17 = f32[16,16,16]{2,1,0:T(8,128)S(1)} copy-done((f32[16,16,16]{2,1,0:T(8,128)S(1)}, f32[16,16,16]{2,1,0:T(8,128)}, u32[]{:S(2)}) %copy-start.17) | copy-done | bytes 16408
  60.7 0.7 copy-done.28
  61.4 0.7 copy-done.34
  62.1 1.0 %folds.1 = f32[32,8,128]{2,1,0:T(8,128)} custom-call(s32[1]{0:T(128)} %bitcast.1.me, f32[128,128]{1,0:T(8,128)S(1)} %bitcast.7, f32[16,256]{1,0:T(8,128)S(1)} %copy-done.34, f32[40,128]{1,0:T(8,128)S(1)} %copy-done.28, f32[16,16,16]{2,1,0:T(8,128)S(1)} %copy-done.17), custom_call_target="tpu_custom_call" | custom-call | flops 4194304 | bytes 249856 | tf_op jit(solution)/shard_map/folds/pallas_call | solution.py:314
  63.1 0.0 copy-start.36
  63.2 6.3 %all-to-all-start.2 = ((f32[32,8,128]{2,1,0:T(8,128)}), f32[32,8,128]{2,1,0:T(8,128)S(1)}, u32[]{:S(2)}, u32[]{:S(2)}) async-start(f32[32,8,128]{2,1,0:T(8,128)} %folds.1), calls=%async_computation.2 | async-start | bytes 262144 | tf_op jit(solution)/shard_map/all_to_all | solution.py:326
  70.1 8.8 %all-to-all-done.2 = f32[32,8,128]{2,1,0:T(8,128)S(1)} async-done(((f32[32,8,128]{2,1,0:T(8,128)}), f32[32,8,128]{2,1,0:T(8,128)S(1)}, u32[]{:S(2)}, u32[]{:S(2)}) %all-to-all-start.2) | async-done | bytes 131104 | tf_op jit(solution)/shard_map/all_to_all | solution.py:326
  78.9 0.0 copy-done.1
  78.9 0.0 copy-done.9
  78.9 0.0 copy-start.10
  78.9 1.0 %copy-done.10 = f32[32,24,64]{2,1,0:T(8,128)S(1)} copy-done((f32[32,24,64]{2,1,0:T(8,128)S(1)}, f32[32,24,64]{2,1,0:T(8,128)}, u32[]{:S(2)}) %copy-start.10) | copy-done | bytes 196632
  79.9 0.9 %copy-done.14 = f32[256,256]{1,0:T(8,128)S(1)} copy-done((f32[256,256]{1,0:T(8,128)S(1)}, f32[256,256]{1,0:T(8,128)}, u32[]{:S(2)}) %copy-start.14) | copy-done | bytes 262168
  80.9 0.8 copy-done.20
  81.7 0.7 copy-done.29
  82.4 3.7 %finish.1 = (f32[256,512]{1,0:T(8,128)S(1)}, f32[1]{0:T(128)S(4)}) custom-call(f32[1]{0:T(128)S(6)} %copy.37.previous, s32[1]{0:T(128)} %bitcast.me, f32[256,128]{1,0:T(8,128)S(1)} %bitcast.6, f32[256,512]{1,0:T(8,128)S(1)} %get-tuple-element.14.block, f32[256,512]{1,0:T(8,128)S(1)} %get-tuple-element.10.weight, f32[256,512]{1,0:T(8,128)S(1)} %copy-done.5, ...), custom_call_target="tpu_custom_call" | custom-call | flops 234881024 | bytes 4456452 | tf_op jit(solution)/shard_map/finish/pallas_call | solution.py:314
  86.7 0.8 copy.34
  (32 shorter events, 0.1 us)
Async XLA Ops:
  0.6 0.7 copy-start.41
  0.6 0.7 copy-start.35
  0.7 0.7 copy-start.40
  0.7 0.7 copy-start.39
  1.4 1.2 %copy-start = (f32[512,512]{1,0:T(8,128)S(1)}, f32[512,512]{1,0:T(8,128)}, u32[]{:S(2)}) copy-start(f32[512,512]{1,0:T(8,128)} %constant.66.clone.col_table) | copy-start | bytes 3145732
  2.6 0.9 %copy-start.2 = (f32[256,256]{1,0:T(8,128)S(1)}, f32[256,256]{1,0:T(8,128)}, u32[]{:S(2)}) copy-start(f32[256,256]{1,0:T(8,128)} %constant.65.clone.row_table) | copy-start | bytes 786436
  3.6 1.0 %copy-start.6 = (f32[256,512]{1,0:T(8,128)S(1)}, f32[256,512]{1,0:T(8,128)}, u32[]{:S(2)}) copy-start(f32[256,512]{1,0:T(8,128)} %field.1) | copy-start | bytes 1572868
  4.6 0.9 %copy-start.18 = (f32[256,1]{1,0:T(8,128)S(1)}, f32[256,1]{1,0:T(8,128)}, u32[]{:S(2)}) copy-start(f32[256,1]{1,0:T(8,128)} %constant.67.clone.row_lam) | copy-start | bytes 3076
  5.5 14.8 %copy-start.15 = (f32[512,1]{1,0:T(8,128)S(1)}, f32[512,1]{1,0:T(8,128)}, u32[]{:S(2)}) copy-start(f32[512,1]{1,0:T(8,128)} %constant.69.clone.col_lam) | copy-start | bytes 6148
  5.5 14.8 %copy-start.26 = (f32[32,1,256]{2,1,0:T(1,128)S(1)}, f32[32,1,256]{2,1,0:T(1,128)}, u32[]{:S(2)}) copy-start(f32[32,1,256]{2,1,0:T(1,128)} %constant.86.clone.wave_energy) | copy-start | bytes 98308
  5.5 14.8 %copy-start.27 = (f32[32,1,256]{2,1,0:T(1,128)S(1)}, f32[32,1,256]{2,1,0:T(1,128)}, u32[]{:S(2)}) copy-start(f32[32,1,256]{2,1,0:T(1,128)} %constant.85.clone.wave_lam) | copy-start | bytes 98308
  5.5 14.8 %copy-start.31 = (f32[32,2]{1,0:T(8,128)S(1)}, f32[32,2]{1,0:T(8,128)}, u32[]{:S(2)}) copy-start(f32[32,2]{1,0:T(8,128)} %constant.74.clone.row_gaps) | copy-start | bytes 772
  5.5 14.8 %copy-start.32 = (f32[8,512]{1,0:T(8,128)S(1)}, f32[8,512]{1,0:T(8,128)}, u32[]{:S(2)}) copy-start(f32[8,512]{1,0:T(8,128)} %constant.73.clone.col_squares) | copy-start | bytes 49156
  5.5 14.8 %copy-start.37 = (f32[16,2]{1,0:T(8,128)S(1)}, f32[16,2]{1,0:T(8,128)}, u32[]{:S(2)}) copy-start(f32[16,2]{1,0:T(8,128)} %constant.75.clone.col_gaps) | copy-start | bytes 388
  5.6 14.8 %copy-start.38 = (f32[8,256]{1,0:T(8,128)S(1)}, f32[8,256]{1,0:T(8,128)}, u32[]{:S(2)}) copy-start(f32[8,256]{1,0:T(8,128)} %constant.72.clone.row_squares) | copy-start | bytes 24580
  9.6 22.1 %copy-start.4 = (f32[32,48,64]{2,1,0:T(8,128)S(1)}, f32[32,48,64]{2,1,0:T(8,128)}, u32[]{:S(2)}) copy-start(f32[32,48,64]{2,1,0:T(8,128)} %constant.80.clone.classes) | copy-start | bytes 1179652
  9.6 22.1 %all-to-all-start = ((f32[32,16,128]{2,1,0:T(8,128)}), f32[32,16,128]{2,1,0:T(8,128)S(1)}, u32[]{:S(2)}, u32[]{:S(2)}) async-start(f32[32,16,128]{2,1,0:T(8,128)} %get-tuple-element.9), calls=%async_computation | async-start | bytes 524288 | tf_op jit(solution)/shard_map/all_to_all | solution.py:326
  20.4 11.4 %copy-start.3 = (f32[256,256]{1,0:T(8,128)S(1)}, f32[256,256]{1,0:T(8,128)}, u32[]{:S(2)}) copy-start(f32[256,256]{1,0:T(8,128)} %constant.65.clone.row_table) | copy-start | bytes 786436
  20.4 11.3 %copy-start.7 = (f32[256,128]{1,0:T(8,128)S(1)}, f32[256,128]{1,0:T(8,128)}, u32[]{:S(2)}) copy-start(f32[256,128]{1,0:T(8,128)} %constant.84.clone.fine_sin) | copy-start | bytes 393220
  20.4 11.3 %copy-start.21 = (f32[8,512]{1,0:T(8,128)S(1)}, f32[8,512]{1,0:T(8,128)}, u32[]{:S(2)}) copy-start(f32[8,512]{1,0:T(8,128)} %constant.71.clone.col_edges) | copy-start | bytes 49156
  21.1 0.6 copy-start.11
  21.7 0.6 copy-start.33
  31.8 0.9 %copy-start.8 = (f32[256,128]{1,0:T(8,128)S(1)}, f32[256,128]{1,0:T(8,128)}, u32[]{:S(2)}) copy-start(f32[256,128]{1,0:T(8,128)} %constant.83.clone.fine_cos) | copy-start | bytes 393220
  32.7 0.8 copy-start.12
  33.5 0.9 %copy-start.16 = (f32[32,8,256]{2,1,0:T(8,128)S(1)}, f32[32,8,256]{2,1,0:T(8,128)}, u32[]{:S(2)}) copy-start(f32[32,8,256]{2,1,0:T(8,128)} %constant.81.clone.twiddle) | copy-start | bytes 786436
  34.5 0.7 copy-start.24
  35.2 0.7 copy-start.30
  35.9 43.0 %copy-start.1 = (f32[512,512]{1,0:T(8,128)S(1)}, f32[512,512]{1,0:T(8,128)}, u32[]{:S(2)}) copy-start(f32[512,512]{1,0:T(8,128)} %constant.66.clone.col_table) | copy-start | bytes 3145732
  37.7 0.6 copy-start.19
  38.3 0.6 copy-start.22
  38.9 39.9 %copy-start.5 = (f32[256,512]{1,0:T(8,128)S(1)}, f32[256,512]{1,0:T(8,128)}, u32[]{:S(2)}) copy-start(f32[256,512]{1,0:T(8,128)} %direction.1) | copy-start | bytes 1572868
  38.9 20.8 %all-to-all-start.1 = ((f32[16,8,128]{2,1,0:T(8,128)}), f32[16,8,128]{2,1,0:T(8,128)S(1)}, u32[]{:S(2)}, u32[]{:S(2)}) async-start(f32[16,8,128]{2,1,0:T(8,128)} %copy-done.22), calls=%async_computation.1 | async-start | bytes 131072 | tf_op jit(solution)/shard_map/all_to_all | solution.py:326
  59.7 0.9 %copy-start.17 = (f32[16,16,16]{2,1,0:T(8,128)S(1)}, f32[16,16,16]{2,1,0:T(8,128)}, u32[]{:S(2)}) copy-start(f32[16,16,16]{2,1,0:T(8,128)} %constant.88.clone.own) | copy-start | bytes 49156
  60.7 0.7 copy-start.28
  61.4 0.7 copy-start.34
  63.1 15.7 %copy-start.9 = (f32[256,128]{1,0:T(8,128)S(1)}, f32[256,128]{1,0:T(8,128)}, u32[]{:S(2)}) copy-start(f32[256,128]{1,0:T(8,128)} %constant.83.clone.fine_cos) | copy-start | bytes 393220
  63.1 15.7 %copy-start.13 = (f32[32,512]{1,0:T(8,128)S(1)}, f32[32,512]{1,0:T(8,128)}, u32[]{:S(2)}) copy-start(f32[32,512]{1,0:T(8,128)} %copy-done.11) | copy-start | bytes 196612
  63.1 15.8 %copy-start.23 = (f32[64,64]{1,0:T(8,128)S(1)}, f32[64,64]{1,0:T(8,128)}, u32[]{:S(2)}) copy-start(f32[64,64]{1,0:T(8,128)} %constant.89.clone.pulls) | copy-start | bytes 49156
  63.1 15.8 %copy-start.25 = (f32[8,256]{1,0:T(8,128)S(1)}, f32[8,256]{1,0:T(8,128)}, u32[]{:S(2)}) copy-start(f32[8,256]{1,0:T(8,128)} %constant.70.clone.row_edges) | copy-start | bytes 24580
  63.1 15.8 %copy-start.36 = (f32[8,256]{1,0:T(8,128)S(1)}, f32[8,256]{1,0:T(8,128)}, u32[]{:S(2)}) copy-start(f32[8,256]{1,0:T(8,128)} %constant.91.clone.pair_rows) | copy-start | bytes 24580
  63.2 15.7 %all-to-all-start.2 = ((f32[32,8,128]{2,1,0:T(8,128)}), f32[32,8,128]{2,1,0:T(8,128)S(1)}, u32[]{:S(2)}, u32[]{:S(2)}) async-start(f32[32,8,128]{2,1,0:T(8,128)} %folds.1), calls=%async_computation.2 | async-start | bytes 262144 | tf_op jit(solution)/shard_map/all_to_all | solution.py:326
  78.9 1.0 %copy-start.10 = (f32[32,24,64]{2,1,0:T(8,128)S(1)}, f32[32,24,64]{2,1,0:T(8,128)}, u32[]{:S(2)}) copy-start(f32[32,24,64]{2,1,0:T(8,128)} %constant.90.clone.own) | copy-start | bytes 589828
  79.9 0.9 %copy-start.14 = (f32[256,256]{1,0:T(8,128)S(1)}, f32[256,256]{1,0:T(8,128)}, u32[]{:S(2)}) copy-start(f32[256,256]{1,0:T(8,128)} %constant.82.clone.twiddle) | copy-start | bytes 786436
  80.9 0.8 copy-start.20
  81.7 0.7 copy-start.29

commit v4 on v3

v4 whole, which is shorter than its diff:
```python
import numpy as np
import jax
import jax.numpy as jnp
from jax import lax
from jax.experimental import pallas as pl
from jax.experimental.pallas import tpu as pltpu
from jax.sharding import PartitionSpec as P

ROW = "row"
COL = "col"
TILE = 8
LANES = 128

HI = lax.Precision.HIGHEST


def cosines(length):
    wave = np.arange(length)[:, None]
    place = np.arange(length)[None, :]
    angle = np.pi * (wave * (2 * place + 1) % (4 * length)) / (2 * length)
    scale = np.where(wave == 0, np.sqrt(1.0 / length), np.sqrt(2.0 / length))
    return scale * np.cos(angle)


def stiffness(waves, length):
    return 4.0 * np.sin(np.pi * waves / (2 * length)) ** 2


def sines(blocks):
    index = np.arange(blocks + 1)
    table = np.sqrt(2.0 / blocks) * np.sin(np.pi * (index[:, None] * index[None, :] % (2 * blocks)) / blocks)
    table[blocks] = 0.0
    return table[:, :blocks]


def block_constants(extent, blocks):
    table = cosines(extent)
    edge = table[:, 0]
    sign = np.where(np.arange(extent) % 2 == 0, 1.0, -1.0)
    dst = sines(blocks)
    theta = np.cos(np.pi * np.arange(blocks) / blocks)
    return dict(
        table=table,
        lam=stiffness(np.arange(extent), extent),
        edges=np.stack([edge, edge * sign]),
        columns=np.stack([edge, edge * sign], axis=1),
        squares=np.stack([edge**2 * (1 + sign), edge**2 * (1 - sign)]),
        dst=dst[:blocks],
        after=dst[1:],
        gaps=np.stack([1 - theta, 1 + theta], axis=1),
    )


def wave_constants(extent, blocks):
    length = extent * blocks
    half = extent // 2
    kind = np.arange(blocks)
    block = np.arange(blocks)
    angle = np.pi * (kind[:, None] * block[None, :] % (2 * blocks)) / blocks
    parity = np.where(block % 2 == 0, 1.0, -1.0)
    mix = np.stack([np.cos(angle), np.where(kind[:, None] > 0, np.sin(angle), parity[None, :])], axis=1)
    first = kind
    second = np.where(kind == 0, blocks, 2 * blocks - kind)
    place = 2 * np.arange(extent) + 1
    phase_one = np.pi * (first[:, None] * place[None, :] % (4 * length)) / (2 * length)
    phase_two = np.pi * (second[:, None] * place[None, :] % (4 * length)) / (2 * length)
    inner = (kind > 0)[:, None] * 1.0
    twiddle = np.stack(
        [
            np.cos(phase_one),
            -inner * np.sin(phase_one),
            -np.sin(phase_one),
            -inner * np.cos(phase_one),
            inner * np.cos(phase_two),
            np.where(kind[:, None] > 0, np.sin(phase_two), np.cos(phase_two)),
            -inner * np.sin(phase_two),
            np.where(kind[:, None] > 0, np.cos(phase_two), -np.sin(phase_two)),
        ],
        axis=1,
    )
    twiddle[0, 2] = 0.0
    steps = np.arange(half)
    fine = np.pi * (steps[None, :] * place[:, None] % (2 * extent)) / extent
    waves = np.stack([first, second], axis=1)[:, :, None] + 2 * blocks * steps[None, None, :]
    energy = np.where(waves == 0, 1.0 / length, 2.0 / length)
    return dict(
        mix=mix,
        twiddle=twiddle,
        fine=np.concatenate([np.cos(fine), np.sin(fine)], axis=0),
        lam=stiffness(waves, length),
        energy=energy,
    )


def kernel_constants(rows, cols, row_count, col_count):
    row = block_constants(rows, row_count)
    col = block_constants(cols, col_count)
    wave = wave_constants(rows, row_count)
    half = rows // 2
    top, bottom = row["edges"]
    left, right = col["edges"]
    mix, dst, after = wave["mix"], row["dst"], row["after"]
    dst_c, after_c = col["dst"], col["after"]
    unmix = np.concatenate([mix[:, 0].T, mix[:, 1].T], axis=1)

    columns = np.zeros((rows, LANES))
    columns[:, 0] = row["lam"]
    for piece in range(cols // rows):
        columns[:, 8 + piece] = col["lam"][piece * rows : (piece + 1) * rows]
    columns[:row_count, 1:3] = row["gaps"]
    columns[:col_count, 3:5] = col["gaps"]

    sends = np.zeros((3 * TILE, cols))
    sends[0, :rows] = sends[1, rows : 2 * rows] = top
    sends[2, :rows] = sends[3, rows : 2 * rows] = bottom
    sends[TILE + 4], sends[TILE + 5] = left, right
    sends[2 * TILE] = col["lam"]

    small = np.zeros((2 * row_count + 5 * TILE, max(3 * LANES, 2 * rows, cols)))
    small[: 2 * row_count, : 2 * row_count] = np.concatenate([after.T @ unmix, dst.T @ unmix], axis=0)
    small[:row_count, LANES : LANES + 2 * row_count] = np.concatenate([after.T, -dst.T], axis=1)
    small[:row_count, 2 * LANES : 2 * LANES + row_count] = dst
    small[row_count : 2 * row_count, 2 * LANES : 2 * LANES + row_count] = after
    base = 2 * row_count
    small[base, :rows], small[base + 1, :rows] = top, bottom
    small[base, rows : 2 * rows], small[base + 1, rows : 2 * rows] = top, -bottom
    small[base + TILE, :cols], small[base + TILE + 1, :cols] = left, right
    small[base + 2 * TILE : base + 2 * TILE + 2, :rows] = row["squares"]
    small[base + 3 * TILE : base + 3 * TILE + 2, :cols] = col["squares"]
    small[base + 4 * TILE + 2, :cols], small[base + 4 * TILE + 3, :cols] = left, right

    leaps = np.zeros((2 * col_count + TILE, TILE * col_count))
    reach = max(LANES, TILE * col_count)
    leaps[:col_count, 1::TILE], leaps[:col_count, 0::TILE] = after_c.T, -dst_c.T
    leaps[col_count : 2 * col_count, 3::TILE], leaps[col_count : 2 * col_count, 2::TILE] = after_c.T, -dst_c.T
    leaps[2 * col_count, 4::TILE] = 1.0
    own_c = np.zeros((TILE * col_count, col_count))
    for at in (0, 2):
        own_c[at::TILE], own_c[at + 1 :: TILE] = dst_c, after_c

    classes = np.zeros((row_count, 2 * TILE, max(rows, 2 * row_count)))
    classes[:, :TILE, :rows] = wave["twiddle"]
    classes[:, 8, :rows] = wave["lam"].reshape(row_count, rows)
    classes[:, 9, :rows] = wave["energy"].reshape(row_count, rows)
    classes[:, 10, :row_count], classes[:, 11, :row_count] = mix[:, 0], mix[:, 1]
    classes[:, 12, : 2 * row_count] = unmix
    classes[:, 13, :row_count], classes[:, 14, :row_count] = dst, after
    slabs = [classes[:, :, :half], classes[:, :, half:rows]]
    return dict(
        row_table=row["table"],
        col_table=col["table"],
        columns=columns,
        sends=sends,
        small=small,
        leaps=np.concatenate(
            [np.pad(table, ((0, 0), (0, reach - table.shape[1]))) for table in (own_c, leaps)], axis=0
        ),
        classes=np.concatenate([slab.reshape(2 * TILE * row_count, half) for slab in slabs], axis=0),
        fine=np.concatenate([wave["fine"][:rows], wave["fine"][rows:]], axis=1),
    )


def nn(a, b):
    return lax.dot_general(a, b, (((1,), (0,)), ((), ())), precision=HI, preferred_element_type=jnp.float32)


def nt(a, b):
    return lax.dot_general(a, b, (((1,), (1,)), ((), ())), precision=HI, preferred_element_type=jnp.float32)


def tn(a, b):
    return lax.dot_general(a, b, (((0,), (0,)), ((), ())), precision=HI, preferred_element_type=jnp.float32)


def row_number(shape):
    return lax.broadcasted_iota(jnp.int32, shape, 0)


def send_all(out_ref, copies_ref, sent, tile):
    for peer in range(out_ref.shape[0]):
        copies_ref[peer] = tile
    copy = pltpu.make_async_copy(copies_ref, out_ref, sent)
    copy.start()
    copy.wait()


def aligned(index, size):
    return pl.ds(pl.multiple_of(index * size, size), size)


def class_rows(classes, me, first):
    start = pl.multiple_of(me * 2 * TILE, TILE) + first
    slab = classes.shape[0] // 2
    return jnp.concatenate([classes[pl.ds(start, TILE), :], classes[pl.ds(slab + start, TILE), :]], axis=1)


def edges_kernel(g, field, col_table, row_table, columns, sends, block_out, weight_out, send_out, field_in, col_in, row_in, columns_in, sends_in, arrived, block_here, copies_here, left_core):
    rows = field.shape[0]
    pairs = [(row_table, row_in), (field, field_in), (columns, columns_in), (sends, sends_in), (col_table, col_in)]
    copies = [pltpu.make_async_copy(src, dst, arrived.at[at]) for at, (src, dst) in enumerate(pairs)]
    for copy in copies:
        copy.start()
    copies[0].wait()
    copies[1].wait()
    halfway = nn(row_in[...], field_in[...])
    copies[2].wait()
    copies[3].wait()
    weight = 1.0 / (columns_in[:, 0:1] + sends_in[2 * TILE : 2 * TILE + 1] + g[0])
    weight_out[...] = weight
    copies[4].wait()
    block = nt(halfway, col_in[...])
    solved = weight * block
    block_here[...] = block
    keep = pltpu.make_async_copy(block_here, block_out, left_core.at[0])
    keep.start()
    energy = jnp.sum(solved * block)
    low, side = sends_in[:TILE], sends_in[TILE : 2 * TILE]
    tile = nn(low[:, :rows], solved[:, :rows]) + nn(low[:, rows:], solved[:, rows:]) + nt(side, solved)
    tile = jnp.where(row_number(tile.shape) == 6, energy, tile)
    tile = jnp.concatenate([tile[:, : rows // 2], tile[:, rows // 2 :]], axis=0)
    send_all(send_out, copies_here, left_core.at[1], tile)
    keep.wait()


def make_kernels(row_count, col_count, rows, cols):
    base = 2 * row_count
    half = rows // 2

    def systems_kernel(g, me, weight, columns, small, classes, out):
        sums = nn(small[base + 2 * TILE : base + 3 * TILE, :rows], weight[...])
        gaps = columns[:row_count, 1:3]
        out[:row_count] = 1.0 / (1.0 + gaps[:, 0:1] * sums[0:1] + gaps[:, 1:2] * sums[1:2])
        mine = class_rows(classes, me[0], TILE)
        down = jnp.concatenate([columns[:, 8 + piece : 9 + piece] for piece in range(cols // rows)], axis=0)
        long_weight = 1.0 / (down + mine[0:1] + g[0])
        sums = nn(small[base + 3 * TILE : base + 4 * TILE, :cols], long_weight)
        gaps = columns[:col_count, 3:5]
        out[row_count : row_count + col_count, :rows] = mine[1:2] / (1.0 + gaps[:, 0:1] * sums[0:1] + gaps[:, 1:2] * sums[1:2])
        sines_here = small[:base, 2 * LANES : 2 * LANES + row_count]
        out[row_count : row_count + TILE, rows : rows + row_count] = nn(mine[:, :row_count], sines_here[:row_count])
        out[row_count + TILE : row_count + 2 * TILE, rows : rows + row_count] = nn(mine[:, :row_count], sines_here[row_count:])

    def classes_kernel(me, seen, weight, systems, row_table, fine, small, classes, jumps_out, send_out, jumps_here, copies_here, left_core):
        def strided(at):
            parts = [seen[pl.ds(at + side, row_count, stride=2 * TILE), :] for side in (0, TILE)]
            return jnp.concatenate(parts, axis=1)

        lows = jnp.concatenate([strided(2), strided(0)], axis=0)
        highs = jnp.concatenate([strided(3), strided(1)], axis=0)
        jump_table = small[:row_count, LANES : LANES + 2 * row_count]
        jumps = nn(jump_table, jnp.concatenate([lows, highs], axis=1))
        jumps_here[...] = jumps
        keep = pltpu.make_async_copy(jumps_here, jumps_out, left_core.at[0])
        keep.start()
        bends = systems[:row_count] * jumps
        energy = jnp.sum(strided(6)[:, 0:1]) - jnp.sum(bends * jumps)
        lefts, rights = small[base + TILE : base + TILE + 1, :cols], small[base + TILE + 1 : base + TILE + 2, :cols]
        moved = nt(jnp.concatenate([bends * lefts, bends * rights], axis=0), weight[...])
        moved = jnp.concatenate([moved[:row_count], moved[row_count:]], axis=1)
        mine = class_rows(classes, me[0], TILE)[:, :row_count]
        mixed = nn(mine, jnp.concatenate([strided(4), strided(5)], axis=1))
        top, bottom = small[base : base + 1, :rows], small[base + 1 : base + 2, :rows]
        bent = nn(systems[row_count : row_count + 2 * TILE, rows : rows + row_count], moved)
        mixed = (
            mixed
            + bent[:TILE] * jnp.concatenate([top, top], axis=1)
            - bent[TILE : 2 * TILE] * jnp.concatenate([bottom, bottom], axis=1)
        )
        placed = nn(jnp.concatenate([mixed[:, :rows], mixed[:, rows:]], axis=0), row_table[...])
        number = row_number((TILE, rows))
        lefty = lax.rem(number, 2) == 0
        real = jnp.where(lefty, placed[2:3], placed[TILE + 2 : TILE + 3])
        imag = jnp.where(lefty, placed[3:4], placed[TILE + 3 : TILE + 4])
        tw = class_rows(classes, me[0], 0)
        opening = number < 2
        even = real * jnp.where(opening, tw[0:1], tw[4:5]) + imag * jnp.where(opening, tw[1:2], tw[5:6])
        odd = real * jnp.where(opening, tw[2:3], tw[6:7]) + imag * jnp.where(opening, tw[3:4], tw[7:8])
        tile = nn(even, fine[:, :half]) + nn(odd, fine[:, half:])
        send_all(send_out, copies_here, left_core.at[1], jnp.where(row_number(tile.shape) == 4, energy, tile))
        keep.wait()

    def folds_kernel(me, seen, systems, leaps, send_out, copies_here, left_core):
        skip = TILE * col_count
        out = nn(leaps[skip:, :skip], seen[...])
        first, second = out[:col_count], out[col_count : 2 * col_count]
        fold_first = systems[row_count : row_count + col_count, :half] * first
        fold_second = systems[row_count : row_count + col_count, half:rows] * second
        energy = out[2 * col_count : 2 * col_count + 1, 0:1] / row_count
        energy = energy - jnp.sum(fold_first * first + fold_second * second)
        table = leaps[aligned(me[0], TILE), :col_count]
        tile = jnp.where(row_number((TILE, half)) < 2, nn(table, fold_first), nn(table, fold_second))
        send_all(send_out, copies_here, left_core.at[0], jnp.where(row_number(tile.shape) == 4, energy, tile))

    def finish_kernel(previous, me, seen, weight, systems, fine, small, classes, row_table, jumps, block, col_table, direction, out, ratio_out, jumps_in, block_in, col_in, direction_in, arrived, ready, left_core):
        pairs = [(jumps, jumps_in), (block, block_in), (col_table, col_in), (direction, direction_in)]
        loads = [pltpu.make_async_copy(src, dst, arrived.at[at]) for at, (src, dst) in enumerate(pairs)]
        for load in loads:
            load.start()

        def strided(at):
            return seen[pl.ds(at, row_count, stride=TILE), :]

        def tw(at):
            slab = classes.shape[0] // 2
            parts = [classes[pl.ds(at + side, row_count, stride=2 * TILE), :] for side in (0, slab)]
            return jnp.concatenate(parts, axis=1)

        waves = jnp.concatenate([strided(0), strided(1), strided(2), strided(3)], axis=0)
        ratio = jnp.sum(strided(4)[:, 0:1]) / previous[0]
        ratio_out[0] = ratio
        even = nt(waves, fine[:, :half])
        odd = nt(waves, fine[:, half:])
        spectra = []
        for at in range(2):
            one, two = slice(at * row_count, (at + 1) * row_count), slice((at + 2) * row_count, (at + 3) * row_count)
            real = even[one] * tw(0) + odd[one] * tw(2) + even[two] * tw(4) + odd[two] * tw(6)
            imag = even[one] * tw(1) + odd[one] * tw(3) + even[two] * tw(5) + odd[two] * tw(7)
            spectra.append(jnp.concatenate([real, imag], axis=0))
        mine = class_rows(classes, me[0], TILE)
        table = jnp.concatenate([small[:base, :base], mine[:, :base]], axis=0)
        pulled = nn(table, jnp.concatenate(spectra, axis=1))
        hats = nt(jnp.concatenate([pulled[:, :rows], pulled[:, rows:]], axis=0), row_table[...])
        top, bottom = small[base : base + 1, :rows], small[base + 1 : base + 2, :rows]
        skip = base + TILE
        both = jnp.concatenate(
            [
                hats[:row_count] * bottom - hats[row_count:base] * top,
                hats[skip : skip + row_count] * bottom - hats[skip + row_count : skip + base] * top,
            ],
            axis=0,
        )
        own_left, own_right = hats[base + 4 : base + 5], hats[skip + base + 4 : skip + base + 5]
        shifts = nn(both, weight[...])
        lefts, rights = small[base + TILE : base + TILE + 1, :cols], small[base + TILE + 1 : base + TILE + 2, :cols]
        loads[0].wait()
        jump = jumps_in[...] + lefts * shifts[:row_count] - rights * shifts[row_count:]
        ends = nn(mine[:, :row_count], systems[:row_count] * jump)
        number = row_number((TILE, rows))
        down = jnp.where(number == 2, own_left, jnp.where(number == 3, -own_right, small[base : base + TILE, rows : 2 * rows]))
        number = row_number((TILE, cols))
        along = jnp.where(number == 0, ends[5:6], jnp.where(number == 1, ends[6:7], small[base + 4 * TILE : base + 5 * TILE, :cols]))
        down = jnp.where(row_number(down.shape) < 4, down, 0.0)
        loads[1].wait()
        spectrum = weight[...] * (block_in[...] + tn(down, along))
        loads[2].wait()
        halfway = nn(spectrum, col_in[...])
        loads[3].wait()
        step = max(cols // 4, half)
        copies = []
        for at in range(cols // step):
            span = slice(at * step, (at + 1) * step)
            ready[:, span] = tn(row_table[...], halfway[:, span]) + ratio * direction_in[:, span]
            copy = pltpu.make_async_copy(ready.at[:, span], out.at[:, span], left_core.at[at])
            copy.start()
            copies.append(copy)
        for copy in copies:
            copy.wait()

    return systems_kernel, classes_kernel, folds_kernel, finish_kernel


def f32(table):
    return jnp.asarray(np.asarray(table, np.float32))


def call(kernel, name, outs, scalars, arrays, flops, scratch=(), room=16 * 2**20):
    spaces = dict(vmem=pltpu.VMEM, hbm=pltpu.HBM, window=pltpu.VMEM, smem=pltpu.SMEM)

    def shape_of(shape, kind):
        made = dict(vmem=pltpu.VMEM, hbm=pltpu.HBM).get(kind, jax.ShapeDtypeStruct)
        return made(shape, jnp.float32)

    def placed(array, kind):
        return array if kind == "window" else pltpu.with_memory_space_constraint(array, spaces[kind])

    moved = sum(4 * int(np.prod(shape)) for shape, _ in outs) + sum(4 * a.size for a, _ in arrays)
    return pl.pallas_call(
        kernel,
        out_shape=[shape_of(*entry) for entry in outs],
        in_specs=[pl.BlockSpec(memory_space=pltpu.SMEM)] * len(scalars)
        + [pl.BlockSpec(memory_space=spaces[kind]) for _, kind in arrays],
        out_specs=[pl.BlockSpec(memory_space=spaces[kind]) for _, kind in outs],
        scratch_shapes=list(scratch),
        name=name,
        compiler_params=pltpu.CompilerParams(vmem_limit_bytes=room),
        cost_estimate=pl.CostEstimate(flops=flops, bytes_accessed=moved, transcendentals=0),
    )(*scalars, *[placed(*entry) for entry in arrays])


def exchange(copies, axis):
    seen = lax.all_to_all(copies, axis, 0, 0, tiled=True)
    return seen.reshape(seen.shape[0] * seen.shape[1], seen.shape[2])


def body(of, row_count, col_count, field, direction, ground, previous):
    rows, cols = field.shape
    half = rows // 2
    me_row = lax.axis_index(ROW).reshape(1)
    me_col = lax.axis_index(COL).reshape(1)
    k = {name: f32(table) for name, table in of.items()}
    systems_kernel, classes_kernel, folds_kernel, finish_kernel = make_kernels(row_count, col_count, rows, cols)

    def space(shape):
        return pltpu.VMEM(shape, jnp.float32)

    two = pltpu.SemaphoreType.DMA((2,))

    def hold(*arrays):
        return [(array, "vmem") for array in arrays]

    loads = (field, k["col_table"], k["row_table"], k["columns"], k["sends"])
    block, weight, send = call(
        edges_kernel,
        "edges",
        [((rows, cols), "hbm"), ((rows, cols), "vmem"), ((row_count, 2 * TILE, half), "hbm")],
        [ground],
        [(array, "hbm") for array in loads],
        2 * rows * cols * (rows + cols),
        [space(array.shape) for array in loads]
        + [pltpu.SemaphoreType.DMA((len(loads),)), space((rows, cols)), space((row_count, 2 * TILE, half)), two],
    )
    seen = exchange(send, ROW)
    (systems,) = call(
        systems_kernel,
        "systems",
        [((row_count + max(col_count, 2 * TILE), cols), "window")],
        [ground, me_row],
        hold(weight, k["columns"], k["small"], k["classes"]),
        2 * rows * cols * 32,
    )
    jumps, send = call(
        classes_kernel,
        "classes",
        [((row_count, cols), "hbm"), ((col_count, TILE, half), "hbm")],
        [me_row],
        hold(seen, weight, systems, k["row_table"], k["fine"], k["small"], k["classes"]),
        2 * rows * cols * 128,
        [space((row_count, cols)), space((col_count, TILE, half)), two],
    )
    seen = exchange(send, COL)
    (send,) = call(
        folds_kernel,
        "folds",
        [((row_count, TILE, half), "hbm")],
        [me_col],
        hold(seen, systems, k["leaps"]),
        2 * rows * cols * 16,
        [space((row_count, TILE, half)), two],
    )
    seen = exchange(send, ROW)
    late = (jumps, block, k["col_table"], direction)
    out, ratio = call(
        finish_kernel,
        "finish",
        [((rows, cols), "hbm"), ((1,), "smem")],
        [previous, me_row],
        hold(seen, weight, systems, k["fine"], k["small"], k["classes"], k["row_table"])
        + [(array, "hbm") for array in late],
        2 * rows * cols * (rows + cols + 128),
        [space(array.shape) for array in late]
        + [pltpu.SemaphoreType.DMA((len(late),)), space((rows, cols)), pltpu.SemaphoreType.DMA((4,))],
    )
    return out, ratio


def solution(mesh):
    row_count, col_count = mesh.shape[ROW], mesh.shape[COL]

    def step(residual, direction, ground_shift, previous):
        rows, cols = residual.shape[0] // row_count, residual.shape[1] // col_count
        of = kernel_constants(rows, cols, row_count, col_count)

        def local(field, heading, ground, last):
            return body(of, row_count, col_count, field, heading, ground, last)

        return jax.shard_map(
            local,
            mesh=mesh,
            in_specs=(P(ROW, COL), P(ROW, COL), P(), P()),
            out_specs=(P(ROW, COL), P()),
            check_vma=False,
        )(residual, direction, ground_shift, previous)

    return step
```

time: 88.5 us -> 75.1 us (0.85)
  local copies, waits for them, and re-layouts: 17.4 us -> 0.04 us
  Pallas kernels: 11.3 us -> 15.4 us
  waiting for transfers between devices: 27.2 us -> 28.5 us
    unnamed x85 -> x12, local copies, waits for them, and re-layouts: 17.4 us -> 0.04 us
    pallas_call x5, Pallas kernels: 11.3 us -> 15.4 us  [call(): pl.pallas_call(kernel, out_shape=[shape_of(*entry) for entry in outs], in...]
    all_to_all x3, waiting for transfers between devices: 27.2 us -> 28.5 us  [exchange(): seen = lax.all_to_all(copies, axis, 0, 0, tiled=True)]
where the time goes in v4:
time: 75.1 us; the launch traced here: 74.7 us
  starting transfers between devices  28.7 us (38%)
  waiting for transfers between devices  28.5 us (38%)
  Pallas kernels  15.4 us (21%)
  between operations  2.06 us (3%)
    all_to_all x3, starting transfers between devices, exchange(): seen = lax.all_to_all(copies, axis, 0, 0, tiled=True)  28.7 us
    all_to_all x3, waiting for transfers between devices, exchange(): seen = lax.all_to_all(copies, axis, 0, 0, tiled=True)  28.5 us
    pallas_call x5, Pallas kernels, call(): pl.pallas_call(kernel, out_shape=[shape_of(*entry) for entry in outs], in...  15.4 us
  transfers between devices with their start and end apart: 3, of which 3 were waited for; matrix products, arithmetic and copies ran while one was open for 0% of the time, Pallas kernels for 1%

profile of v4, /device:TPU:1, one launch (start us, length us, event | category | flops | bytes accessed | tf_op | source)
XLA Modules:
  0.0 74.7 jit_solution(17489909754560206304)
XLA Ops:
  1.3 0.0 copy-start.2
  1.3 0.0 copy-start.4
  1.3 5.5 %edges.1 = (f32[256,512]{1,0:T(8,128)}, f32[256,512]{1,0:T(8,128)S(1)}, f32[32,16,128]{2,1,0:T(8,128)}) custom-call(f32[1]{0:T(128)S(6)} %copy.14.g, f32[256,512]{1,0:T(8,128)} %field.1, f32[512,512]{1,0:T(8,128)} %constant.26.clone.col_table, f32[256,256]{1,0:T(8,128)} %constant.25.clone.row_table, f32[256,128]{1,0:T(8,128)} %constant.27.clone.columns, ...), custom_call_target="tpu_custom_call" | custom-call | flops 201326592 | bytes 3325952 | tf_op jit(solution)/shard_map/edges/pallas_call | solution.py:377
  6.8 0.0 copy-start
  6.8 10.7 %all-to-all-start = ((f32[32,16,128]{2,1,0:T(8,128)}), f32[32,16,128]{2,1,0:T(8,128)S(1)}, u32[]{:S(2)}, u32[]{:S(2)}) async-start(f32[32,16,128]{2,1,0:T(8,128)} %get-tuple-element.7), calls=%async_computation | async-start | bytes 524288 | tf_op jit(solution)/shard_map/all_to_all | solution.py:391
  17.5 0.0 copy-done.2
  17.5 0.0 copy-done.4
  17.5 0.0 copy-done
  17.6 0.0 copy-start.1
  17.6 0.0 copy-start.3
  17.6 0.7 systems.1
  18.3 10.7 %all-to-all-done = f32[32,16,128]{2,1,0:T(8,128)S(1)} async-done(((f32[32,16,128]{2,1,0:T(8,128)}), f32[32,16,128]{2,1,0:T(8,128)S(1)}, u32[]{:S(2)}, u32[]{:S(2)}) %all-to-all-start) | async-done | bytes 262176 | tf_op jit(solution)/shard_map/all_to_all | solution.py:391
  28.9 0.0 copy-done.1
  28.9 0.0 copy-done.3
  29.0 2.4 %classes.4 = (f32[32,512]{1,0:T(8,128)}, f32[16,8,128]{2,1,0:T(8,128)}) custom-call(s32[1]{0:T(128)} %bitcast.me, f32[512,128]{1,0:T(8,128)S(1)} %bitcast.5, f32[256,512]{1,0:T(8,128)S(1)} %get-tuple-element.8.weight, f32[48,512]{1,0:T(8,128)S(1)} %systems.1, f32[256,256]{1,0:T(8,128)S(1)} %copy-done.1, f32[256,256]{1,0:T(8,128)S(1)} %copy-done.3, ...), custom_call_target="tpu_custom_call" | custom-call | flops 33554432 | bytes 2277376 | tf_op jit(solution)/shard_map/classes/pallas_call | solution.py:377
  31.4 0.0 copy-start.5
  31.4 11.8 %all-to-all-start.1 = ((f32[16,8,128]{2,1,0:T(8,128)}), f32[16,8,128]{2,1,0:T(8,128)S(1)}, u32[]{:S(2)}, u32[]{:S(2)}) async-start(f32[16,8,128]{2,1,0:T(8,128)} %get-tuple-element.9), calls=%async_computation.1 | async-start | bytes 131072 | tf_op jit(solution)/shard_map/all_to_all | solution.py:391
  43.3 9.0 %all-to-all-done.1 = f32[16,8,128]{2,1,0:T(8,128)S(1)} async-done(((f32[16,8,128]{2,1,0:T(8,128)}), f32[16,8,128]{2,1,0:T(8,128)S(1)}, u32[]{:S(2)}, u32[]{:S(2)}) %all-to-all-start.1) | async-done | bytes 65568 | tf_op jit(solution)/shard_map/all_to_all | solution.py:391
  52.3 0.0 copy-done.5
  52.3 1.0 %folds.1 = f32[32,8,128]{2,1,0:T(8,128)} custom-call(s32[1]{0:T(128)} %bitcast.1.me, f32[128,128]{1,0:T(8,128)S(1)} %bitcast.7, f32[48,512]{1,0:T(8,128)S(1)} %systems.1, f32[168,128]{1,0:T(8,128)S(1)} %copy-done.5), custom_call_target="tpu_custom_call" | custom-call | flops 4194304 | bytes 380928 | tf_op jit(solution)/shard_map/folds/pallas_call | solution.py:377
  53.3 6.2 %all-to-all-start.2 = ((f32[32,8,128]{2,1,0:T(8,128)}), f32[32,8,128]{2,1,0:T(8,128)S(1)}, u32[]{:S(2)}, u32[]{:S(2)}) async-start(f32[32,8,128]{2,1,0:T(8,128)} %folds.1), calls=%async_computation.2 | async-start | bytes 262144 | tf_op jit(solution)/shard_map/all_to_all | solution.py:391
  60.1 8.8 %all-to-all-done.2 = f32[32,8,128]{2,1,0:T(8,128)S(1)} async-done(((f32[32,8,128]{2,1,0:T(8,128)}), f32[32,8,128]{2,1,0:T(8,128)S(1)}, u32[]{:S(2)}, u32[]{:S(2)}) %all-to-all-start.2) | async-done | bytes 131104 | tf_op jit(solution)/shard_map/all_to_all | solution.py:391
  68.9 5.7 %finish.1 = (f32[256,512]{1,0:T(8,128)}, f32[1]{0:T(128)}) custom-call(f32[1]{0:T(128)S(6)} %copy.15.previous, s32[1]{0:T(128)} %bitcast.me, f32[256,128]{1,0:T(8,128)S(1)} %bitcast.6, f32[256,512]{1,0:T(8,128)S(1)} %get-tuple-element.8.weight, f32[48,512]{1,0:T(8,128)S(1)} %systems.1, f32[256,256]{1,0:T(8,128)S(1)} %copy-done.3, f32[104,512]{1,0:T(8,128)S(1)} %copy-done.2, ...), custom_call_target="tpu_custom_call" | custom-call | flops 234881024 | bytes 4702212 | tf_op jit(solution)/shard_map/finish/pallas_call | solution.py:377
Async XLA Ops:
  1.3 16.3 %copy-start.2 = (f32[104,512]{1,0:T(8,128)S(1)}, f32[104,512]{1,0:T(8,128)}, u32[]{:S(2)}) copy-start(f32[104,512]{1,0:T(8,128)} %constant.29.clone.small) | copy-start | bytes 638980
  1.3 16.2 %copy-start.4 = (f32[256,128]{1,0:T(8,128)S(1)}, f32[256,128]{1,0:T(8,128)}, u32[]{:S(2)}) copy-start(f32[256,128]{1,0:T(8,128)} %constant.27.clone.columns) | copy-start | bytes 393220
  6.8 10.7 %copy-start = (f32[1024,128]{1,0:T(8,128)S(1)}, f32[1024,128]{1,0:T(8,128)}, u32[]{:S(2)}) copy-start(f32[1024,128]{1,0:T(8,128)} %constant.31.clone.classes) | copy-start | bytes 1572868
  6.8 22.1 %all-to-all-start = ((f32[32,16,128]{2,1,0:T(8,128)}), f32[32,16,128]{2,1,0:T(8,128)S(1)}, u32[]{:S(2)}, u32[]{:S(2)}) async-start(f32[32,16,128]{2,1,0:T(8,128)} %get-tuple-element.7), calls=%async_computation | async-start | bytes 524288 | tf_op jit(solution)/shard_map/all_to_all | solution.py:391
  17.6 11.4 %copy-start.1 = (f32[256,256]{1,0:T(8,128)S(1)}, f32[256,256]{1,0:T(8,128)}, u32[]{:S(2)}) copy-start(f32[256,256]{1,0:T(8,128)} %constant.25.clone.row_table) | copy-start | bytes 786436
  17.6 11.4 %copy-start.3 = (f32[256,256]{1,0:T(8,128)S(1)}, f32[256,256]{1,0:T(8,128)}, u32[]{:S(2)}) copy-start(f32[256,256]{1,0:T(8,128)} %constant.32.clone.fine) | copy-start | bytes 786436
  31.4 20.9 %copy-start.5 = (f32[168,128]{1,0:T(8,128)S(1)}, f32[168,128]{1,0:T(8,128)}, u32[]{:S(2)}) copy-start(f32[168,128]{1,0:T(8,128)} %constant.30.clone.leaps) | copy-start | bytes 258052
  31.4 20.9 %all-to-all-start.1 = ((f32[16,8,128]{2,1,0:T(8,128)}), f32[16,8,128]{2,1,0:T(8,128)S(1)}, u32[]{:S(2)}, u32[]{:S(2)}) async-start(f32[16,8,128]{2,1,0:T(8,128)} %get-tuple-element.9), calls=%async_computation.1 | async-start | bytes 131072 | tf_op jit(solution)/shard_map/all_to_all | solution.py:391
  53.3 15.6 %all-to-all-start.2 = ((f32[32,8,128]{2,1,0:T(8,128)}), f32[32,8,128]{2,1,0:T(8,128)S(1)}, u32[]{:S(2)}, u32[]{:S(2)}) async-start(f32[32,8,128]{2,1,0:T(8,128)} %folds.1), calls=%async_computation.2 | async-start | bytes 262144 | tf_op jit(solution)/shard_map/all_to_all | solution.py:391

commit v5 on v4

--- a/solution.py
+++ b/solution.py
@@ -105,15 +105,17 @@
 
     columns = np.zeros((rows, LANES))
     columns[:, 0] = row["lam"]
+    columns[:, 5] = top
     for piece in range(cols // rows):
         columns[:, 8 + piece] = col["lam"][piece * rows : (piece + 1) * rows]
     columns[:row_count, 1:3] = row["gaps"]
     columns[:col_count, 3:5] = col["gaps"]
 
     sends = np.zeros((3 * TILE, cols))
-    sends[0, :rows] = sends[1, rows : 2 * rows] = top
-    sends[2, :rows] = sends[3, rows : 2 * rows] = bottom
-    sends[TILE + 4], sends[TILE + 5] = left, right
+    group = min(LANES, cols)
+    sends[4, :group] = 1.0
+    sends[5, :group] = np.where(np.arange(group) % 2 == 0, 1.0, -1.0)
+    sends[2 * TILE + 1] = left
     sends[2 * TILE] = col["lam"]
 
     small = np.zeros((2 * row_count + 5 * TILE, max(3 * LANES, 2 * rows, cols)))
@@ -156,7 +158,7 @@
             [np.pad(table, ((0, 0), (0, reach - table.shape[1]))) for table in (own_c, leaps)], axis=0
         ),
         classes=np.concatenate([slab.reshape(2 * TILE * row_count, half) for slab in slabs], axis=0),
-        fine=np.concatenate([wave["fine"][:rows], wave["fine"][rows:]], axis=1),
+        fine=wave["fine"],
     )
 
 
@@ -166,6 +168,19 @@
 
 def nt(a, b):
     return lax.dot_general(a, b, (((1,), (1,)), ((), ())), precision=HI, preferred_element_type=jnp.float32)
+
+
+def halves(a):
+    high = a.astype(jnp.bfloat16)
+    return high, (a - high.astype(jnp.float32)).astype(jnp.bfloat16)
+
+
+def three(a, b, dims):
+    def dot(x, y):
+        return lax.dot_general(x, y, (dims, ((), ())), preferred_element_type=jnp.float32)
+
+    (a_high, a_low), (b_high, b_low) = halves(a), halves(b)
+    return dot(a_high, b_high) + (dot(a_high, b_low) + dot(a_low, b_high))
 
 
 def tn(a, b):
@@ -195,27 +210,35 @@
 
 
 def edges_kernel(g, field, col_table, row_table, columns, sends, block_out, weight_out, send_out, field_in, col_in, row_in, columns_in, sends_in, arrived, block_here, copies_here, left_core):
-    rows = field.shape[0]
+    rows, cols = field.shape
     pairs = [(row_table, row_in), (field, field_in), (columns, columns_in), (sends, sends_in), (col_table, col_in)]
     copies = [pltpu.make_async_copy(src, dst, arrived.at[at]) for at, (src, dst) in enumerate(pairs)]
     for copy in copies:
         copy.start()
     copies[0].wait()
     copies[1].wait()
-    halfway = nn(row_in[...], field_in[...])
+    halfway = three(row_in[...], field_in[...], ((1,), (0,)))
     copies[2].wait()
     copies[3].wait()
     weight = 1.0 / (columns_in[:, 0:1] + sends_in[2 * TILE : 2 * TILE + 1] + g[0])
     weight_out[...] = weight
     copies[4].wait()
-    block = nt(halfway, col_in[...])
+    block = three(halfway, col_in[...], ((1,), (1,)))
     solved = weight * block
     block_here[...] = block
     keep = pltpu.make_async_copy(block_here, block_out, left_core.at[0])
     keep.start()
     energy = jnp.sum(solved * block)
-    low, side = sends_in[:TILE], sends_in[TILE : 2 * TILE]
-    tile = nn(low[:, :rows], solved[:, :rows]) + nn(low[:, rows:], solved[:, rows:]) + nt(side, solved)
+    number = row_number((TILE, rows))
+    folded = jnp.sum((solved * columns_in[:, 5:6]).reshape(rows // TILE, TILE, cols), axis=0)
+    tops = jnp.sum(folded, axis=0, keepdims=True)
+    bottoms = jnp.sum(jnp.where(row_number(folded.shape) % 2 == 0, folded, -folded), axis=0, keepdims=True)
+    sided = solved * sends_in[2 * TILE + 1 : 2 * TILE + 2]
+    group = min(LANES, cols)
+    sided = sum(sided[:, at : at + group] for at in range(0, cols, group))
+    tile = nt(sends_in[:TILE, :group], sided)
+    tile = jnp.where(number == 0, tops[:, :rows], jnp.where(number == 1, tops[:, rows:], tile))
+    tile = jnp.where(number == 2, bottoms[:, :rows], jnp.where(number == 3, bottoms[:, rows:], tile))
     tile = jnp.where(row_number(tile.shape) == 6, energy, tile)
     tile = jnp.concatenate([tile[:, : rows // 2], tile[:, rows // 2 :]], axis=0)
     send_all(send_out, copies_here, left_core.at[1], tile)
@@ -275,7 +298,7 @@
         opening = number < 2
         even = real * jnp.where(opening, tw[0:1], tw[4:5]) + imag * jnp.where(opening, tw[1:2], tw[5:6])
         odd = real * jnp.where(opening, tw[2:3], tw[6:7]) + imag * jnp.where(opening, tw[3:4], tw[7:8])
-        tile = nn(even, fine[:, :half]) + nn(odd, fine[:, half:])
+        tile = nn(jnp.concatenate([even, odd], axis=1), fine[...])
         send_all(send_out, copies_here, left_core.at[1], jnp.where(row_number(tile.shape) == 4, energy, tile))
         keep.wait()
 
@@ -308,8 +331,8 @@
         waves = jnp.concatenate([strided(0), strided(1), strided(2), strided(3)], axis=0)
         ratio = jnp.sum(strided(4)[:, 0:1]) / previous[0]
         ratio_out[0] = ratio
-        even = nt(waves, fine[:, :half])
-        odd = nt(waves, fine[:, half:])
+        both = nt(waves, fine[...])
+        even, odd = both[:, :rows], both[:, rows:]
         spectra = []
         for at in range(2):
             one, two = slice(at * row_count, (at + 1) * row_count), slice((at + 2) * row_count, (at + 3) * row_count)
@@ -343,14 +366,13 @@
         loads[1].wait()
         spectrum = weight[...] * (block_in[...] + tn(down, along))
         loads[2].wait()
-        halfway = nn(spectrum, col_in[...])
+        halfway = three(spectrum, col_in[...], ((1,), (0,)))
         loads[3].wait()
-        step = max(cols // 4, half)
         copies = []
-        for at in range(cols // step):
-            span = slice(at * step, (at + 1) * step)
-            ready[:, span] = tn(row_table[...], halfway[:, span]) + ratio * direction_in[:, span]
-            copy = pltpu.make_async_copy(ready.at[:, span], out.at[:, span], left_core.at[at])
+        for at in range(2):
+            span = slice(at * rows // 2, (at + 1) * rows // 2)
+            ready[span] = three(row_table[:, span], halfway, ((0,), (0,))) + ratio * direction_in[span]
+            copy = pltpu.make_async_copy(ready.at[span], out.at[span], left_core.at[at])
             copy.start()
             copies.append(copy)
         for copy in copies:

time: 75.1 us -> 72 us (0.959)
  Pallas kernels: 15.4 us -> 12.3 us
    pallas_call x5, Pallas kernels: 15.4 us -> 12.3 us  [call(): pl.pallas_call(kernel, out_shape=[shape_of(*entry) for entry in outs], in...]
where the time goes in v5:
time: 72 us; the launch traced here: 71.6 us
  starting transfers between devices  28.8 us (40%)
  waiting for transfers between devices  28.4 us (39%)
  Pallas kernels  12.3 us (17%)
  between operations  2.06 us (3%)
    all_to_all x3, starting transfers between devices, exchange(): seen = lax.all_to_all(copies, axis, 0, 0, tiled=True)  28.8 us
    all_to_all x3, waiting for transfers between devices, exchange(): seen = lax.all_to_all(copies, axis, 0, 0, tiled=True)  28.4 us
    pallas_call x5, Pallas kernels, call(): pl.pallas_call(kernel, out_shape=[shape_of(*entry) for entry in outs], in...  12.3 us
  transfers between devices with their start and end apart: 3, of which 3 were waited for; matrix products, arithmetic and copies ran while one was open for 0% of the time, Pallas kernels for 1%

profile of v5, /device:TPU:1, one launch (start us, length us, event | category | flops | bytes accessed | tf_op | source)
XLA Modules:
  0.0 71.6 jit_solution(495718008986764168)
XLA Ops:
  1.3 0.0 copy-start.2
  1.3 0.0 copy-start.4
  1.3 3.5 %edges.1 = (f32[256,512]{1,0:T(8,128)}, f32[256,512]{1,0:T(8,128)S(1)}, f32[32,16,128]{2,1,0:T(8,128)}) custom-call(f32[1]{0:T(128)S(6)} %copy.14.g, f32[256,512]{1,0:T(8,128)} %field.1, f32[512,512]{1,0:T(8,128)} %constant.26.clone.col_table, f32[256,256]{1,0:T(8,128)} %constant.25.clone.row_table, f32[256,128]{1,0:T(8,128)} %constant.27.clone.columns, ...), custom_call_target="tpu_custom_call" | custom-call | flops 201326592 | bytes 3325952 | tf_op jit(solution)/shard_map/edges/pallas_call | solution.py:399
  4.8 0.0 copy-start
  4.8 10.7 %all-to-all-start = ((f32[32,16,128]{2,1,0:T(8,128)}), f32[32,16,128]{2,1,0:T(8,128)S(1)}, u32[]{:S(2)}, u32[]{:S(2)}) async-start(f32[32,16,128]{2,1,0:T(8,128)} %get-tuple-element.7), calls=%async_computation | async-start | bytes 524288 | tf_op jit(solution)/shard_map/all_to_all | solution.py:413
  15.5 0.0 copy-done.2
  15.5 0.0 copy-done.4
  15.5 0.0 copy-done
  15.6 0.0 copy-start.1
  15.6 0.0 copy-start.3
  15.6 0.7 systems.1
  16.3 10.7 %all-to-all-done = f32[32,16,128]{2,1,0:T(8,128)S(1)} async-done(((f32[32,16,128]{2,1,0:T(8,128)}), f32[32,16,128]{2,1,0:T(8,128)S(1)}, u32[]{:S(2)}, u32[]{:S(2)}) %all-to-all-start) | async-done | bytes 262176 | tf_op jit(solution)/shard_map/all_to_all | solution.py:413
  26.9 0.0 copy-done.1
  27.0 0.0 copy-done.3
  27.0 2.4 %classes.4 = (f32[32,512]{1,0:T(8,128)}, f32[16,8,128]{2,1,0:T(8,128)}) custom-call(s32[1]{0:T(128)} %bitcast.me, f32[512,128]{1,0:T(8,128)S(1)} %bitcast.5, f32[256,512]{1,0:T(8,128)S(1)} %get-tuple-element.8.weight, f32[48,512]{1,0:T(8,128)S(1)} %systems.1, f32[256,256]{1,0:T(8,128)S(1)} %copy-done.1, f32[512,128]{1,0:T(8,128)S(1)} %copy-done.3, ...), custom_call_target="tpu_custom_call" | custom-call | flops 33554432 | bytes 2277376 | tf_op jit(solution)/shard_map/classes/pallas_call | solution.py:399
  29.4 0.0 copy-start.5
  29.4 11.8 %all-to-all-start.1 = ((f32[16,8,128]{2,1,0:T(8,128)}), f32[16,8,128]{2,1,0:T(8,128)S(1)}, u32[]{:S(2)}, u32[]{:S(2)}) async-start(f32[16,8,128]{2,1,0:T(8,128)} %get-tuple-element.9), calls=%async_computation.1 | async-start | bytes 131072 | tf_op jit(solution)/shard_map/all_to_all | solution.py:413
  41.3 9.0 %all-to-all-done.1 = f32[16,8,128]{2,1,0:T(8,128)S(1)} async-done(((f32[16,8,128]{2,1,0:T(8,128)}), f32[16,8,128]{2,1,0:T(8,128)S(1)}, u32[]{:S(2)}, u32[]{:S(2)}) %all-to-all-start.1) | async-done | bytes 65568 | tf_op jit(solution)/shard_map/all_to_all | solution.py:413
  50.2 0.0 copy-done.5
  50.2 1.0 %folds.1 = f32[32,8,128]{2,1,0:T(8,128)} custom-call(s32[1]{0:T(128)} %bitcast.1.me, f32[128,128]{1,0:T(8,128)S(1)} %bitcast.7, f32[48,512]{1,0:T(8,128)S(1)} %systems.1, f32[168,128]{1,0:T(8,128)S(1)} %copy-done.5), custom_call_target="tpu_custom_call" | custom-call | flops 4194304 | bytes 380928 | tf_op jit(solution)/shard_map/folds/pallas_call | solution.py:399
  51.3 6.2 %all-to-all-start.2 = ((f32[32,8,128]{2,1,0:T(8,128)}), f32[32,8,128]{2,1,0:T(8,128)S(1)}, u32[]{:S(2)}, u32[]{:S(2)}) async-start(f32[32,8,128]{2,1,0:T(8,128)} %folds.1), calls=%async_computation.2 | async-start | bytes 262144 | tf_op jit(solution)/shard_map/all_to_all | solution.py:413
  58.1 8.8 %all-to-all-done.2 = f32[32,8,128]{2,1,0:T(8,128)S(1)} async-done(((f32[32,8,128]{2,1,0:T(8,128)}), f32[32,8,128]{2,1,0:T(8,128)S(1)}, u32[]{:S(2)}, u32[]{:S(2)}) %all-to-all-start.2) | async-done | bytes 131104 | tf_op jit(solution)/shard_map/all_to_all | solution.py:413
  66.9 4.7 %finish.1 = (f32[256,512]{1,0:T(8,128)}, f32[1]{0:T(128)}) custom-call(f32[1]{0:T(128)S(6)} %copy.15.previous, s32[1]{0:T(128)} %bitcast.me, f32[256,128]{1,0:T(8,128)S(1)} %bitcast.6, f32[256,512]{1,0:T(8,128)S(1)} %get-tuple-element.8.weight, f32[48,512]{1,0:T(8,128)S(1)} %systems.1, f32[512,128]{1,0:T(8,128)S(1)} %copy-done.3, f32[104,512]{1,0:T(8,128)S(1)} %copy-done.2, ...), custom_call_target="tpu_custom_call" | custom-call | flops 234881024 | bytes 4702212 | tf_op jit(solution)/shard_map/finish/pallas_call | solution.py:399
Async XLA Ops:
  1.3 14.3 %copy-start.2 = (f32[104,512]{1,0:T(8,128)S(1)}, f32[104,512]{1,0:T(8,128)}, u32[]{:S(2)}) copy-start(f32[104,512]{1,0:T(8,128)} %constant.29.clone.small) | copy-start | bytes 638980
  1.3 14.3 %copy-start.4 = (f32[256,128]{1,0:T(8,128)S(1)}, f32[256,128]{1,0:T(8,128)}, u32[]{:S(2)}) copy-start(f32[256,128]{1,0:T(8,128)} %constant.27.clone.columns) | copy-start | bytes 393220
  4.8 10.7 %copy-start = (f32[1024,128]{1,0:T(8,128)S(1)}, f32[1024,128]{1,0:T(8,128)}, u32[]{:S(2)}) copy-start(f32[1024,128]{1,0:T(8,128)} %constant.31.clone.classes) | copy-start | bytes 1572868
  4.8 22.1 %all-to-all-start = ((f32[32,16,128]{2,1,0:T(8,128)}), f32[32,16,128]{2,1,0:T(8,128)S(1)}, u32[]{:S(2)}, u32[]{:S(2)}) async-start(f32[32,16,128]{2,1,0:T(8,128)} %get-tuple-element.7), calls=%async_computation | async-start | bytes 524288 | tf_op jit(solution)/shard_map/all_to_all | solution.py:413
  15.6 11.4 %copy-start.1 = (f32[256,256]{1,0:T(8,128)S(1)}, f32[256,256]{1,0:T(8,128)}, u32[]{:S(2)}) copy-start(f32[256,256]{1,0:T(8,128)} %constant.25.clone.row_table) | copy-start | bytes 786436
  15.6 11.4 %copy-start.3 = (f32[512,128]{1,0:T(8,128)S(1)}, f32[512,128]{1,0:T(8,128)}, u32[]{:S(2)}) copy-start(f32[512,128]{1,0:T(8,128)} %constant.32.clone.fine) | copy-start | bytes 786436
  29.4 20.8 %copy-start.5 = (f32[168,128]{1,0:T(8,128)S(1)}, f32[168,128]{1,0:T(8,128)}, u32[]{:S(2)}) copy-start(f32[168,128]{1,0:T(8,128)} %constant.30.clone.leaps) | copy-start | bytes 258052
  29.4 20.8 %all-to-all-start.1 = ((f32[16,8,128]{2,1,0:T(8,128)}), f32[16,8,128]{2,1,0:T(8,128)S(1)}, u32[]{:S(2)}, u32[]{:S(2)}) async-start(f32[16,8,128]{2,1,0:T(8,128)} %get-tuple-element.9), calls=%async_computation.1 | async-start | bytes 131072 | tf_op jit(solution)/shard_map/all_to_all | solution.py:413
  51.3 15.7 %all-to-all-start.2 = ((f32[32,8,128]{2,1,0:T(8,128)}), f32[32,8,128]{2,1,0:T(8,128)S(1)}, u32[]{:S(2)}, u32[]{:S(2)}) async-start(f32[32,8,128]{2,1,0:T(8,128)} %folds.1), calls=%async_computation.2 | async-start | bytes 262144 | tf_op jit(solution)/shard_map/all_to_all | solution.py:413

commit v6 on v5

--- a/solution.py
+++ b/solution.py
@@ -4,11 +4,13 @@
 from jax import lax
 from jax.experimental import pallas as pl
 from jax.experimental.pallas import tpu as pltpu
+from jax.sharding import Mesh
 from jax.sharding import PartitionSpec as P
 
-ROW = "row"
-COL = "col"
+ROW = ("pair", "core")
+PAIR, CORE, COL = "pair", "core", "col"
 TILE = 8
+WAVES = 5
 LANES = 128
 
 HI = lax.Precision.HIGHEST
@@ -103,6 +105,7 @@
     dst_c, after_c = col["dst"], col["after"]
     unmix = np.concatenate([mix[:, 0].T, mix[:, 1].T], axis=1)
 
+    order = np.concatenate([np.arange(0, row_count, 2), np.arange(1, row_count, 2)])
     columns = np.zeros((rows, LANES))
     columns[:, 0] = row["lam"]
     columns[:, 5] = top
@@ -120,7 +123,7 @@
 
     small = np.zeros((2 * row_count + 5 * TILE, max(3 * LANES, 2 * rows, cols)))
     small[: 2 * row_count, : 2 * row_count] = np.concatenate([after.T @ unmix, dst.T @ unmix], axis=0)
-    small[:row_count, LANES : LANES + 2 * row_count] = np.concatenate([after.T, -dst.T], axis=1)
+    small[:row_count, LANES : LANES + 2 * row_count] = np.concatenate([after.T[:, order], -dst.T[:, order]], axis=1)
     small[:row_count, 2 * LANES : 2 * LANES + row_count] = dst
     small[row_count : 2 * row_count, 2 * LANES : 2 * LANES + row_count] = after
     base = 2 * row_count
@@ -145,6 +148,7 @@
     classes[:, 8, :rows] = wave["lam"].reshape(row_count, rows)
     classes[:, 9, :rows] = wave["energy"].reshape(row_count, rows)
     classes[:, 10, :row_count], classes[:, 11, :row_count] = mix[:, 0], mix[:, 1]
+    classes[:, 10, half : half + row_count], classes[:, 11, half : half + row_count] = mix[:, 0][:, order], mix[:, 1][:, order]
     classes[:, 12, : 2 * row_count] = unmix
     classes[:, 13, :row_count], classes[:, 14, :row_count] = dst, after
     slabs = [classes[:, :, :half], classes[:, :, half:rows]]
@@ -183,8 +187,18 @@
     return dot(a_high, b_high) + (dot(a_high, b_low) + dot(a_low, b_high))
 
 
-def tn(a, b):
-    return lax.dot_general(a, b, (((0,), (0,)), ((), ())), precision=HI, preferred_element_type=jnp.float32)
+def thirds(a):
+    high = a.astype(jnp.bfloat16).astype(jnp.float32)
+    rest = a - high
+    middle = rest.astype(jnp.bfloat16).astype(jnp.float32)
+    return high, middle, rest - middle
+
+
+def outer(a, b):
+    (a_one, a_two, a_three), (b_one, b_two, b_three) = thirds(a), thirds(b)
+    left = jnp.concatenate([a_one, a_one, a_two, a_one, a_two, a_three], axis=0).astype(jnp.bfloat16)
+    right = jnp.concatenate([b_one, b_two, b_one, b_three, b_two, b_one], axis=0).astype(jnp.bfloat16)
+    return lax.dot_general(left, right, (((0,), (0,)), ((), ())), preferred_element_type=jnp.float32)
 
 
 def row_number(shape):
@@ -280,7 +294,7 @@
         lefts, rights = small[base + TILE : base + TILE + 1, :cols], small[base + TILE + 1 : base + TILE + 2, :cols]
         moved = nt(jnp.concatenate([bends * lefts, bends * rights], axis=0), weight[...])
         moved = jnp.concatenate([moved[:row_count], moved[row_count:]], axis=1)
-        mine = class_rows(classes, me[0], TILE)[:, :row_count]
+        mine = class_rows(classes, me[0], TILE)[:, half : half + row_count]
         mixed = nn(mine, jnp.concatenate([strided(4), strided(5)], axis=1))
         top, bottom = small[base : base + 1, :rows], small[base + 1 : base + 2, :rows]
         bent = nn(systems[row_count : row_count + 2 * TILE, rows : rows + row_count], moved)
@@ -312,7 +326,12 @@
         energy = energy - jnp.sum(fold_first * first + fold_second * second)
         table = leaps[aligned(me[0], TILE), :col_count]
         tile = jnp.where(row_number((TILE, half)) < 2, nn(table, fold_first), nn(table, fold_second))
-        send_all(send_out, copies_here, left_core.at[0], jnp.where(row_number(tile.shape) == 4, energy, tile))
+        tile = jnp.where(row_number(tile.shape) == 4, energy, tile)
+        for peer in range(row_count):
+            copies_here[pl.ds(peer * WAVES, WAVES), :] = tile[:WAVES]
+        copy = pltpu.make_async_copy(copies_here, send_out, left_core.at[0])
+        copy.start()
+        copy.wait()
 
     def finish_kernel(previous, me, seen, weight, systems, fine, small, classes, row_table, jumps, block, col_table, direction, out, ratio_out, jumps_in, block_in, col_in, direction_in, arrived, ready, left_core):
         pairs = [(jumps, jumps_in), (block, block_in), (col_table, col_in), (direction, direction_in)]
@@ -321,7 +340,7 @@
             load.start()
 
         def strided(at):
-            return seen[pl.ds(at, row_count, stride=TILE), :]
+            return seen[pl.ds(at, row_count, stride=WAVES), :]
 
         def tw(at):
             slab = classes.shape[0] // 2
@@ -364,7 +383,7 @@
         along = jnp.where(number == 0, ends[5:6], jnp.where(number == 1, ends[6:7], small[base + 4 * TILE : base + 5 * TILE, :cols]))
         down = jnp.where(row_number(down.shape) < 4, down, 0.0)
         loads[1].wait()
-        spectrum = weight[...] * (block_in[...] + tn(down, along))
+        spectrum = weight[...] * (block_in[...] + outer(down, along))
         loads[2].wait()
         halfway = three(spectrum, col_in[...], ((1,), (0,)))
         loads[3].wait()
@@ -434,14 +453,15 @@
     block, weight, send = call(
         edges_kernel,
         "edges",
-        [((rows, cols), "hbm"), ((rows, cols), "vmem"), ((row_count, 2 * TILE, half), "hbm")],
+        [((rows, cols), "hbm"), ((rows, cols), "vmem"), ((row_count // 2, 2 * TILE, half), "hbm")],
         [ground],
         [(array, "hbm") for array in loads],
         2 * rows * cols * (rows + cols),
         [space(array.shape) for array in loads]
-        + [pltpu.SemaphoreType.DMA((len(loads),)), space((rows, cols)), space((row_count, 2 * TILE, half)), two],
-    )
-    seen = exchange(send, ROW)
+        + [pltpu.SemaphoreType.DMA((len(loads),)), space((rows, cols)), space((row_count // 2, 2 * TILE, half)), two],
+    )
+    seen = lax.all_gather(lax.all_to_all(send, PAIR, 0, 0, tiled=True), CORE)
+    seen = seen.reshape(2 * TILE * row_count, half)
     (systems,) = call(
         systems_kernel,
         "systems",
@@ -463,13 +483,13 @@
     (send,) = call(
         folds_kernel,
         "folds",
-        [((row_count, TILE, half), "hbm")],
+        [((row_count * WAVES, half), "hbm")],
         [me_col],
         hold(seen, systems, k["leaps"]),
         2 * rows * cols * 16,
-        [space((row_count, TILE, half)), two],
-    )
-    seen = exchange(send, ROW)
+        [space((row_count * WAVES, half)), two],
+    )
+    seen = exchange(send.reshape(row_count, 1, WAVES * half), ROW).reshape(row_count * WAVES, half)
     late = (jumps, block, k["col_table"], direction)
     out, ratio = call(
         finish_kernel,
@@ -486,7 +506,8 @@
 
 
 def solution(mesh):
-    row_count, col_count = mesh.shape[ROW], mesh.shape[COL]
+    row_count, col_count = mesh.shape["row"], mesh.shape[COL]
+    finer = Mesh(mesh.devices.reshape(row_count // 2, 2, col_count), (PAIR, CORE, COL))
 
     def step(residual, direction, ground_shift, previous):
         rows, cols = residual.shape[0] // row_count, residual.shape[1] // col_count
@@ -497,7 +518,7 @@
 
         return jax.shard_map(
             local,
-            mesh=mesh,
+            mesh=finer,
             in_specs=(P(ROW, COL), P(ROW, COL), P(), P()),
             out_specs=(P(ROW, COL), P()),
             check_vma=False,

time: 72 us -> 69.5 us (0.965)
  waiting for transfers between devices: 28.4 us -> 24.6 us
  blocking collectives: 0 us -> 3.71 us
  starting transfers between devices: 28.8 us -> 26.9 us
    all_to_all x3 -> x2, starting transfers between devices: 28.8 us -> 17.2 us  [exchange(): seen = lax.all_to_all(copies, axis, 0, 0, tiled=True)]
    all_to_all x3 -> x2, waiting for transfers between devices: 28.4 us -> 16.9 us  [exchange(): seen = lax.all_to_all(copies, axis, 0, 0, tiled=True)]
    all_to_all x0 -> x1, starting transfers between devices: none -> 9.7 us  [body(): seen = lax.all_gather(lax.all_to_all(send, PAIR, 0, 0, tiled=True), CORE)]
    all_to_all x0 -> x1, waiting for transfers between devices: none -> 7.72 us  [body(): seen = lax.all_gather(lax.all_to_all(send, PAIR, 0, 0, tiled=True), CORE)]
    all_gather x0 -> x1, blocking collectives: none -> 3.71 us  [body(): seen = lax.all_gather(lax.all_to_all(send, PAIR, 0, 0, tiled=True), CORE)]
where the time goes in v6:
time: 69.5 us; the launch traced here: 69.2 us
  starting transfers between devices  26.9 us (39%)
  waiting for transfers between devices  24.6 us (35%)
  Pallas kernels  11.9 us (17%)
  blocking collectives  3.71 us (5%)
  between operations  2.06 us (3%)
    all_to_all x2, starting transfers between devices, exchange(): seen = lax.all_to_all(copies, axis, 0, 0, tiled=True)  17.2 us
    all_to_all x2, waiting for transfers between devices, exchange(): seen = lax.all_to_all(copies, axis, 0, 0, tiled=True)  16.9 us
    pallas_call x5, Pallas kernels, call(): pl.pallas_call(kernel, out_shape=[shape_of(*entry) for entry in outs], in...  11.9 us
    all_to_all x1, starting transfers between devices, body(): seen = lax.all_gather(lax.all_to_all(send, PAIR, 0, 0, tiled=True), CORE)  9.7 us
    all_to_all x1, waiting for transfers between devices, body(): seen = lax.all_gather(lax.all_to_all(send, PAIR, 0, 0, tiled=True), CORE)  7.72 us
    all_gather x1, blocking collectives, body(): seen = lax.all_gather(lax.all_to_all(send, PAIR, 0, 0, tiled=True), CORE)  3.71 us
  transfers between devices with their start and end apart: 3, of which 3 were waited for; matrix products, arithmetic and copies ran while one was open for 0% of the time, Pallas kernels for 1%

profile of v6, /device:TPU:1, one launch (start us, length us, event | category | flops | bytes accessed | tf_op | source)
XLA Modules:
  0.0 69.2 jit_solution(11100054634494196367)
XLA Ops:
  1.3 0.0 copy-start
  1.3 0.0 copy-start.4
  1.3 3.5 %edges.1 = (f32[256,512]{1,0:T(8,128)}, f32[256,512]{1,0:T(8,128)S(1)}, f32[16,16,128]{2,1,0:T(8,128)}) custom-call(f32[1]{0:T(128)S(6)} %copy.15.g, f32[256,512]{1,0:T(8,128)} %field.1, f32[512,512]{1,0:T(8,128)} %constant.32.clone.col_table, f32[256,256]{1,0:T(8,128)} %constant.31.clone.row_table, f32[256,128]{1,0:T(8,128)} %constant.33.clone.columns, ...), custom_call_target="tpu_custom_call" | custom-call | flops 201326592 | bytes 3194880 | tf_op jit(solution)/shard_map/edges/pallas_call | solution.py:418
  4.8 0.0 copy-start.2
  4.8 9.7 %all-to-all-start = ((f32[16,16,128]{2,1,0:T(8,128)}), f32[16,16,128]{2,1,0:T(8,128)S(1)}, u32[]{:S(2)}, u32[]{:S(2)}) async-start(f32[16,16,128]{2,1,0:T(8,128)} %get-tuple-element.7), calls=%async_computation | async-start | bytes 262144 | tf_op jit(solution)/shard_map/all_to_all | solution.py:463
  14.5 0.0 copy-done
  14.5 0.0 copy-done.4
  14.5 0.0 copy-done.2
  14.5 0.0 copy-start.3
  14.5 0.7 systems.1
  15.2 0.0 copy-start.1
  15.2 7.7 %all-to-all-done = f32[16,16,128]{2,1,0:T(8,128)S(1)} async-done(((f32[16,16,128]{2,1,0:T(8,128)}), f32[16,16,128]{2,1,0:T(8,128)S(1)}, u32[]{:S(2)}, u32[]{:S(2)}) %all-to-all-start) | async-done | bytes 131104 | tf_op jit(solution)/shard_map/all_to_all | solution.py:463
  23.0 3.7 %all-gather = f32[32,16,128]{2,1,0:T(8,128)S(1)} all-gather(f32[16,16,128]{2,1,0:T(8,128)S(1)} %all-to-all-done), channel_id=2, replica_groups=mesh['pair'=16,'core'=2,'col'=16] {'core'}, dimensions={0}, use_global_device_ids=true | all-gather | bytes 393216 | tf_op jit(solution)/shard_map/all_gather | solution.py:463
  26.7 0.0 copy-done.3
  26.7 0.0 copy-done.1
  26.7 2.4 %classes.4 = (f32[32,512]{1,0:T(8,128)}, f32[16,8,128]{2,1,0:T(8,128)}) custom-call(s32[1]{0:T(128)} %bitcast.me, f32[512,128]{1,0:T(8,128)S(1)} %bitcast.6, f32[256,512]{1,0:T(8,128)S(1)} %get-tuple-element.8.weight, f32[48,512]{1,0:T(8,128)S(1)} %systems.1, f32[256,256]{1,0:T(8,128)S(1)} %copy-done.1, f32[512,128]{1,0:T(8,128)S(1)} %copy-done.3, ...), custom_call_target="tpu_custom_call" | custom-call | flops 33554432 | bytes 2277376 | tf_op jit(solution)/shard_map/classes/pallas_call | solution.py:418
  29.1 0.0 copy-start.5
  29.1 11.8 %all-to-all-start.1 = ((f32[16,8,128]{2,1,0:T(8,128)}), f32[16,8,128]{2,1,0:T(8,128)S(1)}, u32[]{:S(2)}, u32[]{:S(2)}) async-start(f32[16,8,128]{2,1,0:T(8,128)} %get-tuple-element.9), calls=%async_computation.1 | async-start | bytes 131072 | tf_op jit(solution)/shard_map/all_to_all | solution.py:432
  41.0 8.9 %all-to-all-done.1 = f32[16,8,128]{2,1,0:T(8,128)S(1)} async-done(((f32[16,8,128]{2,1,0:T(8,128)}), f32[16,8,128]{2,1,0:T(8,128)S(1)}, u32[]{:S(2)}, u32[]{:S(2)}) %all-to-all-start.1) | async-done | bytes 65568 | tf_op jit(solution)/shard_map/all_to_all | solution.py:432
  49.9 0.0 copy-done.5
  49.9 1.0 %folds.1 = f32[160,128]{1,0:T(8,128)} custom-call(s32[1]{0:T(128)} %bitcast.1.me, f32[128,128]{1,0:T(8,128)S(1)} %bitcast.8, f32[48,512]{1,0:T(8,128)S(1)} %systems.1, f32[168,128]{1,0:T(8,128)S(1)} %copy-done.5), custom_call_target="tpu_custom_call" | custom-call | flops 4194304 | bytes 331776 | tf_op jit(solution)/shard_map/folds/pallas_call | solution.py:418
  50.9 5.3 %all-to-all-start.2 = ((f32[32,1,640]{2,1,0:T(1,128)}), f32[32,1,640]{2,1,0:T(1,128)S(1)}, u32[]{:S(2)}, u32[]{:S(2)}) async-start(f32[32,1,640]{2,1,0:T(1,128)} %bitcast.9), calls=%async_computation.2 | async-start | bytes 163840 | tf_op jit(solution)/shard_map/all_to_all | solution.py:432
  56.9 7.9 %all-to-all-done.2 = f32[32,1,640]{2,1,0:T(1,128)S(1)} async-done(((f32[32,1,640]{2,1,0:T(1,128)}), f32[32,1,640]{2,1,0:T(1,128)S(1)}, u32[]{:S(2)}, u32[]{:S(2)}) %all-to-all-start.2) | async-done | bytes 81952 | tf_op jit(solution)/shard_map/all_to_all | solution.py:432
  64.9 4.3 %finish.1 = (f32[256,512]{1,0:T(8,128)}, f32[1]{0:T(128)}) custom-call(f32[1]{0:T(128)S(6)} %copy.16.previous, s32[1]{0:T(128)} %bitcast.me, f32[160,128]{1,0:T(8,128)S(1)} %bitcast.7, f32[256,512]{1,0:T(8,128)S(1)} %get-tuple-element.8.weight, f32[48,512]{1,0:T(8,128)S(1)} %systems.1, f32[512,128]{1,0:T(8,128)S(1)} %copy-done.3, f32[104,512]{1,0:T(8,128)S(1)} %copy-done.2, ...), custom_call_target="tpu_custom_call" | custom-call | flops 234881024 | bytes 4653060 | tf_op jit(solution)/shard_map/finish/pallas_call | solution.py:418
Async XLA Ops:
  1.3 13.2 %copy-start = (f32[1024,128]{1,0:T(8,128)S(1)}, f32[1024,128]{1,0:T(8,128)}, u32[]{:S(2)}) copy-start(f32[1024,128]{1,0:T(8,128)} %constant.37.clone.classes) | copy-start | bytes 1572868
  1.3 13.2 %copy-start.4 = (f32[256,128]{1,0:T(8,128)S(1)}, f32[256,128]{1,0:T(8,128)}, u32[]{:S(2)}) copy-start(f32[256,128]{1,0:T(8,128)} %constant.33.clone.columns) | copy-start | bytes 393220
  4.8 9.8 %copy-start.2 = (f32[104,512]{1,0:T(8,128)S(1)}, f32[104,512]{1,0:T(8,128)}, u32[]{:S(2)}) copy-start(f32[104,512]{1,0:T(8,128)} %constant.35.clone.small) | copy-start | bytes 638980
  4.8 18.2 %all-to-all-start = ((f32[16,16,128]{2,1,0:T(8,128)}), f32[16,16,128]{2,1,0:T(8,128)S(1)}, u32[]{:S(2)}, u32[]{:S(2)}) async-start(f32[16,16,128]{2,1,0:T(8,128)} %get-tuple-element.7), calls=%async_computation | async-start | bytes 262144 | tf_op jit(solution)/shard_map/all_to_all | solution.py:463
  14.5 12.1 %copy-start.3 = (f32[512,128]{1,0:T(8,128)S(1)}, f32[512,128]{1,0:T(8,128)}, u32[]{:S(2)}) copy-start(f32[512,128]{1,0:T(8,128)} %constant.38.clone.fine) | copy-start | bytes 786436
  15.2 11.4 %copy-start.1 = (f32[256,256]{1,0:T(8,128)S(1)}, f32[256,256]{1,0:T(8,128)}, u32[]{:S(2)}) copy-start(f32[256,256]{1,0:T(8,128)} %constant.31.clone.row_table) | copy-start | bytes 786436
  29.1 20.8 %copy-start.5 = (f32[168,128]{1,0:T(8,128)S(1)}, f32[168,128]{1,0:T(8,128)}, u32[]{:S(2)}) copy-start(f32[168,128]{1,0:T(8,128)} %constant.36.clone.leaps) | copy-start | bytes 258052
  29.1 20.8 %all-to-all-start.1 = ((f32[16,8,128]{2,1,0:T(8,128)}), f32[16,8,128]{2,1,0:T(8,128)S(1)}, u32[]{:S(2)}, u32[]{:S(2)}) async-start(f32[16,8,128]{2,1,0:T(8,128)} %get-tuple-element.9), calls=%async_computation.1 | async-start | bytes 131072 | tf_op jit(solution)/shard_map/all_to_all | solution.py:432
  50.9 13.9 %all-to-all-start.2 = ((f32[32,1,640]{2,1,0:T(1,128)}), f32[32,1,640]{2,1,0:T(1,128)S(1)}, u32[]{:S(2)}, u32[]{:S(2)}) async-start(f32[32,1,640]{2,1,0:T(1,128)} %bitcast.9), calls=%async_computation.2 | async-start | bytes 163840 | tf_op jit(solution)/shard_map/all_to_all | solution.py:432

commit v7 on v6

--- a/solution.py
+++ b/solution.py
@@ -312,7 +312,7 @@
         opening = number < 2
         even = real * jnp.where(opening, tw[0:1], tw[4:5]) + imag * jnp.where(opening, tw[1:2], tw[5:6])
         odd = real * jnp.where(opening, tw[2:3], tw[6:7]) + imag * jnp.where(opening, tw[3:4], tw[7:8])
-        tile = nn(jnp.concatenate([even, odd], axis=1), fine[...])
+        tile = three(jnp.concatenate([even, odd], axis=1), fine[...], ((1,), (0,)))
         send_all(send_out, copies_here, left_core.at[1], jnp.where(row_number(tile.shape) == 4, energy, tile))
         keep.wait()
 
@@ -350,7 +350,7 @@
         waves = jnp.concatenate([strided(0), strided(1), strided(2), strided(3)], axis=0)
         ratio = jnp.sum(strided(4)[:, 0:1]) / previous[0]
         ratio_out[0] = ratio
-        both = nt(waves, fine[...])
+        both = three(waves, fine[...], ((1,), (1,)))
         even, odd = both[:, :rows], both[:, rows:]
         spectra = []
         for at in range(2):
@@ -361,7 +361,7 @@
         mine = class_rows(classes, me[0], TILE)
         table = jnp.concatenate([small[:base, :base], mine[:, :base]], axis=0)
         pulled = nn(table, jnp.concatenate(spectra, axis=1))
-        hats = nt(jnp.concatenate([pulled[:, :rows], pulled[:, rows:]], axis=0), row_table[...])
+        hats = three(jnp.concatenate([pulled[:, :rows], pulled[:, rows:]], axis=0), row_table[...], ((1,), (1,)))
         top, bottom = small[base : base + 1, :rows], small[base + 1 : base + 2, :rows]
         skip = base + TILE
         both = jnp.concatenate(

time: 69.5 us -> 69.2 us (level)
  no operation moved by 1% of the time
where the time goes in v7:
time: 69.2 us; the launch traced here: 68.9 us
  starting transfers between devices  26.9 us (39%)
  waiting for transfers between devices  24.6 us (36%)
  Pallas kernels  11.6 us (17%)
  blocking collectives  3.71 us (5%)
  between operations  2.06 us (3%)
    all_to_all x2, starting transfers between devices, exchange(): seen = lax.all_to_all(copies, axis, 0, 0, tiled=True)  17.2 us
    all_to_all x2, waiting for transfers between devices, exchange(): seen = lax.all_to_all(copies, axis, 0, 0, tiled=True)  16.9 us
    pallas_call x5, Pallas kernels, call(): pl.pallas_call(kernel, out_shape=[shape_of(*entry) for entry in outs], in...  11.6 us
    all_to_all x1, starting transfers between devices, body(): seen = lax.all_gather(lax.all_to_all(send, PAIR, 0, 0, tiled=True), CORE)  9.7 us
    all_to_all x1, waiting for transfers between devices, body(): seen = lax.all_gather(lax.all_to_all(send, PAIR, 0, 0, tiled=True), CORE)  7.72 us
    all_gather x1, blocking collectives, body(): seen = lax.all_gather(lax.all_to_all(send, PAIR, 0, 0, tiled=True), CORE)  3.71 us
  transfers between devices with their start and end apart: 3, of which 3 were waited for; matrix products, arithmetic and copies ran while one was open for 0% of the time, Pallas kernels for 1%

profile of v7, /device:TPU:1, one launch (start us, length us, event | category | flops | bytes accessed | tf_op | source)
XLA Modules:
  0.0 68.9 jit_solution(5708636144241769553)
XLA Ops:
  1.3 0.0 copy-start
  1.3 0.0 copy-start.4
  1.3 3.5 %edges.1 = (f32[256,512]{1,0:T(8,128)}, f32[256,512]{1,0:T(8,128)S(1)}, f32[16,16,128]{2,1,0:T(8,128)}) custom-call(f32[1]{0:T(128)S(6)} %copy.15.g, f32[256,512]{1,0:T(8,128)} %field.1, f32[512,512]{1,0:T(8,128)} %constant.32.clone.col_table, f32[256,256]{1,0:T(8,128)} %constant.31.clone.row_table, f32[256,128]{1,0:T(8,128)} %constant.33.clone.columns, ...), custom_call_target="tpu_custom_call" | custom-call | flops 201326592 | bytes 3194880 | tf_op jit(solution)/shard_map/edges/pallas_call | solution.py:418
  4.8 0.0 copy-start.2
  4.8 9.7 %all-to-all-start = ((f32[16,16,128]{2,1,0:T(8,128)}), f32[16,16,128]{2,1,0:T(8,128)S(1)}, u32[]{:S(2)}, u32[]{:S(2)}) async-start(f32[16,16,128]{2,1,0:T(8,128)} %get-tuple-element.7), calls=%async_computation | async-start | bytes 262144 | tf_op jit(solution)/shard_map/all_to_all | solution.py:463
  14.5 0.0 copy-done
  14.5 0.0 copy-done.4
  14.5 0.0 copy-done.2
  14.5 0.0 copy-start.3
  14.5 0.7 systems.1
  15.2 0.0 copy-start.1
  15.2 7.7 %all-to-all-done = f32[16,16,128]{2,1,0:T(8,128)S(1)} async-done(((f32[16,16,128]{2,1,0:T(8,128)}), f32[16,16,128]{2,1,0:T(8,128)S(1)}, u32[]{:S(2)}, u32[]{:S(2)}) %all-to-all-start) | async-done | bytes 131104 | tf_op jit(solution)/shard_map/all_to_all | solution.py:463
  23.0 3.7 %all-gather = f32[32,16,128]{2,1,0:T(8,128)S(1)} all-gather(f32[16,16,128]{2,1,0:T(8,128)S(1)} %all-to-all-done), channel_id=2, replica_groups=mesh['pair'=16,'core'=2,'col'=16] {'core'}, dimensions={0}, use_global_device_ids=true | all-gather | bytes 393216 | tf_op jit(solution)/shard_map/all_gather | solution.py:463
  26.7 0.0 copy-done.3
  26.7 0.0 copy-done.1
  26.7 2.3 %classes.4 = (f32[32,512]{1,0:T(8,128)}, f32[16,8,128]{2,1,0:T(8,128)}) custom-call(s32[1]{0:T(128)} %bitcast.me, f32[512,128]{1,0:T(8,128)S(1)} %bitcast.6, f32[256,512]{1,0:T(8,128)S(1)} %get-tuple-element.8.weight, f32[48,512]{1,0:T(8,128)S(1)} %systems.1, f32[256,256]{1,0:T(8,128)S(1)} %copy-done.1, f32[512,128]{1,0:T(8,128)S(1)} %copy-done.3, ...), custom_call_target="tpu_custom_call" | custom-call | flops 33554432 | bytes 2277376 | tf_op jit(solution)/shard_map/classes/pallas_call | solution.py:418
  29.0 0.0 copy-start.5
  29.0 11.8 %all-to-all-start.1 = ((f32[16,8,128]{2,1,0:T(8,128)}), f32[16,8,128]{2,1,0:T(8,128)S(1)}, u32[]{:S(2)}, u32[]{:S(2)}) async-start(f32[16,8,128]{2,1,0:T(8,128)} %get-tuple-element.9), calls=%async_computation.1 | async-start | bytes 131072 | tf_op jit(solution)/shard_map/all_to_all | solution.py:432
  40.9 8.9 %all-to-all-done.1 = f32[16,8,128]{2,1,0:T(8,128)S(1)} async-done(((f32[16,8,128]{2,1,0:T(8,128)}), f32[16,8,128]{2,1,0:T(8,128)S(1)}, u32[]{:S(2)}, u32[]{:S(2)}) %all-to-all-start.1) | async-done | bytes 65568 | tf_op jit(solution)/shard_map/all_to_all | solution.py:432
  49.8 0.0 copy-done.5
  49.8 1.0 %folds.1 = f32[160,128]{1,0:T(8,128)} custom-call(s32[1]{0:T(128)} %bitcast.1.me, f32[128,128]{1,0:T(8,128)S(1)} %bitcast.8, f32[48,512]{1,0:T(8,128)S(1)} %systems.1, f32[168,128]{1,0:T(8,128)S(1)} %copy-done.5), custom_call_target="tpu_custom_call" | custom-call | flops 4194304 | bytes 331776 | tf_op jit(solution)/shard_map/folds/pallas_call | solution.py:418
  50.8 5.3 %all-to-all-start.2 = ((f32[32,1,640]{2,1,0:T(1,128)}), f32[32,1,640]{2,1,0:T(1,128)S(1)}, u32[]{:S(2)}, u32[]{:S(2)}) async-start(f32[32,1,640]{2,1,0:T(1,128)} %bitcast.9), calls=%async_computation.2 | async-start | bytes 163840 | tf_op jit(solution)/shard_map/all_to_all | solution.py:432
  56.8 7.9 %all-to-all-done.2 = f32[32,1,640]{2,1,0:T(1,128)S(1)} async-done(((f32[32,1,640]{2,1,0:T(1,128)}), f32[32,1,640]{2,1,0:T(1,128)S(1)}, u32[]{:S(2)}, u32[]{:S(2)}) %all-to-all-start.2) | async-done | bytes 81952 | tf_op jit(solution)/shard_map/all_to_all | solution.py:432
  64.7 4.1 %finish.1 = (f32[256,512]{1,0:T(8,128)}, f32[1]{0:T(128)}) custom-call(f32[1]{0:T(128)S(6)} %copy.16.previous, s32[1]{0:T(128)} %bitcast.me, f32[160,128]{1,0:T(8,128)S(1)} %bitcast.7, f32[256,512]{1,0:T(8,128)S(1)} %get-tuple-element.8.weight, f32[48,512]{1,0:T(8,128)S(1)} %systems.1, f32[512,128]{1,0:T(8,128)S(1)} %copy-done.3, f32[104,512]{1,0:T(8,128)S(1)} %copy-done.2, ...), custom_call_target="tpu_custom_call" | custom-call | flops 234881024 | bytes 4653060 | tf_op jit(solution)/shard_map/finish/pallas_call | solution.py:418
Async XLA Ops:
  1.3 13.2 %copy-start = (f32[1024,128]{1,0:T(8,128)S(1)}, f32[1024,128]{1,0:T(8,128)}, u32[]{:S(2)}) copy-start(f32[1024,128]{1,0:T(8,128)} %constant.37.clone.classes) | copy-start | bytes 1572868
  1.3 13.2 %copy-start.4 = (f32[256,128]{1,0:T(8,128)S(1)}, f32[256,128]{1,0:T(8,128)}, u32[]{:S(2)}) copy-start(f32[256,128]{1,0:T(8,128)} %constant.33.clone.columns) | copy-start | bytes 393220
  4.8 9.8 %copy-start.2 = (f32[104,512]{1,0:T(8,128)S(1)}, f32[104,512]{1,0:T(8,128)}, u32[]{:S(2)}) copy-start(f32[104,512]{1,0:T(8,128)} %constant.35.clone.small) | copy-start | bytes 638980
  4.8 18.2 %all-to-all-start = ((f32[16,16,128]{2,1,0:T(8,128)}), f32[16,16,128]{2,1,0:T(8,128)S(1)}, u32[]{:S(2)}, u32[]{:S(2)}) async-start(f32[16,16,128]{2,1,0:T(8,128)} %get-tuple-element.7), calls=%async_computation | async-start | bytes 262144 | tf_op jit(solution)/shard_map/all_to_all | solution.py:463
  14.5 12.1 %copy-start.3 = (f32[512,128]{1,0:T(8,128)S(1)}, f32[512,128]{1,0:T(8,128)}, u32[]{:S(2)}) copy-start(f32[512,128]{1,0:T(8,128)} %constant.38.clone.fine) | copy-start | bytes 786436
  15.2 11.4 %copy-start.1 = (f32[256,256]{1,0:T(8,128)S(1)}, f32[256,256]{1,0:T(8,128)}, u32[]{:S(2)}) copy-start(f32[256,256]{1,0:T(8,128)} %constant.31.clone.row_table) | copy-start | bytes 786436
  29.0 20.8 %copy-start.5 = (f32[168,128]{1,0:T(8,128)S(1)}, f32[168,128]{1,0:T(8,128)}, u32[]{:S(2)}) copy-start(f32[168,128]{1,0:T(8,128)} %constant.36.clone.leaps) | copy-start | bytes 258052
  29.0 20.8 %all-to-all-start.1 = ((f32[16,8,128]{2,1,0:T(8,128)}), f32[16,8,128]{2,1,0:T(8,128)S(1)}, u32[]{:S(2)}, u32[]{:S(2)}) async-start(f32[16,8,128]{2,1,0:T(8,128)} %get-tuple-element.9), calls=%async_computation.1 | async-start | bytes 131072 | tf_op jit(solution)/shard_map/all_to_all | solution.py:432
  50.8 13.9 %all-to-all-start.2 = ((f32[32,1,640]{2,1,0:T(1,128)}), f32[32,1,640]{2,1,0:T(1,128)S(1)}, u32[]{:S(2)}, u32[]{:S(2)}) async-start(f32[32,1,640]{2,1,0:T(1,128)} %bitcast.9), calls=%async_computation.2 | async-start | bytes 163840 | tf_op jit(solution)/shard_map/all_to_all | solution.py:432

commit v8 on v7

--- a/solution.py
+++ b/solution.py
@@ -303,7 +303,7 @@
             + bent[:TILE] * jnp.concatenate([top, top], axis=1)
             - bent[TILE : 2 * TILE] * jnp.concatenate([bottom, bottom], axis=1)
         )
-        placed = nn(jnp.concatenate([mixed[:, :rows], mixed[:, rows:]], axis=0), row_table[...])
+        placed = three(jnp.concatenate([mixed[:, :rows], mixed[:, rows:]], axis=0), row_table[...], ((1,), (0,)))
         number = row_number((TILE, rows))
         lefty = lax.rem(number, 2) == 0
         real = jnp.where(lefty, placed[2:3], placed[TILE + 2 : TILE + 3])

time: 69.2 us -> 69 us (level)
  no operation moved by 1% of the time
where the time goes in v8:
time: 69 us; the launch traced here: 68.7 us
  starting transfers between devices  26.9 us (39%)
  waiting for transfers between devices  24.6 us (36%)
  Pallas kernels  11.4 us (17%)
  blocking collectives  3.71 us (5%)
  between operations  2.06 us (3%)
    all_to_all x2, starting transfers between devices, exchange(): seen = lax.all_to_all(copies, axis, 0, 0, tiled=True)  17.2 us
    all_to_all x2, waiting for transfers between devices, exchange(): seen = lax.all_to_all(copies, axis, 0, 0, tiled=True)  16.9 us
    pallas_call x5, Pallas kernels, call(): pl.pallas_call(kernel, out_shape=[shape_of(*entry) for entry in outs], in...  11.4 us
    all_to_all x1, starting transfers between devices, body(): seen = lax.all_gather(lax.all_to_all(send, PAIR, 0, 0, tiled=True), CORE)  9.7 us
    all_to_all x1, waiting for transfers between devices, body(): seen = lax.all_gather(lax.all_to_all(send, PAIR, 0, 0, tiled=True), CORE)  7.72 us
    all_gather x1, blocking collectives, body(): seen = lax.all_gather(lax.all_to_all(send, PAIR, 0, 0, tiled=True), CORE)  3.71 us
  transfers between devices with their start and end apart: 3, of which 3 were waited for; matrix products, arithmetic and copies ran while one was open for 0% of the time, Pallas kernels for 1%

profile of v8, /device:TPU:1, one launch (start us, length us, event | category | flops | bytes accessed | tf_op | source)
XLA Modules:
  0.0 68.7 jit_solution(15155331080331427244)
XLA Ops:
  1.3 0.0 copy-start
  1.3 0.0 copy-start.4
  1.3 3.5 %edges.1 = (f32[256,512]{1,0:T(8,128)}, f32[256,512]{1,0:T(8,128)S(1)}, f32[16,16,128]{2,1,0:T(8,128)}) custom-call(f32[1]{0:T(128)S(6)} %copy.15.g, f32[256,512]{1,0:T(8,128)} %field.1, f32[512,512]{1,0:T(8,128)} %constant.32.clone.col_table, f32[256,256]{1,0:T(8,128)} %constant.31.clone.row_table, f32[256,128]{1,0:T(8,128)} %constant.33.clone.columns, ...), custom_call_target="tpu_custom_call" | custom-call | flops 201326592 | bytes 3194880 | tf_op jit(solution)/shard_map/edges/pallas_call | solution.py:418
  4.8 0.0 copy-start.2
  4.8 9.7 %all-to-all-start = ((f32[16,16,128]{2,1,0:T(8,128)}), f32[16,16,128]{2,1,0:T(8,128)S(1)}, u32[]{:S(2)}, u32[]{:S(2)}) async-start(f32[16,16,128]{2,1,0:T(8,128)} %get-tuple-element.7), calls=%async_computation | async-start | bytes 262144 | tf_op jit(solution)/shard_map/all_to_all | solution.py:463
  14.5 0.0 copy-done
  14.5 0.0 copy-done.4
  14.5 0.0 copy-done.2
  14.5 0.0 copy-start.3
  14.5 0.7 systems.1
  15.2 0.0 copy-start.1
  15.2 7.7 %all-to-all-done = f32[16,16,128]{2,1,0:T(8,128)S(1)} async-done(((f32[16,16,128]{2,1,0:T(8,128)}), f32[16,16,128]{2,1,0:T(8,128)S(1)}, u32[]{:S(2)}, u32[]{:S(2)}) %all-to-all-start) | async-done | bytes 131104 | tf_op jit(solution)/shard_map/all_to_all | solution.py:463
  23.0 3.7 %all-gather = f32[32,16,128]{2,1,0:T(8,128)S(1)} all-gather(f32[16,16,128]{2,1,0:T(8,128)S(1)} %all-to-all-done), channel_id=2, replica_groups=mesh['pair'=16,'core'=2,'col'=16] {'core'}, dimensions={0}, use_global_device_ids=true | all-gather | bytes 393216 | tf_op jit(solution)/shard_map/all_gather | solution.py:463
  26.7 0.0 copy-done.3
  26.7 0.0 copy-done.1
  26.7 2.1 %classes.4 = (f32[32,512]{1,0:T(8,128)}, f32[16,8,128]{2,1,0:T(8,128)}) custom-call(s32[1]{0:T(128)} %bitcast.me, f32[512,128]{1,0:T(8,128)S(1)} %bitcast.6, f32[256,512]{1,0:T(8,128)S(1)} %get-tuple-element.8.weight, f32[48,512]{1,0:T(8,128)S(1)} %systems.1, f32[256,256]{1,0:T(8,128)S(1)} %copy-done.1, f32[512,128]{1,0:T(8,128)S(1)} %copy-done.3, ...), custom_call_target="tpu_custom_call" | custom-call | flops 33554432 | bytes 2277376 | tf_op jit(solution)/shard_map/classes/pallas_call | solution.py:418
  28.8 0.0 copy-start.5
  28.8 11.8 %all-to-all-start.1 = ((f32[16,8,128]{2,1,0:T(8,128)}), f32[16,8,128]{2,1,0:T(8,128)S(1)}, u32[]{:S(2)}, u32[]{:S(2)}) async-start(f32[16,8,128]{2,1,0:T(8,128)} %get-tuple-element.9), calls=%async_computation.1 | async-start | bytes 131072 | tf_op jit(solution)/shard_map/all_to_all | solution.py:432
  40.7 8.9 %all-to-all-done.1 = f32[16,8,128]{2,1,0:T(8,128)S(1)} async-done(((f32[16,8,128]{2,1,0:T(8,128)}), f32[16,8,128]{2,1,0:T(8,128)S(1)}, u32[]{:S(2)}, u32[]{:S(2)}) %all-to-all-start.1) | async-done | bytes 65568 | tf_op jit(solution)/shard_map/all_to_all | solution.py:432
  49.6 0.0 copy-done.5
  49.6 1.0 %folds.1 = f32[160,128]{1,0:T(8,128)} custom-call(s32[1]{0:T(128)} %bitcast.1.me, f32[128,128]{1,0:T(8,128)S(1)} %bitcast.8, f32[48,512]{1,0:T(8,128)S(1)} %systems.1, f32[168,128]{1,0:T(8,128)S(1)} %copy-done.5), custom_call_target="tpu_custom_call" | custom-call | flops 4194304 | bytes 331776 | tf_op jit(solution)/shard_map/folds/pallas_call | solution.py:418
  50.6 5.3 %all-to-all-start.2 = ((f32[32,1,640]{2,1,0:T(1,128)}), f32[32,1,640]{2,1,0:T(1,128)S(1)}, u32[]{:S(2)}, u32[]{:S(2)}) async-start(f32[32,1,640]{2,1,0:T(1,128)} %bitcast.9), calls=%async_computation.2 | async-start | bytes 163840 | tf_op jit(solution)/shard_map/all_to_all | solution.py:432
  56.6 7.9 %all-to-all-done.2 = f32[32,1,640]{2,1,0:T(1,128)S(1)} async-done(((f32[32,1,640]{2,1,0:T(1,128)}), f32[32,1,640]{2,1,0:T(1,128)S(1)}, u32[]{:S(2)}, u32[]{:S(2)}) %all-to-all-start.2) | async-done | bytes 81952 | tf_op jit(solution)/shard_map/all_to_all | solution.py:432
  64.5 4.1 %finish.1 = (f32[256,512]{1,0:T(8,128)}, f32[1]{0:T(128)}) custom-call(f32[1]{0:T(128)S(6)} %copy.16.previous, s32[1]{0:T(128)} %bitcast.me, f32[160,128]{1,0:T(8,128)S(1)} %bitcast.7, f32[256,512]{1,0:T(8,128)S(1)} %get-tuple-element.8.weight, f32[48,512]{1,0:T(8,128)S(1)} %systems.1, f32[512,128]{1,0:T(8,128)S(1)} %copy-done.3, f32[104,512]{1,0:T(8,128)S(1)} %copy-done.2, ...), custom_call_target="tpu_custom_call" | custom-call | flops 234881024 | bytes 4653060 | tf_op jit(solution)/shard_map/finish/pallas_call | solution.py:418
Async XLA Ops:
  1.3 13.2 %copy-start = (f32[1024,128]{1,0:T(8,128)S(1)}, f32[1024,128]{1,0:T(8,128)}, u32[]{:S(2)}) copy-start(f32[1024,128]{1,0:T(8,128)} %constant.37.clone.classes) | copy-start | bytes 1572868
  1.3 13.2 %copy-start.4 = (f32[256,128]{1,0:T(8,128)S(1)}, f32[256,128]{1,0:T(8,128)}, u32[]{:S(2)}) copy-start(f32[256,128]{1,0:T(8,128)} %constant.33.clone.columns) | copy-start | bytes 393220
  4.8 9.8 %copy-start.2 = (f32[104,512]{1,0:T(8,128)S(1)}, f32[104,512]{1,0:T(8,128)}, u32[]{:S(2)}) copy-start(f32[104,512]{1,0:T(8,128)} %constant.35.clone.small) | copy-start | bytes 638980
  4.8 18.2 %all-to-all-start = ((f32[16,16,128]{2,1,0:T(8,128)}), f32[16,16,128]{2,1,0:T(8,128)S(1)}, u32[]{:S(2)}, u32[]{:S(2)}) async-start(f32[16,16,128]{2,1,0:T(8,128)} %get-tuple-element.7), calls=%async_computation | async-start | bytes 262144 | tf_op jit(solution)/shard_map/all_to_all | solution.py:463
  14.5 12.1 %copy-start.3 = (f32[512,128]{1,0:T(8,128)S(1)}, f32[512,128]{1,0:T(8,128)}, u32[]{:S(2)}) copy-start(f32[512,128]{1,0:T(8,128)} %constant.38.clone.fine) | copy-start | bytes 786436
  15.2 11.4 %copy-start.1 = (f32[256,256]{1,0:T(8,128)S(1)}, f32[256,256]{1,0:T(8,128)}, u32[]{:S(2)}) copy-start(f32[256,256]{1,0:T(8,128)} %constant.31.clone.row_table) | copy-start | bytes 786436
  28.8 20.8 %copy-start.5 = (f32[168,128]{1,0:T(8,128)S(1)}, f32[168,128]{1,0:T(8,128)}, u32[]{:S(2)}) copy-start(f32[168,128]{1,0:T(8,128)} %constant.36.clone.leaps) | copy-start | bytes 258052
  28.8 20.8 %all-to-all-start.1 = ((f32[16,8,128]{2,1,0:T(8,128)}), f32[16,8,128]{2,1,0:T(8,128)S(1)}, u32[]{:S(2)}, u32[]{:S(2)}) async-start(f32[16,8,128]{2,1,0:T(8,128)} %get-tuple-element.9), calls=%async_computation.1 | async-start | bytes 131072 | tf_op jit(solution)/shard_map/all_to_all | solution.py:432
  50.6 13.9 %all-to-all-start.2 = ((f32[32,1,640]{2,1,0:T(1,128)}), f32[32,1,640]{2,1,0:T(1,128)S(1)}, u32[]{:S(2)}, u32[]{:S(2)}) async-start(f32[32,1,640]{2,1,0:T(1,128)} %bitcast.9), calls=%async_computation.2 | async-start | bytes 163840 | tf_op jit(solution)/shard_map/all_to_all | solution.py:432
